TPU v7x, 32 devices: a whole 2x2x4 slice. The times are simulated.
32 devices in a mesh: section: 4 (over y, x), dom: 8 (over z, core).
Axes of the slice: x: 2, y: 2, z: 4, core: 2. Of those that a mesh axis runs over, the one named last changes fastest.
Arguments:
- source: float32 [4, 32, 2048], P('section', None, 'dom'), may hold values from -6 to 6
- initial: float32 [4, 2048], P('section', 'dom'), may hold values from -4 to 4
- capacitance: float32 [4, 2048], P('section', 'dom'), may hold values from 0.5 to 2
- block_matrix: float32 [4, 16, 128, 128], P('section', 'dom')
- block_inverse: float32 [4, 16, 128, 128], P('section', 'dom'), as said below
- net_weight: float32 [4, 2048, 512], P('section', 'dom'), may hold values from -0.125 to 0.125
- tap_nodes: int32 [4, 1024], P('section', 'dom'), may hold values from 0 to 255
- drive_nodes: int32 [4, 1024], P('section', 'dom'), may hold values from 0 to 255
- drive_gain: float32 [4, 1024], P('section', 'dom'), may hold values from 0.5 to 2
- attenuation: float32 [4, 1024], P('section', 'dom'), may hold values from 0 to 1
Outputs:
- waveform: float32 [4, 32, 2048], P('section', None, 'dom')
- mean_square: float32 [4], replicated
Inputs may be any that keep to these rules, and one draw needn't show every extreme that they name: block_matrix holds symmetric positive definite blocks and block_inverse their inverses up to float32 rounding. `tap_nodes`: offsets within the device's own 256 nodes. `drive_nodes`: offsets within the device's own 256 nodes.
All inputs are finite; a program needn't handle non-finite values.
Results may differ from a plain program's by a relative error of at most 0.0001.
Values sent between devices are 32-bit elements; how exact they have to be, the bound alone decides.
No kernel may reach another device: no remote copies, remote signals or barrier semaphores. Data moves between devices by JAX's collectives and lax.ppermute only.
A program may use at most 64 MiB of HBM per device.

v0:
```python
import jax
import jax.numpy as jnp
from jax import lax
from jax.sharding import PartitionSpec as P

NEWTON = 2
SWEEPS = 2


HIGH = lax.Precision.HIGHEST


def prefix(part, axis, combine, identity):
    place = lax.axis_index(axis)
    gathered = jax.tree.map(lambda a: lax.all_gather(a, axis), part)
    state = jax.tree.map(lambda a, e: jnp.zeros_like(a) + jnp.asarray(e, a.dtype), part, identity)

    def one(turn, state):
        return combine(
            state, jax.tree.map(lambda a: lax.dynamic_index_in_dim(a, turn, 0, False), gathered)
        )

    return lax.fori_loop(0, place, one, state)


def block_apply(matrices, values):
    return jnp.einsum("kij,tkj->tki", matrices, values, precision=HIGH)


def time_march(residual, inverse, powers):
    steps_here = residual.shape[0]
    moved = block_apply(inverse, residual)
    offset = 1
    for power in powers:
        lagged = jnp.concatenate(
            [jnp.zeros((offset,) + moved.shape[1:], jnp.float32), moved[: steps_here - offset]],
            axis=0,
        )
        moved = moved + block_apply(power, lagged)
        offset = offset * 2
    return moved


def compose(earlier, later):
    return (earlier[0] * later[0], later[0][None, :] * earlier[1] + later[1])


def per_device(
    source,
    initial,
    capacitance,
    block_matrix,
    block_inverse,
    net_weight,
    tap_nodes,
    drive_nodes,
    drive_gain,
    attenuation,
):
    source = source[0]
    initial = initial[0]
    capacitance = capacitance[0]
    block_matrix = block_matrix[0]
    block_inverse = block_inverse[0]
    net_weight = net_weight[0]
    tap_nodes = tap_nodes[0]
    drive_nodes = drive_nodes[0]
    drive_gain = drive_gain[0]
    attenuation = attenuation[0]
    steps_here = source.shape[0]
    node_here = source.shape[1]
    blocks_here = block_matrix.shape[0]
    width = block_matrix.shape[1]
    cell_count = float(lax.axis_size("section") * lax.axis_size("dom") * steps_here * node_here)
    node_range = jnp.arange(node_here, dtype=jnp.int32)
    tap_table = (tap_nodes[:, None] == node_range[None, :]).astype(jnp.float32)
    drive_table = (drive_nodes[:, None] == node_range[None, :]).astype(jnp.float32) * drive_gain[
        :, None
    ]
    cap_blocks = capacitance.reshape(blocks_here, width)
    powers = []
    power = block_inverse * cap_blocks[:, None, :]
    offset = 1
    while offset < steps_here:
        powers.append(power)
        power = jnp.einsum("kij,kjl->kil", power, power, precision=HIGH)
        offset = offset * 2
    waveform = jnp.broadcast_to(initial[None, :], (steps_here, node_here))
    history = []
    for sweep_index in range(SWEEPS):
        taps = jnp.einsum("tn,cn->tc", waveform, tap_table, precision=HIGH)
        identity = (jnp.ones_like(attenuation), jnp.zeros_like(taps))
        unused, drive = prefix((attenuation, taps), "section", compose, identity)
        inject = jnp.dot(drive, drive_table, precision=HIGH)
        for newton_index in range(NEWTON):
            net_volts = lax.psum(jnp.dot(waveform, net_weight, precision=HIGH), "dom")
            previous = jnp.concatenate([initial[None, :], waveform[:-1]], axis=0)
            residual_shaped = waveform.reshape(steps_here, blocks_here, width)
            applied = block_apply(block_matrix, residual_shaped).reshape(steps_here, node_here)
            back = jnp.einsum("tm,nm->tn", net_volts, net_weight, precision=HIGH)
            residual = (
                applied
                - capacitance[None, :] * previous
                + 0.5 * jnp.tanh(waveform)
                + back
                - source
                - inject
            )
            total_sq = lax.psum(jnp.sum(residual * residual), ("section", "dom"))
            mean_sq = total_sq / cell_count
            damping = 1.0 / (1.0 + jnp.sqrt(mean_sq))
            shaped = residual.reshape(steps_here, blocks_here, width)
            waveform = waveform - damping * time_march(shaped, block_inverse, powers).reshape(
                steps_here, node_here
            )
            history.append(mean_sq)
    return (waveform[None], jnp.stack(history))


def solution(mesh):
    return jax.shard_map(
        per_device,
        mesh=mesh,
        in_specs=(
            P("section", None, "dom"),
            P("section", "dom"),
            P("section", "dom"),
            P("section", "dom", None, None),
            P("section", "dom", None, None),
            P("section", "dom", None),
            P("section", "dom"),
            P("section", "dom"),
            P("section", "dom"),
            P("section", "dom"),
        ),
        out_specs=(P("section", None, "dom"), P()),
        check_vma=False,
    )
```

profile of v0, /device:TPU:0, one launch (start us, length us, event | category | flops | bytes accessed | tf_op | source)
XLA Modules:
  0.0 429.4 jit_solution(8033621293391351705)
XLA Ops:
  7.2 1.0 copy-done
  8.2 1.0 fusion.42
  9.4 0.6 copy-done.6
  10.0 9.4 %all-gather.2 = f32[4,1,128]{2,1,0:T(1,128)S(1)} all-gather(f32[1,1,128]{2,1,0:T(1,128)S(1)} %bitcast.354), channel_id=1, replica_groups=mesh['section'=4,'dom'=8] {'section'}, dimensions={0}, use_global_device_ids=true | all-gather | bytes 2560 | tf_op jit(solution)/shard_map/all_gather | solution.py:15
  19.4 0.7 copy-done.7
  20.4 8.3 %all-gather = f32[128,128]{1,0:T(8,128)S(1)} all-gather(f32[32,128]{1,0:T(8,128)S(1)} %convolution_bitcast_fusion.28), channel_id=2, replica_groups=mesh['section'=4,'dom'=8] {'section'}, dimensions={0}, use_global_device_ids=true | all-gather | bytes 81920 | tf_op jit(solution)/shard_map/all_gather | solution.py:15
  28.7 0.7 copy-done.5
  31.7 36.1 %all-reduce.25.cloned.1.call-done = f32[32,512]{1,0:T(8,128)} async-done(((f32[32,512]{1,0:T(8,128)}), f32[32,512]{1,0:T(8,128)}) %all-reduce.25.cloned.1.call-update) | async-done | bytes 65552 | tf_op jit(solution)/shard_map/psum | solution.py:96
  67.9 2.1 multiply_reduce_fusion.3
  69.9 39.5 %psum.57 = f32[]{:T(128)} all-reduce(f32[]{:T(128)} %get-tuple-element.112), channel_id=1, replica_groups=mesh['section'=4,'dom'=8] {'section','dom'}, use_global_device_ids=true, to_apply=%region_4.5 | all-reduce | flops 1 | bytes 8 | tf_op jit(solution)/shard_map/psum | solution.py:109
  112.0 1.0 fusion.39
  113.5 54.5 %all-reduce.27.cloned.1.call-done = f32[32,512]{1,0:T(8,128)} async-done(((f32[32,512]{1,0:T(8,128)}), f32[32,512]{1,0:T(8,128)}) %all-reduce.27.cloned.1.call-update) | async-done | bytes 65552 | tf_op jit(solution)/shard_map/psum | solution.py:96
  168.0 2.1 multiply_reduce_fusion.2
  170.0 39.5 %psum.59 = f32[]{:T(128)} all-reduce(f32[]{:T(128)} %get-tuple-element.114), channel_id=1, replica_groups=mesh['section'=4,'dom'=8] {'section','dom'}, use_global_device_ids=true, to_apply=%region_7.8 | all-reduce | flops 1 | bytes 8 | tf_op jit(solution)/shard_map/psum | solution.py:109
  212.5 9.3 %all-gather.1 = f32[128,128]{1,0:T(8,128)S(1)} all-gather(f32[32,128]{1,0:T(8,128)S(1)} %fusion.56), channel_id=3, replica_groups=mesh['section'=4,'dom'=8] {'section'}, dimensions={0}, use_global_device_ids=true | all-gather | bytes 81920 | tf_op jit(solution)/shard_map/all_gather | solution.py:15
  222.1 1.0 fusion.36
  223.5 53.7 %all-reduce.29.cloned.1.call-done = f32[32,512]{1,0:T(8,128)} async-done(((f32[32,512]{1,0:T(8,128)}), f32[32,512]{1,0:T(8,128)}) %all-reduce.29.cloned.1.call-update) | async-done | bytes 65552 | tf_op jit(solution)/shard_map/psum | solution.py:96
  277.2 2.0 multiply_reduce_fusion.1
  279.2 39.5 %psum.61 = f32[]{:T(128)} all-reduce(f32[]{:T(128)} %get-tuple-element.118), channel_id=1, replica_groups=mesh['section'=4,'dom'=8] {'section','dom'}, use_global_device_ids=true, to_apply=%region_12.13 | all-reduce | flops 1 | bytes 8 | tf_op jit(solution)/shard_map/psum | solution.py:109
  321.4 1.0 fusion.33
  322.9 54.5 %all-reduce.31.cloned.1.call-done = f32[32,512]{1,0:T(8,128)} async-done(((f32[32,512]{1,0:T(8,128)}), f32[32,512]{1,0:T(8,128)}) %all-reduce.31.cloned.1.call-update) | async-done | bytes 65552 | tf_op jit(solution)/shard_map/psum | solution.py:96
  377.4 2.0 multiply_reduce_fusion
  379.4 39.5 %psum.63 = f32[]{:T(128)} all-reduce(f32[]{:T(128)} %get-tuple-element.120), channel_id=1, replica_groups=mesh['section'=4,'dom'=8] {'section','dom'}, use_global_device_ids=true, to_apply=%region_15.16 | all-reduce | flops 1 | bytes 8 | tf_op jit(solution)/shard_map/psum | solution.py:109
  422.3 0.6 subtract_subtract_fusion
  (86 shorter events, 12.9 us)
Async XLA Ops:
  7.2 1.0 copy-start
  7.2 1.0 copy-start.4
  7.2 60.7 %all-reduce.25.cloned.1.call-start = ((), (), s32[]{:S(2)}) async-start(), calls=%async_computation | async-start | bytes 131072 | tf_op jit(solution)/shard_map/psum | solution.py:96
  9.3 158.7 %all-reduce.27.cloned.1.call-start = ((), (), s32[]{:S(2)}) async-start(), calls=%async_computation.1 | async-start | bytes 131072 | tf_op jit(solution)/shard_map/psum | solution.py:96
  9.3 0.7 copy-start.6
  19.4 0.7 copy-start.7
  20.3 8.4 %copy-start.1 = (f32[1,2,128,128]{3,2,1,0:T(8,128)S(1)}, f32[1,2,128,128]{3,2,1,0:T(8,128)}, u32[]{:S(2)}) copy-start(f32[1,2,128,128]{3,2,1,0:T(8,128)} %param.18) | copy-start | bytes 393220
  28.7 0.7 copy-start.5
  30.2 0.7 copy-start.8
  30.2 0.7 copy-start.9
  30.5 0.9 copy-start.2
  31.7 36.1 %copy-start.3 = (f32[1,32,256]{2,1,0:T(8,128)S(1)}, f32[1,32,256]{2,1,0:T(8,128)}, u32[]{:S(2)}) copy-start(f32[1,32,256]{2,1,0:T(8,128)} %param.14) | copy-start | bytes 98308
  113.1 164.1 %all-reduce.29.cloned.1.call-start = ((), (), s32[]{:S(2)}) async-start(), calls=%async_computation.2 | async-start | bytes 131072 | tf_op jit(solution)/shard_map/psum | solution.py:96
  223.1 154.3 %all-reduce.31.cloned.1.call-start = ((), (), s32[]{:S(2)}) async-start(), calls=%async_computation.3 | async-start | bytes 131072 | tf_op jit(solution)/shard_map/psum | solution.py:96
Sparse Core Ops, SparseCore 0:
  10.3 57.5 all-reduce.24
  113.2 54.7 all-reduce.26
  223.2 53.9 all-reduce.28
  322.6 54.7 all-reduce.30
where the time goes:
time: 430 us; the launch traced here: 429 us
  waiting for transfers between devices  199 us (46%)
  blocking collectives  185 us (43%)
  matrix products  23.2 us (5%)
  between operations  17 us (4%)
    psum x4, waiting for transfers between devices, per_device(): net_volts = lax.psum(jnp.dot(waveform, net_weight, precision=HIGH), 'dom')  199 us
    psum x4, blocking collectives, per_device(): total_sq = lax.psum(jnp.sum(residual * residual), ('section', 'dom'))  158 us
    all_gather x3, blocking collectives, prefix(): gathered = jax.tree.map(lambda a: lax.all_gather(a, axis), part)  27 us
    dot_general x28, matrix products, block_apply(): return jnp.einsum('kij,tkj->tki', matrices, values, precision=HIGH)  8.9 us
  transfers between devices with their start and end apart: 4, of which 4 were waited for; matrix products, arithmetic and copies ran while one was open for 1% of the time, Pallas kernels for 0%

commit v1 on v0

v1 whole, which is shorter than its diff:
```python
import functools

import jax
import jax.numpy as jnp
from jax import lax
from jax.experimental import pallas as pl
from jax.experimental.pallas import tpu as pltpu
from jax.sharding import PartitionSpec as P

NEWTON = 2
SWEEPS = 2
HIGHEST = lax.Precision.HIGHEST
F32 = jnp.float32
BF16 = jnp.bfloat16
LANES = 128
SUB = 8


def fdot(a, b):
    return jnp.dot(a, b, precision=HIGHEST, preferred_element_type=F32)


def bdot(a, b):
    return jnp.dot(a, b, preferred_element_type=F32)


def split(x):
    high = x.astype(BF16)
    return high, (x - high.astype(F32)).astype(BF16)


def dot3(x, high, low):
    rows = x.shape[0]
    xh, xl = split(x)
    both = bdot(jnp.concatenate([xh, xl], axis=0), high)
    return both[:rows] + both[rows:] + bdot(xh, low)


def dot2(x, exact):
    rows = x.shape[0]
    xh, xl = split(x)
    both = bdot(jnp.concatenate([xh, xl], axis=0), exact)
    return both[:rows] + both[rows:]


def lag(x, offset):
    if offset == 0:
        return x
    if offset >= x.shape[0]:
        return jnp.zeros_like(x)
    if offset % SUB == 0:
        return jnp.concatenate([jnp.zeros((offset, x.shape[1]), F32), x[: x.shape[0] - offset]], axis=0)
    row = lax.broadcasted_iota(jnp.int32, x.shape, 0)
    return jnp.where(row >= offset, pltpu.roll(x, offset, 0), 0.0)


def stages(steps):
    plan = [(0, 1)]
    span = 2
    while span < steps:
        wide = min(4, -(-steps // span))
        plan.append(tuple(span * i for i in range(1, wide)))
        span *= wide
    return plan


def powers_of(plan):
    return [p for stage in plan[1:] for p in stage]


def tile_sum(x):
    total = None
    for i in range(0, x.shape[0], SUB):
        for j in range(0, x.shape[1], LANES):
            part = x[i : i + SUB, j : j + LANES]
            total = part if total is None else total + part
    return total


def first_kernel(source, initial, capacitance, matrix, weight, tap, drive, gain, att, msg, pack):
    steps, nodes = source.shape
    blocks, width = matrix.shape[0], matrix.shape[1]
    channels = tap.shape[1]
    start = initial[...]
    net = fdot(start, weight[...])
    rows = []
    for j in range(0, net.shape[1], LANES):
        rows.append(net[:, j : j + LANES])
    node = lax.broadcasted_iota(jnp.int32, (nodes, channels), 0)
    taps = fdot(start, (node == tap[...]).astype(F32))
    for row in (taps, att[...]):
        for j in range(0, channels, LANES):
            rows.append(row[:, j : j + LANES])
    assert len(rows) <= SUB
    rows += [jnp.zeros((1, LANES), F32)] * (SUB - len(rows))
    tile = jnp.concatenate(rows, axis=0)
    msg[...] = jnp.broadcast_to(tile[None], msg.shape)
    pack[0:steps, :] = source[...]
    parts = []
    for k in range(blocks):
        parts.append(
            lax.dot_general(
                start[:, k * width : (k + 1) * width],
                matrix[k],
                (((1,), (1,)), ((), ())),
                precision=HIGHEST,
                preferred_element_type=F32,
            )
        )
    held = jnp.concatenate(parts, axis=1) - capacitance[...] * start
    pad = jnp.zeros((1, nodes - channels), F32)
    pack[steps : steps + SUB, :] = jnp.concatenate(
        [
            held,
            start,
            capacitance[...],
            jnp.concatenate([gain[...], pad], axis=1),
            jnp.concatenate([tap[...].astype(F32), pad], axis=1),
            jnp.concatenate([drive[...].astype(F32), pad], axis=1),
            jnp.zeros((2, nodes), F32),
        ],
        axis=0,
    )


def both(ref_other, ref_own, lo, hi):
    return jnp.concatenate([ref_other[lo:hi, :], ref_own[lo:hi, :]], axis=1)


def prep_kernel(plan, steps, channels, w_other, w_own, i_other, i_own, p_other, p_own, wh, wl, th, tl, ah, al, tap, drv):
    nodes = w_own.shape[0]
    blocks, width = i_own.shape[0], i_own.shape[1]
    cap = both(p_other, p_own, steps + 2, steps + 3)
    for half, ref in enumerate((w_other, w_own)):
        here = slice(half * nodes, (half + 1) * nodes)
        h, l = split(ref[...])
        wh[here, :] = h
        wl[here, :] = l
        turned = ref[...].T
        h, l = split(turned)
        th[:, here] = h
        tl[:, here] = l
    wanted = powers_of(plan)
    eye = lax.broadcasted_iota(jnp.int32, (width, width), 0) == lax.broadcasted_iota(jnp.int32, (width, width), 1)
    for b in range(2 * blocks):
        inverse = (i_other if b < blocks else i_own)[b % blocks].T
        scale = jnp.where(eye, cap[:, b * width : (b + 1) * width], 0.0)
        step = fdot(scale, inverse)
        made = {1: step}
        todo = [inverse, fdot(inverse, step)]
        power = 2
        while power <= max(wanted):
            made[power] = fdot(made[power // 2], made[power // 2])
            power *= 2
        for p in wanted:
            if p not in made:
                top = 1 << (p.bit_length() - 1)
                made[p] = fdot(made[top], made[p - top])
            todo.append(made[p])
        for i, value in enumerate(todo):
            h, l = split(value)
            ah[i, b] = h
            al[i, b] = l
    for half, ref in enumerate((p_other, p_own)):
        taps = ref[steps + 4 : steps + 5, 0:channels]
        node = lax.broadcasted_iota(jnp.int32, (nodes, channels), 0).astype(F32)
        tap[half] = (node == taps).astype(F32).astype(BF16)
        driven = ref[steps + 5 : steps + 6, 0:channels]
        drv[half] = (node == driven).astype(F32).T.astype(BF16)


def march(plan, r, ah, al):
    blocks, width = ah.shape[1], ah.shape[2]
    out = []
    for b in range(blocks):
        x = r[:, b * width : (b + 1) * width]
        unit = 0
        for s, stage in enumerate(plan):
            total = None
            for offset in stage:
                part = dot3(lag(x, offset), ah[unit, b], al[unit, b])
                total = part if total is None else total + part
                unit += 1
            x = total if s == 0 else total + x
        out.append(x)
    return jnp.concatenate(out, axis=1)


def finish_round(plan, r, c_ref, p_ref, msg, ah, al, wh, wl, north):
    tile = tile_sum(r * r) * north
    msg[...] = jnp.broadcast_to(tile[None], msg.shape)
    c = march(plan, r, ah, al)
    c_ref[...] = c
    p_ref[...] = dot3(c, wh[...], wl[...])
    return c


def bit_masks(my, sections, level):
    mine, other = [], []
    for s in range(sections):
        here = s >> level
        mine.append(here == (my >> level))
        other.append(here == ((my >> level) ^ 1))
    return mine, other


def opening_kernel(plan, steps, channels, sections, doms, levels, info, got, p_other, p_own, ah, al, wh, wl, th, tl, drv,
                   w_ref, q_ref, r_ref, c_ref, p_ref, msg, inj_ref, mix_ref):
    my, chip = info[0], info[1]
    north = info[2].astype(F32)
    nets = wh.shape[1]
    net_rows = nets // LANES
    tap_rows = channels // LANES
    mine = jnp.zeros((SUB, LANES), F32)
    base = my * doms
    for d in range(doms):
        mine = mine + got[base + d]
    net = jnp.concatenate([mine[i : i + 1, :] for i in range(net_rows)], axis=1)

    def channel_row(s, first):
        pieces = []
        for half in range(2):
            tile = got[s * doms + 2 * chip + half]
            pieces += [tile[first + i : first + i + 1, :] for i in range(tap_rows)]
        return jnp.concatenate(pieces, axis=1)

    decay, carried, drive = [], None, jnp.zeros((1, 2 * channels), F32)
    for s in range(sections):
        a = channel_row(s, net_rows + tap_rows)
        decay.append(a)
        if carried is not None:
            drive = jnp.where(my == s, carried, drive)
        tapped = channel_row(s, net_rows)
        carried = tapped if carried is None else a * carried + tapped
    one = jnp.ones((1, 2 * channels), F32)
    rows = []
    for level in range(levels):
        bit = (my >> level) & 1
        own_a, other_a, past_a = one, one, one
        for s in range(sections):
            here = s >> level
            own_a = jnp.where(here == (my >> level), own_a * decay[s], own_a)
            other_a = jnp.where(here == ((my >> level) ^ 1), other_a * decay[s], other_a)
            past_a = jnp.where((here == (my >> level)) & (s < my), past_a * decay[s], past_a)
        rows += [jnp.where(bit == 1, one, other_a), jnp.where(bit == 1, own_a, one), jnp.where(bit == 1, past_a, 0.0)]
    mix_ref[...] = jnp.concatenate(rows, axis=0)

    gain = jnp.concatenate([p_other[steps + 3 : steps + 4, 0:channels], p_own[steps + 3 : steps + 4, 0:channels]], axis=1)
    inj = spread(jnp.broadcast_to(drive * gain, (SUB, 2 * channels)), drv)[0:1]
    inj_ref[...] = inj
    back = dot3(jnp.broadcast_to(net, (SUB, nets)), th[...], tl[...])[0:1]
    start = both(p_other, p_own, steps + 1, steps + 2)
    held = both(p_other, p_own, steps, steps + 1)
    q = (held + back - inj) - both(p_other, p_own, 0, steps)
    r = q + 0.5 * jnp.tanh(start)
    w_ref[...] = jnp.broadcast_to(start, w_ref.shape)
    q_ref[...] = q
    r_ref[...] = r
    finish_round(plan, r, c_ref, p_ref, msg, ah, al, wh, wl, north)


def spread(drive, drv):
    channels = drv.shape[1]
    return jnp.concatenate([dot2(drive[:, h * channels : (h + 1) * channels], drv[h]) for h in range(2)], axis=1)


def damping_of(got, cells):
    total = got[0]
    for i in range(1, got.shape[0]):
        total = total + got[i]
    mean = jnp.sum(jnp.sum(total, axis=0, keepdims=True), axis=1, keepdims=True) / cells
    return mean, 1.0 / (1.0 + jnp.sqrt(mean))


def round_kernel(plan, steps, channels, cells, mode, *refs):
    refs = list(refs)
    take = lambda n: [refs.pop(0) for _ in range(n)]
    (info, got, own, recv, w0, q0, r0, c0, ah, al, wh, wl, th, tl) = take(14)
    if mode == "taps":
        (tap,) = take(1)
    if mode == "drive":
        pre, inj, p_other, p_own, drv = take(5)
    w_ref, q_ref, r_ref, c_ref, p_ref, msg, mean_ref = take(7)
    north = info[2].astype(F32)
    mean, damp = damping_of(got, cells)
    mean_ref[...] = jnp.broadcast_to(mean, mean_ref.shape)
    back = dot3(own[...] + recv[...], th[...], tl[...])
    w = w0[...] - damp * c0[...]
    q = q0[...] - damp * (r0[...] + back)
    if mode == "drive":
        drive = pre[0:steps, :] - damp * pre[steps : 2 * steps, :]
        gain = jnp.concatenate([p_other[steps + 3 : steps + 4, 0:channels], p_own[steps + 3 : steps + 4, 0:channels]], axis=1)
        q = q - (spread(drive * gain, drv) - inj[...])
    r = q + 0.5 * jnp.tanh(w)
    w_ref[...] = w
    q_ref[...] = q
    r_ref[...] = r
    if mode != "last":
        c = finish_round(plan, r, c_ref, p_ref, msg, ah, al, wh, wl, north)
    else:
        tile = tile_sum(r * r) * north
        msg[...] = jnp.broadcast_to(tile[None], msg.shape)
        c = march(plan, r, ah, al)
        c_ref[...] = c
        half = w.shape[1] // 2
        p_ref[0:steps, :] = w[:, 0:half]
        p_ref[steps : 2 * steps, :] = c[:, 0:half]
    if mode == "taps":
        (tt_ref,) = take(1)
        half = w.shape[1] // 2
        for h in range(2):
            here = slice(h * half, (h + 1) * half)
            both_taps = dot2(jnp.concatenate([w[:, here], c[:, here]], axis=0), tap[h])
            tt_ref[:, h * channels : (h + 1) * channels] = both_taps


def last_kernel(steps, cells, info, got, w, c, given, m1, m2, m3, out, means):
    mean, damp = damping_of(got, cells)
    half = out.shape[1]
    north = info[2] == 1
    w_here = jnp.where(north, w[:, half : 2 * half], given[0:steps, :])
    c_here = jnp.where(north, c[:, half : 2 * half], given[steps : 2 * steps, :])
    out[...] = w_here - damp * c_here
    lane = lax.broadcasted_iota(jnp.int32, (1, LANES), 1)
    row = jnp.where(lane == 0, m1[...], jnp.where(lane == 1, m2[...], jnp.where(lane == 2, m3[...], mean)))
    means[...] = row


def call(kernel, outs, *args, smem=()):
    specs = [
        pl.BlockSpec(memory_space=pltpu.SMEM if i in smem else pltpu.VMEM) for i in range(len(args))
    ]
    return pl.pallas_call(
        kernel,
        out_shape=[jax.ShapeDtypeStruct(s, d) for s, d in outs],
        in_specs=specs,
        out_specs=[pl.BlockSpec(memory_space=pltpu.VMEM) for _ in outs],
    )(*args)


def per_device(
    source,
    initial,
    capacitance,
    block_matrix,
    block_inverse,
    net_weight,
    tap_nodes,
    drive_nodes,
    drive_gain,
    attenuation,
):
    source = source[0]
    block_matrix = block_matrix[0]
    block_inverse = block_inverse[0]
    net_weight = net_weight[0]
    steps, nodes = source.shape
    blocks, width = block_matrix.shape[:2]
    nets = net_weight.shape[1]
    channels = tap_nodes.shape[1]
    sections, doms = lax.axis_size("section"), lax.axis_size("dom")
    devices = sections * doms
    everywhere = ("section", "dom")
    wide = 2 * nodes
    cells = float(devices * steps * nodes)
    plan = stages(steps)
    units = 2 + len(powers_of(plan))
    levels = max(1, (sections - 1).bit_length())

    def swap(x):
        return lax.ppermute(x, "dom", [(i, i ^ 1) for i in range(doms)])

    def pair(x, odd, even):
        links = []
        for s in range(sections):
            for d in range(doms):
                ps, pd = odd(s, d) if d % 2 else even(s, d)
                links.append((s * doms + d, ps * doms + pd))
        return lax.ppermute(x, everywhere, links)

    def along_dom(x, bit):
        return pair(x, lambda s, d: (s, d ^ (2 << bit)), lambda s, d: (s ^ 1, d))

    def along_section(x, bit):
        return pair(x, lambda s, d: (s ^ (1 << bit), d), lambda s, d: (s, d ^ 2))

    def gather(msg):
        return lax.all_to_all(msg, everywhere, 0, 0, tiled=False)

    place = lax.axis_index("dom")
    info = jnp.stack([lax.axis_index("section"), place // 2, place % 2]).astype(jnp.int32)

    w_other = swap(net_weight)
    i_other = swap(block_inverse)
    message = ((devices, SUB, LANES), F32)
    msg, pack = call(
        first_kernel,
        [message, ((steps + SUB, nodes), F32)],
        source, initial, capacitance, block_matrix, net_weight, tap_nodes, drive_nodes, drive_gain, attenuation,
    )
    got = gather(msg)
    p_other = swap(pack)
    wh, wl, th, tl, ah, al, tap, drv = call(
        functools.partial(prep_kernel, plan, steps, channels),
        [
            ((wide, nets), BF16), ((wide, nets), BF16), ((nets, wide), BF16), ((nets, wide), BF16),
            ((units, 2 * blocks, width, width), BF16), ((units, 2 * blocks, width, width), BF16),
            ((2, nodes, channels), BF16), ((2, channels, nodes), BF16),
        ],
        w_other, net_weight, i_other, block_inverse, p_other, pack,
    )
    state = [((steps, wide), F32)] * 4
    w, q, r, c, part, msg, inj, mix = call(
        functools.partial(opening_kernel, plan, steps, channels, sections, doms, levels),
        state + [((steps, nets), F32), message, ((1, wide), F32), ((3 * levels, 2 * channels), F32)],
        info, got, p_other, pack, ah, al, wh, wl, th, tl, drv,
        smem=(0,),
    )
    means = []
    taps = None
    bits = (doms // 2 - 1).bit_length()
    for index in range(1, NEWTON * SWEEPS):
        own = part
        recv = jnp.zeros_like(part) if bits == 0 else along_dom(own, 0)
        got = gather(msg)
        for bit in range(1, bits):
            own = own + recv
            recv = along_dom(own, bit)
        last = index == NEWTON * SWEEPS - 1
        boundary = index % NEWTON == 0
        before = index % NEWTON == NEWTON - 1 and not last
        mode = "last" if last else "drive" if boundary else "taps" if before else "plain"
        extra = []
        if mode == "taps":
            extra = [tap]
        if mode == "drive":
            prefix, total = jnp.zeros_like(taps), taps
            for level in range(levels):
                if sections == 1:
                    break
                got_taps = along_section(total, level)
                prefix = prefix + mix[3 * level + 2][None] * got_taps
                total = mix[3 * level][None] * total + mix[3 * level + 1][None] * got_taps
            extra = [prefix, inj, p_other, pack, drv]
        outs = state + [((2 * steps, nodes), F32) if last else ((steps, nets), F32), message, ((1, LANES), F32)]
        if mode == "taps":
            outs = outs + [((2 * steps, 2 * channels), F32)]
        result = call(
            functools.partial(round_kernel, plan, steps, channels, cells, mode),
            outs,
            info, got, own, recv, w, q, r, c, ah, al, wh, wl, th, tl, *extra,
            smem=(0,),
        )
        w, q, r, c, part, msg, mean = result[:7]
        means.append(mean)
        if mode == "taps":
            taps = result[7]
    got = gather(msg)
    given = swap(part)
    out, history = call(
        functools.partial(last_kernel, steps, cells),
        [((steps, nodes), F32), ((1, LANES), F32)],
        info, got, w, c, given, *means,
        smem=(0,),
    )
    return (out[None], history[0, : NEWTON * SWEEPS])


def solution(mesh):
    return jax.shard_map(
        per_device,
        mesh=mesh,
        in_specs=(
            P("section", None, "dom"),
            P("section", "dom"),
            P("section", "dom"),
            P("section", "dom", None, None),
            P("section", "dom", None, None),
            P("section", "dom", None),
            P("section", "dom"),
            P("section", "dom"),
            P("section", "dom"),
            P("section", "dom"),
        ),
        out_specs=(P("section", None, "dom"), P()),
        check_vma=False,
    )
```

time: 430 us -> 109 us (0.25)
  blocking collectives: 185 us -> 0 us
  waiting for transfers between devices: 199 us -> 25.7 us
  starting transfers between devices: 0.16 us -> 42 us
  Pallas kernels: 0 us -> 31.4 us
  matrix products: 23.2 us -> 0 us
  between operations: 17 us -> 0.85 us
    psum x4 -> x0, waiting for transfers between devices: 199 us -> none  [per_device(): net_volts = lax.psum(jnp.dot(waveform, net_weight, precision=HIGH), 'dom')]
    psum x4 -> x0, blocking collectives: 158 us -> none  [per_device(): total_sq = lax.psum(jnp.sum(residual * residual), ('section', 'dom'))]
    pallas_call x0 -> x7, Pallas kernels: none -> 31.4 us  [call(): pl.pallas_call(kernel, out_shape=[jax.ShapeDtypeStruct(s, d) for s, d in...]
    all_gather x3 -> x0, blocking collectives: 27 us -> none  [prefix(): gathered = jax.tree.map(lambda a: lax.all_gather(a, axis), part)]
    all_to_all x0 -> x5, starting transfers between devices: none -> 25.5 us  [gather(): return lax.all_to_all(msg, everywhere, 0, 0, tiled=False)]
    dot_general x44 -> x0, matrix products: 23.2 us -> none  [the longest x28 8.9 us: block_apply(): return jnp.einsum('kij,tkj->tki', matrices, values, precision=HIGH)]
    ppermute x0 -> x12, starting transfers between devices: none -> 16.4 us  [the longest x8 15 us: pair(): return lax.ppermute(x, everywhere, links)]
    ppermute x0 -> x12, waiting for transfers between devices: none -> 15.3 us  [the longest x8 14 us: pair(): return lax.ppermute(x, everywhere, links)]
  transfers between devices with their start and end apart: 4 -> 17, of which waited for: 4 -> 10; matrix products, arithmetic and copies ran while one was open for 1% -> 2% of each run, Pallas kernels for 0% -> 9%
where the time goes in v1:
time: 109 us; the launch traced here: 108 us
  starting transfers between devices  42 us (39%)
  Pallas kernels  31.4 us (29%)
  waiting for transfers between devices  25.7 us (24%)
  local copies, waits for them, and re-layouts  5.99 us (5%)
  other arithmetic  2.18 us (2%)
    pallas_call x7, Pallas kernels, call(): pl.pallas_call(kernel, out_shape=[jax.ShapeDtypeStruct(s, d) for s, d in...  31.4 us
    all_to_all x5, starting transfers between devices, gather(): return lax.all_to_all(msg, everywhere, 0, 0, tiled=False)  25.5 us
    ppermute x8, starting transfers between devices, pair(): return lax.ppermute(x, everywhere, links)  15 us
    ppermute x8, waiting for transfers between devices, pair(): return lax.ppermute(x, everywhere, links)  14 us
    all_to_all x5, waiting for transfers between devices, gather(): return lax.all_to_all(msg, everywhere, 0, 0, tiled=False)  10.3 us
    unnamed x46, local copies, waits for them, and re-layouts  5.47 us
  transfers between devices with their start and end apart: 17, of which 10 were waited for; matrix products, arithmetic and copies ran while one was open for 2% of the time, Pallas kernels for 9%

profile of v1, /device:TPU:0, one launch (start us, length us, event | category | flops | bytes accessed | tf_op | source)
XLA Modules:
  0.0 108.1 jit_solution(8561680385293919209)
XLA Ops:
  1.2 2.4 %shard_map.113 = (f32[32,8,128]{2,1,0:T(8,128)}, f32[40,256]{1,0:T(8,128)}) custom-call(f32[32,256]{1,0:T(8,128)} %bitcast.20, f32[1,256]{1,0:T(1,128)} %initial.1, f32[1,256]{1,0:T(1,128)} %capacitance.1, f32[2,128,128]{2,1,0:T(8,128)} %bitcast.17, f32[256,512]{1,0:T(8,128)} %bitcast.15, s32[1,128]{1,0:T(1,128)} %tap.1, s32[1,128]{1,0:T(1,128)} %drive.1, ...), custom_call_target="tpu_custom_call" | custom-call | tf_op jit(solution)/shard_map/pallas_call | solution.py:333
  3.6 6.9 %all-to-all-start = ((f32[32,8,128]{2,1,0:T(8,128)}), f32[32,8,128]{2,1,0:T(8,128)S(1)}, u32[]{:S(2)}, u32[]{:S(2)}) async-start(f32[32,8,128]{2,1,0:T(8,128)} %get-tuple-element.42), calls=%async_computation | async-start | bytes 262144 | tf_op jit(solution)/shard_map/all_to_all | solution.py:388
  13.6 7.3 %shard_map.114 = (bf16[512,512]{1,0:T(8,128)(2,1)}, bf16[512,512]{1,0:T(8,128)(2,1)}, bf16[512,512]{1,0:T(8,128)(2,1)}, bf16[512,512]{1,0:T(8,128)(2,1)}, bf16[8...) custom-call(f32[256,512]{1,0:T(8,128)} %copy-done.4, ...), custom_call_target="tpu_custom_call" | custom-call | tf_op jit(solution)/shard_map/pallas_call | solution.py:333
  21.6 4.9 %shard_map.115 = (f32[32,512]{1,0:T(8,128)}, f32[32,512]{1,0:T(8,128)}, f32[32,512]{1,0:T(8,128)}, f32[32,512]{1,0:T(8,128)}, f32[32,512]{1,0:T(8,128)}, /*index...) custom-call(s32[3]{0:T(128)} %pad_add_fusion.info.refs_0_, f32[32,8,128]{2,1,0:T(8,128)} %copy-done, ...), custom_call_target="tpu_custom_call" | custom-call | tf_op jit(solution)/shard_map/pallas_call | solution.py:333
  26.5 5.8 %all-to-all-start.1 = ((f32[32,8,128]{2,1,0:T(8,128)}), f32[32,8,128]{2,1,0:T(8,128)S(1)}, u32[]{:S(2)}, u32[]{:S(2)}) async-start(f32[32,8,128]{2,1,0:T(8,128)} %get-tuple-element.51), calls=%async_computation.1 | async-start | bytes 262144 | tf_op jit(solution)/shard_map/all_to_all | solution.py:388
  32.3 1.8 %collective-permute-start.3 = (f32[32,512]{1,0:T(8,128)S(1)}, f32[32,512]{1,0:T(8,128)S(1)}, u32[]{:S(2)}, u32[]{:S(2)}) collective-permute-start(f32[32,512]{1,0:T(8,128)S(1)} %copy-done.18), channel_id=1, source_target_pairs={{0,8},{1,3},{2,10},{3,1},{4,12},{5,7},{6,14},{7,5},{8,0},{9,11},{1... | collective-permute-start | bytes 196616 | tf_op jit(solution)/shard_map/ppermute | solution.py:379
  34.1 2.8 %collective-permute-done.3 = f32[32,512]{1,0:T(8,128)S(1)} collective-permute-done((f32[32,512]{1,0:T(8,128)S(1)}, f32[32,512]{1,0:T(8,128)S(1)}, u32[]{:S(2)}, u32[]{:S(2)}) %collective-permute-start.3) | collective-permute-done | bytes 65568 | tf_op jit(solution)/shard_map/ppermute | solution.py:379
  36.9 1.9 %collective-permute-start.4 = (f32[32,512]{1,0:T(8,128)S(1)}, f32[32,512]{1,0:T(8,128)S(1)}, u32[]{:S(2)}, u32[]{:S(2)}) collective-permute-start(f32[32,512]{1,0:T(8,128)S(1)} %add.21.refs_2_), channel_id=1, source_target_pairs={{0,8},{1,5},{2,10},{3,7},{4,12},{5,1},{6,14},{7,3},{8,0},{9,13},{1... | collective-permute-start | bytes 196616 | tf_op jit(solution)/shard_map/ppermute | solution.py:379
  38.8 2.4 %collective-permute-done.4.refs_3_ = f32[32,512]{1,0:T(8,128)S(1)} collective-permute-done((f32[32,512]{1,0:T(8,128)S(1)}, f32[32,512]{1,0:T(8,128)S(1)}, u32[]{:S(2)}, u32[]{:S(2)}) %collective-permute-start.4) | collective-permute-done | bytes 65568 | tf_op jit(solution)/shard_map/ppermute | solution.py:379
  41.9 5.1 %shard_map.116 = (f32[32,512]{1,0:T(8,128)}, f32[32,512]{1,0:T(8,128)}, f32[32,512]{1,0:T(8,128)}, f32[32,512]{1,0:T(8,128)}, f32[32,512]{1,0:T(8,128)}, /*index...) custom-call(s32[3]{0:T(128)} %pad_add_fusion.info.refs_0_, f32[32,8,128]{2,1,0:T(8,128)} %copy-done.3, ...), custom_call_target="tpu_custom_call" | custom-call | tf_op jit(solution)/shard_map/pallas_call | solution.py:333
  47.0 1.9 %collective-permute-start.7 = (f32[64,256]{1,0:T(8,128)}, f32[64,256]{1,0:T(8,128)S(1)}, u32[]{:S(2)}, u32[]{:S(2)}) collective-permute-start(f32[64,256]{1,0:T(8,128)} %get-tuple-element.65), channel_id=1, source_target_pairs={{0,2},{1,9},{2,0},{3,11},{4,6},{5,13},{6,4},{7,15},{8,10},{9,1},{1... | collective-permute-start | bytes 196616 | tf_op jit(solution)/shard_map/ppermute | solution.py:379
  52.6 2.4 %collective-permute-start.8 = (f32[64,256]{1,0:T(8,128)S(1)}, f32[64,256]{1,0:T(8,128)S(1)}, u32[]{:S(2)}, u32[]{:S(2)}) collective-permute-start(f32[64,256]{1,0:T(8,128)S(1)} %multiply_add_fusion.1), channel_id=1, source_target_pairs={{0,2},{1,17},{2,0},{3,19},{4,6},{5,21},{6,4},{7,23},{8,10},{9,25},... | collective-permute-start | bytes 196616 | tf_op jit(solution)/shard_map/ppermute | solution.py:379
  55.0 4.3 %all-to-all-start.2 = ((f32[32,8,128]{2,1,0:T(8,128)}), f32[32,8,128]{2,1,0:T(8,128)S(1)}, u32[]{:S(2)}, u32[]{:S(2)}) async-start(f32[32,8,128]{2,1,0:T(8,128)} %get-tuple-element.58), calls=%async_computation.2 | async-start | bytes 262144 | tf_op jit(solution)/shard_map/all_to_all | solution.py:388
  59.4 1.8 %collective-permute-start.6 = (f32[32,512]{1,0:T(8,128)S(1)}, f32[32,512]{1,0:T(8,128)S(1)}, u32[]{:S(2)}, u32[]{:S(2)}) collective-permute-start(f32[32,512]{1,0:T(8,128)S(1)} %add.22.refs_2_), channel_id=1, source_target_pairs={{0,8},{1,5},{2,10},{3,7},{4,12},{5,1},{6,14},{7,3},{8,0},{9,13},{1... | collective-permute-start | bytes 196616 | tf_op jit(solution)/shard_map/ppermute | solution.py:379
  61.9 2.2 %collective-permute-done.6.refs_3_ = f32[32,512]{1,0:T(8,128)S(1)} collective-permute-done((f32[32,512]{1,0:T(8,128)S(1)}, f32[32,512]{1,0:T(8,128)S(1)}, u32[]{:S(2)}, u32[]{:S(2)}) %collective-permute-start.6) | collective-permute-done | bytes 65568 | tf_op jit(solution)/shard_map/ppermute | solution.py:379
  64.1 3.5 %all-to-all-done.2.refs_1_ = f32[32,8,128]{2,1,0:T(8,128)S(1)} async-done(((f32[32,8,128]{2,1,0:T(8,128)}), f32[32,8,128]{2,1,0:T(8,128)S(1)}, u32[]{:S(2)}, u32[]{:S(2)}) %all-to-all-start.2) | async-done | bytes 131104 | tf_op jit(solution)/shard_map/all_to_all | solution.py:388
  68.3 5.1 %shard_map.117 = (f32[32,512]{1,0:T(8,128)}, f32[32,512]{1,0:T(8,128)}, f32[32,512]{1,0:T(8,128)}, f32[32,512]{1,0:T(8,128)}, f32[32,512]{1,0:T(8,128)}, /*index=5*/f32[32,8,128]{2,1,0:T(8,128)}, f32[1,128]{1,0:T(1,128)}) custom-call(s32[3]{0:T(128)} %pad_add_fusion.info.refs_0_, f32[32,8,128]{2,1,0:T(8,128)} %copy-done.1, f32[32,512]{1,0:T(8,128)} %copy-done.8, ...), custom_call_target="tpu_custom_call" | custom-call | tf_op jit(solution)/shard_map/pallas_call | solution.py:333
  73.4 2.8 %all-to-all-start.3 = ((f32[32,8,128]{2,1,0:T(8,128)}), f32[32,8,128]{2,1,0:T(8,128)S(1)}, u32[]{:S(2)}, u32[]{:S(2)}) async-start(f32[32,8,128]{2,1,0:T(8,128)} %get-tuple-element.67), calls=%async_computation.3 | async-start | bytes 262144 | tf_op jit(solution)/shard_map/all_to_all | solution.py:388
  78.1 2.8 %collective-permute-done.9 = f32[32,512]{1,0:T(8,128)S(1)} collective-permute-done((f32[32,512]{1,0:T(8,128)S(1)}, f32[32,512]{1,0:T(8,128)S(1)}, u32[]{:S(2)}, u32[]{:S(2)}) %collective-permute-start.9) | collective-permute-done | bytes 65568 | tf_op jit(solution)/shard_map/ppermute | solution.py:379
  80.8 1.9 %collective-permute-start.10 = (f32[32,512]{1,0:T(8,128)S(1)}, f32[32,512]{1,0:T(8,128)S(1)}, u32[]{:S(2)}, u32[]{:S(2)}) collective-permute-start(f32[32,512]{1,0:T(8,128)S(1)} %add.25.refs_2_), channel_id=1, source_target_pairs={{0,8},{1,5},{2,10},{3,7},{4,12},{5,1},{6,14},{7,3},{8,0},{9,13},{1... | collective-permute-start | bytes 196616 | tf_op jit(solution)/shard_map/ppermute | solution.py:379
  82.7 2.4 %collective-permute-done.10.refs_3_ = f32[32,512]{1,0:T(8,128)S(1)} collective-permute-done((f32[32,512]{1,0:T(8,128)S(1)}, f32[32,512]{1,0:T(8,128)S(1)}, u32[]{:S(2)}, u32[]{:S(2)}) %collective-permute-start.10) | collective-permute-done | bytes 65568 | tf_op jit(solution)/shard_map/ppermute | solution.py:379
  85.9 4.8 %shard_map.118 = (f32[32,512]{1,0:T(8,128)}, f32[32,512]{1,0:T(8,128)}, f32[32,512]{1,0:T(8,128)}, f32[32,512]{1,0:T(8,128)}, f32[64,256]{1,0:T(8,128)}, /*index=5*/f32[32,8,128]{2,1,0:T(8,128)}, f32[1,128]{1,0:T(1,128)}) custom-call(s32[3]{0:T(128)} %pad_add_fusion.info.refs_0_, f32[32,8,128]{2,1,0:T(8,128)} %copy-done.2, f32[32,512]{1,0:T(8,128)} %copy-done.9, ...), custom_call_target="tpu_custom_call" | custom-call | tf_op jit(solution)/shard_map/pallas_call | solution.py:333
  90.7 5.7 %all-to-all-start.4 = ((f32[32,8,128]{2,1,0:T(8,128)}), f32[32,8,128]{2,1,0:T(8,128)S(1)}, u32[]{:S(2)}, u32[]{:S(2)}) async-start(f32[32,8,128]{2,1,0:T(8,128)} %get-tuple-element.73), calls=%async_computation.4 | async-start | bytes 262144 | tf_op jit(solution)/shard_map/all_to_all | solution.py:388
  97.8 6.8 %all-to-all-done.4.got = f32[32,8,128]{2,1,0:T(8,128)S(1)} async-done(((f32[32,8,128]{2,1,0:T(8,128)}), f32[32,8,128]{2,1,0:T(8,128)S(1)}, u32[]{:S(2)}, u32[]{:S(2)}) %all-to-all-start.4) | async-done | bytes 131104 | tf_op jit(solution)/shard_map/all_to_all | solution.py:388
  (71 shorter events, 17.3 us)
Async XLA Ops:
  0.6 11.5 %collective-permute-start.1 = (f32[256,512]{1,0:T(8,128)}, f32[256,512]{1,0:T(8,128)S(1)}, u32[]{:S(2)}, u32[]{:S(2)}) collective-permute-start(f32[256,512]{1,0:T(8,128)} %bitcast.14), channel_id=1, source_target_pairs={{0,1},{1,0},{2,3},{3,2},{4,5},{5,4},{6,7},{7,6},{8,9},{9,8},{10,11... | collective-permute-start | bytes 1572872 | tf_op jit(solution)/shard_map/ppermute | solution.py:371
  3.6 7.0 %copy-start.11 = (f32[1,2,128,128]{3,2,1,0:T(8,128)S(1)}, f32[1,2,128,128]{3,2,1,0:T(8,128)}, u32[]{:S(2)}) copy-start(f32[1,2,128,128]{3,2,1,0:T(8,128)} %param.14) | copy-start | bytes 393220
  3.6 7.3 %copy-start.6 = (f32[40,256]{1,0:T(8,128)S(1)}, f32[40,256]{1,0:T(8,128)}, u32[]{:S(2)}) copy-start(f32[40,256]{1,0:T(8,128)} %get-tuple-element.43.p_own.refs_17_) | copy-start | bytes 122884
  3.6 17.3 %all-to-all-start = ((f32[32,8,128]{2,1,0:T(8,128)}), f32[32,8,128]{2,1,0:T(8,128)S(1)}, u32[]{:S(2)}, u32[]{:S(2)}) async-start(f32[32,8,128]{2,1,0:T(8,128)} %get-tuple-element.42), calls=%async_computation | async-start | bytes 262144 | tf_op jit(solution)/shard_map/all_to_all | solution.py:388
  10.6 1.5 %collective-permute-start.2 = (f32[2,128,128]{2,1,0:T(8,128)S(1)}, f32[2,128,128]{2,1,0:T(8,128)S(1)}, u32[]{:S(2)}, u32[]{:S(2)}) collective-permute-start(f32[2,128,128]{2,1,0:T(8,128)S(1)} %bitcast.19), channel_id=1, source_target_pairs={{0,1},{1,0},{2,3},{3,2},{4,5},{5,4},{6,7},{7,6},{8,9},{9,8},{10,11... | collective-permute-start | bytes 393224 | tf_op jit(solution)/shard_map/ppermute | solution.py:371
  10.9 1.2 %collective-permute-start = (f32[40,256]{1,0:T(8,128)S(1)}, f32[40,256]{1,0:T(8,128)S(1)}, u32[]{:S(2)}, u32[]{:S(2)}) collective-permute-start(f32[40,256]{1,0:T(8,128)S(1)} %copy-done.6), channel_id=1, source_target_pairs={{0,1},{1,0},{2,3},{3,2},{4,5},{5,4},{6,7},{7,6},{8,9},{9,8},{10,11... | collective-permute-start | bytes 122888 | tf_op jit(solution)/shard_map/ppermute | solution.py:371
  26.5 5.8 %copy-start.18 = (f32[32,512]{1,0:T(8,128)S(1)}, f32[32,512]{1,0:T(8,128)}, u32[]{:S(2)}) copy-start(f32[32,512]{1,0:T(8,128)} %get-tuple-element.52) | copy-start | bytes 196612
  26.5 14.8 %all-to-all-start.1 = ((f32[32,8,128]{2,1,0:T(8,128)}), f32[32,8,128]{2,1,0:T(8,128)S(1)}, u32[]{:S(2)}, u32[]{:S(2)}) async-start(f32[32,8,128]{2,1,0:T(8,128)} %get-tuple-element.51), calls=%async_computation.1 | async-start | bytes 262144 | tf_op jit(solution)/shard_map/all_to_all | solution.py:388
  32.3 4.6 %collective-permute-start.3 = (f32[32,512]{1,0:T(8,128)S(1)}, f32[32,512]{1,0:T(8,128)S(1)}, u32[]{:S(2)}, u32[]{:S(2)}) collective-permute-start(f32[32,512]{1,0:T(8,128)S(1)} %copy-done.18), channel_id=1, source_target_pairs={{0,8},{1,3},{2,10},{3,1},{4,12},{5,7},{6,14},{7,5},{8,0},{9,11},{1... | collective-permute-start | bytes 196616 | tf_op jit(solution)/shard_map/ppermute | solution.py:379
  36.9 4.4 %copy-start.10 = (f32[32,512]{1,0:T(8,128)}, f32[32,512]{1,0:T(8,128)S(1)}, u32[]{:S(2)}) copy-start(f32[32,512]{1,0:T(8,128)S(1)} %add.21.refs_2_) | copy-start | bytes 196612
  36.9 4.3 %collective-permute-start.4 = (f32[32,512]{1,0:T(8,128)S(1)}, f32[32,512]{1,0:T(8,128)S(1)}, u32[]{:S(2)}, u32[]{:S(2)}) collective-permute-start(f32[32,512]{1,0:T(8,128)S(1)} %add.21.refs_2_), channel_id=1, source_target_pairs={{0,8},{1,5},{2,10},{3,7},{4,12},{5,1},{6,14},{7,3},{8,0},{9,13},{1... | collective-permute-start | bytes 196616 | tf_op jit(solution)/shard_map/ppermute | solution.py:379
  41.9 7.0 %copy-start.20 = (f32[6,256]{1,0:T(8,128)S(1)}, f32[6,256]{1,0:T(8,128)}, u32[]{:S(2)}) copy-start(f32[6,256]{1,0:T(8,128)} %get-tuple-element.64) | copy-start | bytes 18436
  47.0 4.7 %collective-permute-start.7 = (f32[64,256]{1,0:T(8,128)}, f32[64,256]{1,0:T(8,128)S(1)}, u32[]{:S(2)}, u32[]{:S(2)}) collective-permute-start(f32[64,256]{1,0:T(8,128)} %get-tuple-element.65), channel_id=1, source_target_pairs={{0,2},{1,9},{2,0},{3,11},{4,6},{5,13},{6,4},{7,15},{8,10},{9,1},{1... | collective-permute-start | bytes 196616 | tf_op jit(solution)/shard_map/ppermute | solution.py:379
  49.0 10.4 %collective-permute-start.5 = (f32[32,512]{1,0:T(8,128)}, f32[32,512]{1,0:T(8,128)S(1)}, u32[]{:S(2)}, u32[]{:S(2)}) collective-permute-start(f32[32,512]{1,0:T(8,128)} %get-tuple-element.59), channel_id=1, source_target_pairs={{0,8},{1,3},{2,10},{3,1},{4,12},{5,7},{6,14},{7,5},{8,0},{9,11},{1... | collective-permute-start | bytes 196616 | tf_op jit(solution)/shard_map/ppermute | solution.py:379
  52.6 8.7 %collective-permute-start.8 = (f32[64,256]{1,0:T(8,128)S(1)}, f32[64,256]{1,0:T(8,128)S(1)}, u32[]{:S(2)}, u32[]{:S(2)}) collective-permute-start(f32[64,256]{1,0:T(8,128)S(1)} %multiply_add_fusion.1), channel_id=1, source_target_pairs={{0,2},{1,17},{2,0},{3,19},{4,6},{5,21},{6,4},{7,23},{8,10},{9,25},... | collective-permute-start | bytes 196616 | tf_op jit(solution)/shard_map/ppermute | solution.py:379
  55.0 12.6 %all-to-all-start.2 = ((f32[32,8,128]{2,1,0:T(8,128)}), f32[32,8,128]{2,1,0:T(8,128)S(1)}, u32[]{:S(2)}, u32[]{:S(2)}) async-start(f32[32,8,128]{2,1,0:T(8,128)} %get-tuple-element.58), calls=%async_computation.2 | async-start | bytes 262144 | tf_op jit(solution)/shard_map/all_to_all | solution.py:388
  59.4 4.7 %collective-permute-start.6 = (f32[32,512]{1,0:T(8,128)S(1)}, f32[32,512]{1,0:T(8,128)S(1)}, u32[]{:S(2)}, u32[]{:S(2)}) collective-permute-start(f32[32,512]{1,0:T(8,128)S(1)} %add.22.refs_2_), channel_id=1, source_target_pairs={{0,8},{1,5},{2,10},{3,7},{4,12},{5,1},{6,14},{7,3},{8,0},{9,13},{1... | collective-permute-start | bytes 196616 | tf_op jit(solution)/shard_map/ppermute | solution.py:379
  73.4 11.7 %all-to-all-start.3 = ((f32[32,8,128]{2,1,0:T(8,128)}), f32[32,8,128]{2,1,0:T(8,128)S(1)}, u32[]{:S(2)}, u32[]{:S(2)}) async-start(f32[32,8,128]{2,1,0:T(8,128)} %get-tuple-element.67), calls=%async_computation.3 | async-start | bytes 262144 | tf_op jit(solution)/shard_map/all_to_all | solution.py:388
  76.2 4.6 %collective-permute-start.9 = (f32[32,512]{1,0:T(8,128)S(1)}, f32[32,512]{1,0:T(8,128)S(1)}, u32[]{:S(2)}, u32[]{:S(2)}) collective-permute-start(f32[32,512]{1,0:T(8,128)S(1)} %copy-done.17), channel_id=1, source_target_pairs={{0,8},{1,3},{2,10},{3,1},{4,12},{5,7},{6,14},{7,5},{8,0},{9,11},{1... | collective-permute-start | bytes 196616 | tf_op jit(solution)/shard_map/ppermute | solution.py:379
  80.8 4.3 %collective-permute-start.10 = (f32[32,512]{1,0:T(8,128)S(1)}, f32[32,512]{1,0:T(8,128)S(1)}, u32[]{:S(2)}, u32[]{:S(2)}) collective-permute-start(f32[32,512]{1,0:T(8,128)S(1)} %add.25.refs_2_), channel_id=1, source_target_pairs={{0,8},{1,5},{2,10},{3,7},{4,12},{5,1},{6,14},{7,3},{8,0},{9,13},{1... | collective-permute-start | bytes 196616 | tf_op jit(solution)/shard_map/ppermute | solution.py:379
  90.7 5.7 %copy-start.21 = (f32[64,256]{1,0:T(8,128)S(1)}, f32[64,256]{1,0:T(8,128)}, u32[]{:S(2)}) copy-start(f32[64,256]{1,0:T(8,128)} %get-tuple-element.76) | copy-start | bytes 196612
  90.7 13.9 %all-to-all-start.4 = ((f32[32,8,128]{2,1,0:T(8,128)}), f32[32,8,128]{2,1,0:T(8,128)S(1)}, u32[]{:S(2)}, u32[]{:S(2)}) async-start(f32[32,8,128]{2,1,0:T(8,128)} %get-tuple-element.73), calls=%async_computation.4 | async-start | bytes 262144 | tf_op jit(solution)/shard_map/all_to_all | solution.py:388
  96.5 1.3 %collective-permute-start.11 = (f32[64,256]{1,0:T(8,128)S(1)}, f32[64,256]{1,0:T(8,128)S(1)}, u32[]{:S(2)}, u32[]{:S(2)}) collective-permute-start(f32[64,256]{1,0:T(8,128)S(1)} %copy-done.21), channel_id=1, source_target_pairs={{0,1},{1,0},{2,3},{3,2},{4,5},{5,4},{6,7},{7,6},{8,9},{9,8},{10,11... | collective-permute-start | bytes 196616 | tf_op jit(solution)/shard_map/ppermute | solution.py:371
  97.8 6.8 %copy-start.19 = (f32[64,256]{1,0:T(8,128)}, f32[64,256]{1,0:T(8,128)S(1)}, u32[]{:S(2)}) copy-start(f32[64,256]{1,0:T(8,128)S(1)} %collective-permute-done.11.given) | copy-start | bytes 196612
  (16 other events, 24.8 us)

commit v2 on v1

v2 whole, which is shorter than its diff:
```python
import functools

import jax
import jax.numpy as jnp
from jax import lax
from jax.experimental import pallas as pl
from jax.experimental.pallas import tpu as pltpu
from jax.sharding import PartitionSpec as P


NEWTON = 2
SWEEPS = 2
HIGHEST = lax.Precision.HIGHEST
F32 = jnp.float32
BF16 = jnp.bfloat16
LANES = 128
SUB = 8


def fdot(a, b):
    return jnp.dot(a, b, precision=HIGHEST, preferred_element_type=F32)


def dot6(a, b):
    return fdot(a, b)


def bdot(a, b):
    return jnp.dot(a, b, preferred_element_type=F32)


def tdot(a, b):
    return lax.dot_general(a, b, (((1,), (1,)), ((), ())), preferred_element_type=F32)


def split(x):
    high = x.astype(BF16)
    return high, (x - high.astype(F32)).astype(BF16)


def dot3(x, high, low):
    rows = x.shape[0]
    xh, xl = split(x)
    both = bdot(jnp.concatenate([xh, xl], axis=0), high)
    return both[:rows] + both[rows:] + bdot(xh, low)


def dot2(x, exact):
    rows = x.shape[0]
    xh, xl = split(x)
    both = bdot(jnp.concatenate([xh, xl], axis=0), exact)
    return both[:rows] + both[rows:]


def lag(x, offset):
    if offset == 0:
        return x
    if offset >= x.shape[0]:
        return jnp.zeros_like(x)
    if offset % SUB == 0:
        return jnp.concatenate([jnp.zeros((offset, x.shape[1]), F32), x[: x.shape[0] - offset]], axis=0)
    row = lax.broadcasted_iota(jnp.int32, x.shape, 0)
    return jnp.where(row >= offset, pltpu.roll(x, offset, 0), 0.0)


def stages(steps):
    plan = [(0, 1)]
    span = 2
    while span < steps:
        wide = 2
        plan.append(tuple(span * i for i in range(1, wide)))
        span *= wide
    return plan


def powers_of(plan):
    return [p for stage in plan[1:] for p in stage]


def tile_sum(x):
    total = None
    for i in range(0, x.shape[0], SUB):
        for j in range(0, x.shape[1], LANES):
            part = x[i : i + SUB, j : j + LANES]
            total = part if total is None else total + part
    return total


def first_kernel(source, initial, capacitance, matrix, weight, tap, drive, gain, att, msg, pack,
                 b_initial, b_capacitance, b_matrix, b_weight, b_tap, b_drive, b_gain, b_att, sems):
    steps, nodes = source.shape
    blocks, width = matrix.shape[0], matrix.shape[1]
    channels = tap.shape[1]
    moves = [(initial, b_initial), (weight, b_weight), (att, b_att), (tap, b_tap), (matrix, b_matrix),
             (capacitance, b_capacitance), (drive, b_drive), (gain, b_gain), (source, pack.at[0:steps, :])]
    copies = [pltpu.make_async_copy(src, dst, sems.at[i]) for i, (src, dst) in enumerate(moves)]
    for copy in copies:
        copy.start()
    pack[steps : steps + SUB, :] = jnp.zeros((SUB, nodes), F32)
    for copy in copies:
        copy.wait()
    start = b_initial[...]
    net = dot6(start, b_weight[...])
    rows = []
    for j in range(0, net.shape[1], LANES):
        rows.append(net[:, j : j + LANES])
    node = lax.broadcasted_iota(jnp.int32, (nodes, channels), 0)
    taps = fdot(start, (node == b_tap[...]).astype(F32))
    for row in (taps, b_att[...]):
        for j in range(0, channels, LANES):
            rows.append(row[:, j : j + LANES])
    assert len(rows) <= SUB
    rows += [jnp.zeros((1, LANES), F32)] * (SUB - len(rows))
    tile = jnp.concatenate(rows, axis=0)
    msg[...] = jnp.broadcast_to(tile[None], msg.shape)
    parts = []
    for k in range(blocks):
        parts.append(
            lax.dot_general(
                start[:, k * width : (k + 1) * width],
                b_matrix[k],
                (((1,), (1,)), ((), ())),
                precision=HIGHEST,
                preferred_element_type=F32,
            )
        )
    held = jnp.concatenate(parts, axis=1) - b_capacitance[...] * start
    for i, row in enumerate((held, start, b_capacitance[...])):
        pack[steps + i : steps + i + 1, :] = row
    for i, row in enumerate((b_gain[...], b_tap[...].astype(F32), b_drive[...].astype(F32))):
        pack[steps + 3 + i : steps + 4 + i, 0:channels] = row


def both(ref_other, ref_own, lo, hi):
    return jnp.concatenate([ref_other[lo:hi, :], ref_own[lo:hi, :]], axis=1)


def prep_kernel(plan, steps, w_other, w_own, i_other, i_own, p_other, p_own, th, tl, wh, wl, ah, al,
                b_w, b_i, s_wh, s_wl, sems):
    nodes = w_own.shape[0]
    blocks, width = i_own.shape[0], i_own.shape[1]
    moves = [(i_other, b_i.at[0]), (i_own, b_i.at[1]), (w_other, b_w.at[0]), (w_own, b_w.at[1])]
    copies = [pltpu.make_async_copy(src, dst, sems.at[i]) for i, (src, dst) in enumerate(moves)]
    for copy in copies:
        copy.start()
    cap = both(p_other, p_own, steps + 2, steps + 3)
    for copy in copies[2:]:
        copy.wait()
    for half in range(2):
        here = slice(half * nodes, (half + 1) * nodes)
        h, l = split(b_w[half])
        s_wh[here, :] = h
        s_wl[here, :] = l
    backs = [pltpu.make_async_copy(s_wh, wh, sems.at[4]), pltpu.make_async_copy(s_wl, wl, sems.at[5])]
    for copy in backs:
        copy.start()
    for copy in copies[:2]:
        copy.wait()
    wanted = powers_of(plan)
    eye = lax.broadcasted_iota(jnp.int32, (width, width), 0) == lax.broadcasted_iota(jnp.int32, (width, width), 1)

    def times(x, y):
        return bdot(x[0], y[0]) + bdot(x[1], y[0]) + bdot(x[0], y[1])

    every = range(2 * blocks)
    inverse = [split(b_i[b // blocks, b % blocks].T) for b in every]
    scale = [split(jnp.where(eye, cap[:, b * width : (b + 1) * width], 0.0)) for b in every]
    made = {1: [split(times(scale[b], inverse[b])) for b in every]}
    todo = [inverse, [split(times(inverse[b], made[1][b])) for b in every]]
    power = 2
    while power <= max(wanted):
        made[power] = [split(times(x, x)) for x in made[power // 2]]
        power *= 2
    for p in wanted:
        if p not in made:
            top = 1 << (p.bit_length() - 1)
            made[p] = [split(times(made[top][b], made[p - top][b])) for b in every]
        todo.append(made[p])
    for i, value in enumerate(todo):
        for b in every:
            ah[i, b], al[i, b] = value[b]
    for half in range(2):
        here = slice(half * nodes, (half + 1) * nodes)
        h, l = split(b_w[half].T)
        th[:, here] = h
        tl[:, here] = l
    for copy in backs:
        copy.wait()


def march(plan, r, ah, al):
    blocks, width = ah.shape[1], ah.shape[2]
    out = []
    for b in range(blocks):
        x = r[:, b * width : (b + 1) * width]
        unit = 0
        for s, stage in enumerate(plan):
            total = None
            for offset in stage:
                part = dot3(lag(x, offset), ah[unit, b], al[unit, b])
                total = part if total is None else total + part
                unit += 1
            x = total if s == 0 else total + x
        out.append(x)
    return jnp.concatenate(out, axis=1)


def fetch(wh, wl, b_wh, b_wl, sems):
    copies = [pltpu.make_async_copy(wh, b_wh, sems.at[0]), pltpu.make_async_copy(wl, b_wl, sems.at[1])]
    for copy in copies:
        copy.start()
    return copies


def send_squares(r, north, msg):
    row = jnp.sum(tile_sum(r * r), axis=0, keepdims=True) * north
    msg[...] = jnp.broadcast_to(row[None], msg.shape)


def finish_round(plan, r, c_ref, p_ref, msg, ah, al, copies, b_wh, b_wl, north):
    send_squares(r, north, msg)
    c = march(plan, r, ah, al)
    c_ref[...] = c
    for copy in copies:
        copy.wait()
    p_ref[...] = dot3(c, b_wh[...], b_wl[...])
    return c


def opening_kernel(plan, steps, channels, sections, doms, levels, info, got, p_other, p_own, ah, al, th, tl, wh, wl,
                   w_ref, q_ref, c_ref, p_ref, msg, aux_ref, b_wh, b_wl, sems):
    copies = fetch(wh, wl, b_wh, b_wl, sems)
    my, chip = info[0], info[1]
    north = info[2].astype(F32)
    nets = th.shape[0]
    net_rows = nets // LANES
    tap_rows = channels // LANES
    mine = jnp.zeros((SUB, LANES), F32)
    base = my * doms
    for d in range(doms):
        mine = mine + got[base + d]
    net = jnp.concatenate([mine[i : i + 1, :] for i in range(net_rows)], axis=1)

    def channel_row(s, first):
        pieces = []
        for half in range(2):
            tile = got[s * doms + 2 * chip + half]
            pieces += [tile[first + i : first + i + 1, :] for i in range(tap_rows)]
        return jnp.concatenate(pieces, axis=1)

    decay, carried, drive = [], None, jnp.zeros((1, 2 * channels), F32)
    for s in range(sections):
        a = channel_row(s, net_rows + tap_rows)
        decay.append(a)
        if carried is not None:
            drive = jnp.where(my == s, carried, drive)
        tapped = channel_row(s, net_rows)
        carried = tapped if carried is None else a * carried + tapped
    one = jnp.ones((1, 2 * channels), F32)
    rows = []
    for level in range(levels):
        bit = (my >> level) & 1
        own_a, other_a, past_a = one, one, one
        for s in range(sections):
            here = s >> level
            own_a = jnp.where(here == (my >> level), own_a * decay[s], own_a)
            other_a = jnp.where(here == ((my >> level) ^ 1), other_a * decay[s], other_a)
            past_a = jnp.where((here == (my >> level)) & (s < my), past_a * decay[s], past_a)
        rows += [jnp.where(bit == 1, one, other_a), jnp.where(bit == 1, own_a, one), jnp.where(bit == 1, past_a, 0.0)]
    nodes = p_own.shape[1]
    kept = [
        jnp.concatenate([p_other[i : i + 1, 0:channels], p_own[i : i + 1, 0:channels]], axis=1)
        for i in (steps + 3, steps + 4, steps + 5)
    ]
    inj = spread(jnp.broadcast_to(drive * kept[0], (SUB, 2 * channels)), kept[2], nodes)[0:1]
    aux_ref[...] = jnp.zeros_like(aux_ref)
    aux_ref[0:1, 0 : inj.shape[1]] = inj
    for i, row in enumerate(kept + rows):
        aux_ref[1 + i : 2 + i, 0 : 2 * channels] = row
    back = dot3(jnp.broadcast_to(net, (SUB, nets)), th[...], tl[...])[0:1]
    start = both(p_other, p_own, steps + 1, steps + 2)
    held = both(p_other, p_own, steps, steps + 1)
    q = (held + back - inj) - both(p_other, p_own, 0, steps)
    r = q + 0.5 * jnp.tanh(start)
    w_ref[...] = jnp.broadcast_to(start, w_ref.shape)
    q_ref[...] = q
    finish_round(plan, r, c_ref, p_ref, msg, ah, al, copies, b_wh, b_wl, north)


def chosen(index, nodes):
    node = lax.broadcasted_iota(jnp.int32, (nodes, index.shape[1]), 0).astype(F32)
    return (node == index).astype(BF16)


def spread(drive, index, nodes):
    rows = drive.shape[0]
    channels = drive.shape[1] // 2
    out = []
    for h in range(2):
        here = slice(h * channels, (h + 1) * channels)
        xh, xl = split(drive[:, here])
        two = tdot(jnp.concatenate([xh, xl], axis=0), chosen(index[:, here], nodes))
        out.append(two[:rows] + two[rows:])
    return jnp.concatenate(out, axis=1)


def damping_of(got, cells):
    total = got[0]
    for i in range(1, got.shape[0]):
        total = total + got[i]
    mean = jnp.sum(jnp.sum(total, axis=0, keepdims=True), axis=1, keepdims=True) / cells
    return mean, 1.0 / (1.0 + jnp.sqrt(mean))


def advance(got, own, recv, w0, q0, c0, th, tl, cells, mean_ref):
    mean, damp = damping_of(got, cells)
    mean_ref[...] = jnp.broadcast_to(mean, mean_ref.shape)
    back = dot3(own[...] + recv[...], th[...], tl[...])
    w = w0[...] - damp * c0[...]
    q = q0[...] - damp * (q0[...] + 0.5 * jnp.tanh(w0[...]) + back)
    return w, q, damp


def round_kernel(plan, steps, channels, cells, mode, *refs):
    refs = list(refs)
    take = lambda n: [refs.pop(0) for _ in range(n)]
    (info, got, own, recv, w0, q0, c0, ah, al, th, tl, wh, wl, aux) = take(14)
    if mode == "drive":
        (pre,) = take(1)
    w_ref, q_ref, c_ref, p_ref, msg, mean_ref = take(6)
    if mode == "taps":
        (tt_ref,) = take(1)
    b_wh, b_wl, sems = take(3)
    copies = fetch(wh, wl, b_wh, b_wl, sems)
    north = info[2].astype(F32)
    w, q, damp = advance(got, own, recv, w0, q0, c0, th, tl, cells, mean_ref)
    if mode == "drive":
        drive = pre[0:steps, :] - damp * pre[steps : 2 * steps, :]
        gain, _, driven = (aux[i : i + 1, 0 : 2 * channels] for i in (1, 2, 3))
        q = q - (spread(drive * gain, driven, w.shape[1] // 2) - aux[0:1, 0 : w.shape[1]])
    r = q + 0.5 * jnp.tanh(w)
    w_ref[...] = w
    q_ref[...] = q
    c = finish_round(plan, r, c_ref, p_ref, msg, ah, al, copies, b_wh, b_wl, north)
    if mode == "taps":
        half = w.shape[1] // 2
        for h in range(2):
            here = slice(h * half, (h + 1) * half)
            there = slice(h * channels, (h + 1) * channels)
            tapped = chosen(aux[2:3, there], half)
            tt_ref[:, there] = dot2(jnp.concatenate([w[:, here], c[:, here]], axis=0), tapped)


def residual_kernel(cells, info, got, own, recv, w0, q0, c0, th, tl, w_ref, r_ref, msg, mean_ref):
    w, q, _ = advance(got, own, recv, w0, q0, c0, th, tl, cells, mean_ref)
    r = q + 0.5 * jnp.tanh(w)
    w_ref[...] = w
    r_ref[...] = r
    send_squares(r, info[2].astype(F32), msg)


def correct_kernel(plan, w_in, r_in, ah, al, w_ref, c_ref, give):
    steps = r_in.shape[0]
    c = march(plan, r_in[...], ah, al)
    half = c.shape[1] // 2
    w = w_in[...]
    w_ref[...] = w[:, half:]
    c_ref[...] = c[:, half:]
    give[0:steps, :] = w[:, 0:half]
    give[steps : 2 * steps, :] = c[:, 0:half]


def last_kernel(steps, cells, info, got, w, c, given, m1, m2, m3, out, means):
    mean, damp = damping_of(got, cells)
    north = info[2] == 1
    w_here = jnp.where(north, w[...], given[0:steps, :])
    c_here = jnp.where(north, c[...], given[steps : 2 * steps, :])
    out[...] = w_here - damp * c_here
    lane = lax.broadcasted_iota(jnp.int32, (1, LANES), 1)
    row = jnp.where(lane == 0, m1[...], jnp.where(lane == 1, m2[...], jnp.where(lane == 2, m3[...], mean)))
    means[...] = row


def call(kernel, outs, *args, smem=(), hbm=(), hbm_outs=(), scratch=()):
    def place(i, far, scalar=()):
        return pl.BlockSpec(memory_space=pltpu.SMEM if i in scalar else pltpu.HBM if i in far else pltpu.VMEM)

    args = [pltpu.with_memory_space_constraint(x, pltpu.HBM) if i in hbm else x for i, x in enumerate(args)]
    return pl.pallas_call(
        kernel,
        out_shape=[pltpu.HBM(s, d) if i in hbm_outs else jax.ShapeDtypeStruct(s, d) for i, (s, d) in enumerate(outs)],
        in_specs=[place(i, hbm, smem) for i in range(len(args))],
        out_specs=[place(i, hbm_outs) for i in range(len(outs))],
        scratch_shapes=scratch,
        compiler_params=pltpu.CompilerParams(vmem_limit_bytes=16 << 20),
    )(*args)


def per_device(
    source,
    initial,
    capacitance,
    block_matrix,
    block_inverse,
    net_weight,
    tap_nodes,
    drive_nodes,
    drive_gain,
    attenuation,
):
    source = source[0]
    block_matrix = block_matrix[0]
    block_inverse = block_inverse[0]
    net_weight = net_weight[0]
    steps, nodes = source.shape
    blocks, width = block_matrix.shape[:2]
    nets = net_weight.shape[1]
    channels = tap_nodes.shape[1]
    sections, doms = lax.axis_size("section"), lax.axis_size("dom")
    devices = sections * doms
    everywhere = ("section", "dom")
    wide = 2 * nodes
    cells = float(devices * steps * nodes)
    plan = stages(steps)
    units = 2 + len(powers_of(plan))
    levels = max(1, (sections - 1).bit_length())

    def swap(x):
        return lax.ppermute(x, "dom", [(i, i ^ 1) for i in range(doms)])

    def pair(x, odd, even):
        links = []
        for s in range(sections):
            for d in range(doms):
                ps, pd = odd(s, d) if d % 2 else even(s, d)
                links.append((s * doms + d, ps * doms + pd))
        return lax.ppermute(x, everywhere, links)

    def along_dom(x, bit):
        return pair(x, lambda s, d: (s, d ^ (2 << bit)), lambda s, d: (s ^ 1, d))

    def along_section(x, bit):
        return pair(x, lambda s, d: (s ^ (1 << bit), d), lambda s, d: (s, d ^ 2))

    def gather(msg):
        return lax.all_to_all(msg, everywhere, 0, 0, tiled=False)

    place = lax.axis_index("dom")
    info = jnp.stack([lax.axis_index("section"), place // 2, place % 2]).astype(jnp.int32)

    w_other = swap(net_weight)
    i_other = swap(block_inverse)
    first_message = ((devices, SUB, LANES), F32)
    message = ((devices, 1, LANES), F32)
    row = lambda n, d=F32: pltpu.VMEM((1, n), d)
    msg, pack = call(
        first_kernel,
        [first_message, ((steps + SUB, nodes), F32)],
        source, initial, capacitance, block_matrix, net_weight, tap_nodes, drive_nodes, drive_gain, attenuation,
        hbm=range(9),
        scratch=[
            row(nodes), row(nodes), pltpu.VMEM(block_matrix.shape, F32), pltpu.VMEM(net_weight.shape, F32),
            row(channels, jnp.int32), row(channels, jnp.int32), row(channels), row(channels),
            pltpu.SemaphoreType.DMA((9,)),
        ],
    )
    got = gather(msg)
    p_other = swap(pack)
    cut = ((units, 2 * blocks, width, width), BF16)
    th, tl, wh, wl, ah, al = call(
        functools.partial(prep_kernel, plan, steps),
        [((nets, wide), BF16), ((nets, wide), BF16), ((wide, nets), BF16), ((wide, nets), BF16), cut, cut],
        w_other, net_weight, i_other, block_inverse, p_other, pack,
        hbm=range(4),
        hbm_outs=(2, 3),
        scratch=[
            pltpu.VMEM((2, nodes, nets), F32), pltpu.VMEM((2, blocks, width, width), F32),
            pltpu.VMEM((wide, nets), BF16), pltpu.VMEM((wide, nets), BF16), pltpu.SemaphoreType.DMA((6,)),
        ],
    )
    state = [((steps, wide), F32)] * 3
    aux_shape = (-(-(4 + 3 * levels) // SUB) * SUB, max(wide, 2 * channels))
    landing = [pltpu.VMEM((wide, nets), BF16), pltpu.VMEM((wide, nets), BF16), pltpu.SemaphoreType.DMA((2,))]
    w, q, c, part, msg, aux = call(
        functools.partial(opening_kernel, plan, steps, channels, sections, doms, levels),
        state + [((steps, nets), F32), message, (aux_shape, F32)],
        info, got, p_other, pack, ah, al, th, tl, wh, wl,
        smem=(0,),
        hbm=(8, 9),
        scratch=landing,
    )
    means = []
    taps = None
    bits = (doms // 2 - 1).bit_length()
    for index in range(1, NEWTON * SWEEPS):
        own = part
        recv = jnp.zeros_like(part) if bits == 0 else along_dom(own, 0)
        got = gather(msg)
        for bit in range(1, bits):
            own = own + recv
            recv = along_dom(own, bit)
        if index == NEWTON * SWEEPS - 1:
            break
        boundary = index % NEWTON == 0
        before = index % NEWTON == NEWTON - 1
        mode = "drive" if boundary else "taps" if before else "plain"
        extra = []
        if mode == "drive":
            prefix, total = jnp.zeros_like(taps), taps
            mix = aux[4 : 4 + 3 * levels, : 2 * channels]
            for level in range(levels):
                if sections == 1:
                    break
                got_taps = along_section(total, level)
                prefix = prefix + mix[3 * level + 2][None] * got_taps
                total = mix[3 * level][None] * total + mix[3 * level + 1][None] * got_taps
            extra = [prefix]
        outs = state + [((steps, nets), F32), message, ((1, LANES), F32)]
        if mode == "taps":
            outs = outs + [((2 * steps, 2 * channels), F32)]
        result = call(
            functools.partial(round_kernel, plan, steps, channels, cells, mode),
            outs,
            info, got, own, recv, w, q, c, ah, al, th, tl, wh, wl, aux, *extra,
            smem=(0,),
            hbm=(11, 12),
            scratch=landing,
        )
        w, q, c, part, msg, mean = result[:6]
        means.append(mean)
        if mode == "taps":
            taps = result[6]
    w, r, msg, mean = call(
        functools.partial(residual_kernel, cells),
        [((steps, wide), F32), ((steps, wide), F32), message, ((1, LANES), F32)],
        info, got, own, recv, w, q, c, th, tl,
        smem=(0,),
    )
    means.append(mean)
    got = gather(msg)
    w, c, give = call(
        functools.partial(correct_kernel, plan),
        [((steps, nodes), F32), ((steps, nodes), F32), ((2 * steps, nodes), F32)],
        w, r, ah, al,
    )
    given = swap(give)
    out, history = call(
        functools.partial(last_kernel, steps, cells),
        [((steps, nodes), F32), ((1, LANES), F32)],
        info, got, w, c, given, *means,
        smem=(0,),
    )
    return (out[None], history[0, : NEWTON * SWEEPS])


def solution(mesh):
    return jax.shard_map(
        per_device,
        mesh=mesh,
        in_specs=(
            P("section", None, "dom"),
            P("section", "dom"),
            P("section", "dom"),
            P("section", "dom", None, None),
            P("section", "dom", None, None),
            P("section", "dom", None),
            P("section", "dom"),
            P("section", "dom"),
            P("section", "dom"),
            P("section", "dom"),
        ),
        out_specs=(P("section", None, "dom"), P()),
        check_vma=False,
    )
```

time: 109 us -> 87.4 us (0.80)
  blocking collectives: 0 us -> 28.2 us
  starting transfers between devices: 42 us -> 17.4 us
  Pallas kernels: 31.4 us -> 19.8 us
  waiting for transfers between devices: 25.7 us -> 19.6 us
  local copies, waits for them, and re-layouts: 5.99 us -> 1.18 us
  other arithmetic: 2.18 us -> 0.13 us
    all_to_all x0 -> x3, blocking collectives: none -> 28.2 us  [gather(): return lax.all_to_all(msg, everywhere, 0, 0, tiled=False)]
    all_to_all x5 -> x2, starting transfers between devices: 25.5 us -> 9.54 us  [gather(): return lax.all_to_all(msg, everywhere, 0, 0, tiled=False)]
    pallas_call x7 -> x8, Pallas kernels: 31.4 us -> 19.8 us  [call(): pl.pallas_call(kernel, out_shape=[pltpu.HBM(s, d) if i in hbm_outs else j...]
    ppermute x8, starting transfers between devices: 15 us -> 6.72 us  [pair(): return lax.ppermute(x, everywhere, links)]
    unnamed x46 -> x4, local copies, waits for them, and re-layouts: 5.47 us -> 0.67 us
    ppermute x8, waiting for transfers between devices: 14 us -> 10.3 us  [pair(): return lax.ppermute(x, everywhere, links)]
    all_to_all x5 -> x2, waiting for transfers between devices: 10.3 us -> 8.45 us  [gather(): return lax.all_to_all(msg, everywhere, 0, 0, tiled=False)]
  transfers between devices with their start and end apart: 17 -> 14, of which waited for: 10 -> 6; matrix products, arithmetic and copies ran while one was open for 2% -> 0% of each run, Pallas kernels for 9% -> 6%
where the time goes in v2:
time: 87.4 us; the launch traced here: 87 us
  blocking collectives  28.2 us (32%)
  Pallas kernels  19.8 us (23%)
  waiting for transfers between devices  19.6 us (22%)
  starting transfers between devices  17.4 us (20%)
  local copies, waits for them, and re-layouts  1.18 us (1%)
    all_to_all x3, blocking collectives, gather(): return lax.all_to_all(msg, everywhere, 0, 0, tiled=False)  28.2 us
    pallas_call x8, Pallas kernels, call(): pl.pallas_call(kernel, out_shape=[pltpu.HBM(s, d) if i in hbm_outs else j...  19.8 us
    ppermute x8, waiting for transfers between devices, pair(): return lax.ppermute(x, everywhere, links)  10.3 us
    all_to_all x2, starting transfers between devices, gather(): return lax.all_to_all(msg, everywhere, 0, 0, tiled=False)  9.54 us
    all_to_all x2, waiting for transfers between devices, gather(): return lax.all_to_all(msg, everywhere, 0, 0, tiled=False)  8.45 us
    ppermute x8, starting transfers between devices, pair(): return lax.ppermute(x, everywhere, links)  6.72 us
  transfers between devices with their start and end apart: 14, of which 6 were waited for; matrix products, arithmetic and copies ran while one was open for 0% of the time, Pallas kernels for 6%

profile of v2, /device:TPU:0, one launch (start us, length us, event | category | flops | bytes accessed | tf_op | source)
XLA Modules:
  0.0 87.0 jit_solution(2584733758657423187)
XLA Ops:
  1.2 2.3 %shard_map.113 = (f32[32,8,128]{2,1,0:T(8,128)}, f32[40,256]{1,0:T(8,128)S(1)}) custom-call(f32[32,256]{1,0:T(8,128)} %bitcast.20, f32[1,256]{1,0:T(1,128)} %initial.1, f32[1,256]{1,0:T(1,128)} %capacitance.1, f32[2,128,128]{2,1,0:T(8,128)} %bitcast.17, f32[256,512]{1,0:T(8,128)} %bitcast.15, s32[1,128]{1,0:T(1,128)} %tap.1, s32[1,128]{1,0:T(1,128)} %drive.1, ...), custom_call_target="tpu_custom_call" | custom-call | tf_op jit(solution)/shard_map/pallas_call | solution.py:389
  3.5 7.0 %all-to-all-start = ((f32[32,8,128]{2,1,0:T(8,128)}), f32[32,8,128]{2,1,0:T(8,128)S(1)}, u32[]{:S(2)}, u32[]{:S(2)}) async-start(f32[32,8,128]{2,1,0:T(8,128)} %get-tuple-element.38), calls=%async_computation | async-start | bytes 262144 | tf_op jit(solution)/shard_map/all_to_all | solution.py:446
  11.1 0.9 %collective-permute-done.p_other = f32[40,256]{1,0:T(8,128)S(1)} collective-permute-done((f32[40,256]{1,0:T(8,128)S(1)}, f32[40,256]{1,0:T(8,128)S(1)}, u32[]{:S(2)}, u32[]{:S(2)}) %collective-permute-start) | collective-permute-done | bytes 40992 | tf_op jit(solution)/shard_map/ppermute | solution.py:429
  12.7 2.8 %shard_map.114 = (bf16[512,512]{1,0:T(8,128)(2,1)S(1)}, bf16[512,512]{1,0:T(8,128)(2,1)S(1)}, bf16[512,512]{1,0:T(8,128)(2,1)}, bf16[512,512]{1,0:T(8,128)(2,1)}...) custom-call(f32[256,512]{1,0:T(8,128)} %collective-permute-done.1.w_other, ...), custom_call_target="tpu_custom_call" | custom-call | tf_op jit(solution)/shard_map/pallas_call | solution.py:389
  15.4 3.2 %all-to-all-done.got = f32[32,8,128]{2,1,0:T(8,128)S(1)} async-done(((f32[32,8,128]{2,1,0:T(8,128)}), f32[32,8,128]{2,1,0:T(8,128)S(1)}, u32[]{:S(2)}, u32[]{:S(2)}) %all-to-all-start) | async-done | bytes 131104 | tf_op jit(solution)/shard_map/all_to_all | solution.py:446
  18.6 3.4 %shard_map.115 = (f32[32,512]{1,0:T(8,128)S(1)}, f32[32,512]{1,0:T(8,128)S(1)}, f32[32,512]{1,0:T(8,128)S(1)}, f32[32,512]{1,0:T(8,128)S(1)}, f32[32,1,128]{2,1,0:T(1,128)S(1)}, /*index=5*/f32[16,512]{1,0:T(8,128)S(1)}) custom-call(s32[3]{0:T(128)S(1)} %pad_add_fusion.info.refs_0_, f32[32,8,128]{2,1,0:T(8,128)S(1)} %all-to-all-done.got, ...), custom_call_target="tpu_custom_call" | custom-call | tf_op jit(solution)/shard_map/pallas_call | solution.py:389
  22.0 0.9 %collective-permute-start.3 = (f32[32,512]{1,0:T(8,128)S(1)}, f32[32,512]{1,0:T(8,128)S(1)}, u32[]{:S(2)}, u32[]{:S(2)}) collective-permute-start(f32[32,512]{1,0:T(8,128)S(1)} %get-tuple-element.47), channel_id=1, source_target_pairs={{0,8},{1,3},{2,10},{3,1},{4,12},{5,7},{6,14},{7,5},{8,0},{9,11},{1... | collective-permute-start | bytes 196616 | tf_op jit(solution)/shard_map/ppermute | solution.py:437
  22.9 3.5 %collective-permute-done.3 = f32[32,512]{1,0:T(8,128)S(1)} collective-permute-done((f32[32,512]{1,0:T(8,128)S(1)}, f32[32,512]{1,0:T(8,128)S(1)}, u32[]{:S(2)}, u32[]{:S(2)}) %collective-permute-start.3) | collective-permute-done | bytes 65568 | tf_op jit(solution)/shard_map/ppermute | solution.py:437
  26.4 0.9 %collective-permute-start.4 = (f32[32,512]{1,0:T(8,128)S(1)}, f32[32,512]{1,0:T(8,128)S(1)}, u32[]{:S(2)}, u32[]{:S(2)}) collective-permute-start(f32[32,512]{1,0:T(8,128)S(1)} %add.21.refs_2_), channel_id=1, source_target_pairs={{0,8},{1,5},{2,10},{3,7},{4,12},{5,1},{6,14},{7,3},{8,0},{9,13},{1... | collective-permute-start | bytes 196616 | tf_op jit(solution)/shard_map/ppermute | solution.py:437
  27.2 9.3 %all_to_all.25.refs_1_ = f32[32,1,128]{2,1,0:T(1,128)S(1)} all-to-all(f32[32,1,128]{2,1,0:T(1,128)S(1)} %get-tuple-element.46), channel_id=1, replica_groups=mesh['section'=4,'dom'=8] {'section','dom'}, dimensions={0} | all-to-all | bytes 32768 | tf_op jit(solution)/shard_map/all_to_all | solution.py:446
  36.6 3.7 %shard_map.116 = (f32[32,512]{1,0:T(8,128)S(1)}, f32[32,512]{1,0:T(8,128)S(1)}, f32[32,512]{1,0:T(8,128)S(1)}, f32[32,512]{1,0:T(8,128)S(1)}, f32[32,1,128]{2,1,...) custom-call(s32[3]{0:T(128)S(1)} %pad_add_fusion.info.refs_0_, f32[32,1,128]{2,1,0:T(1,128)S(1)} %all_to_all.25.refs_1_, ...), custom_call_target="tpu_custom_call" | custom-call | tf_op jit(solution)/shard_map/pallas_call | solution.py:389
  41.5 3.1 %collective-permute-done.7 = f32[64,256]{1,0:T(8,128)S(1)} collective-permute-done((f32[64,256]{1,0:T(8,128)S(1)}, f32[64,256]{1,0:T(8,128)S(1)}, u32[]{:S(2)}, u32[]{:S(2)}) %collective-permute-start.7) | collective-permute-done | bytes 65568 | tf_op jit(solution)/shard_map/ppermute | solution.py:437
  45.3 2.6 %all-to-all-start.2 = ((f32[32,1,128]{2,1,0:T(1,128)}), f32[32,1,128]{2,1,0:T(1,128)S(1)}, u32[]{:S(2)}, u32[]{:S(2)}) async-start(f32[32,1,128]{2,1,0:T(1,128)} %get-tuple-element.52), calls=%async_computation.2 | async-start | bytes 32768 | tf_op jit(solution)/shard_map/all_to_all | solution.py:446
  47.9 1.8 %collective-permute-start.6 = (f32[32,512]{1,0:T(8,128)S(1)}, f32[32,512]{1,0:T(8,128)S(1)}, u32[]{:S(2)}, u32[]{:S(2)}) collective-permute-start(f32[32,512]{1,0:T(8,128)S(1)} %add.22.refs_2_), channel_id=1, source_target_pairs={{0,8},{1,5},{2,10},{3,7},{4,12},{5,1},{6,14},{7,3},{8,0},{9,13},{1... | collective-permute-start | bytes 196616 | tf_op jit(solution)/shard_map/ppermute | solution.py:437
  49.8 5.3 %all-to-all-done.2.refs_1_ = f32[32,1,128]{2,1,0:T(1,128)S(1)} async-done(((f32[32,1,128]{2,1,0:T(1,128)}), f32[32,1,128]{2,1,0:T(1,128)S(1)}, u32[]{:S(2)}, u32[]{:S(2)}) %all-to-all-start.2) | async-done | bytes 16416 | tf_op jit(solution)/shard_map/all_to_all | solution.py:446
  55.0 3.3 %shard_map.117 = (f32[32,512]{1,0:T(8,128)S(1)}, f32[32,512]{1,0:T(8,128)S(1)}, f32[32,512]{1,0:T(8,128)S(1)}, f32[32,512]{1,0:T(8,128)S(1)}, f32[32,1,128]{2,1,0:T(1,128)S(1)}, /*index=5*/f32[1,128]{1,0:T(1,128)S(1)}) custom-call(s32[3]{0:T(128)S(1)} %pad_add_fusion.info.refs_0_, f32[32,1,128]{2,1,0:T(1,128)S(1)} %all-to-all-done.2.refs_1_, ...), custom_call_target="tpu_custom_call" | custom-call | tf_op jit(solution)/shard_map/pallas_call | solution.py:389
  58.4 0.7 collective-permute-start.9
  59.1 3.7 %collective-permute-done.9 = f32[32,512]{1,0:T(8,128)S(1)} collective-permute-done((f32[32,512]{1,0:T(8,128)S(1)}, f32[32,512]{1,0:T(8,128)S(1)}, u32[]{:S(2)}, u32[]{:S(2)}) %collective-permute-start.9) | collective-permute-done | bytes 65568 | tf_op jit(solution)/shard_map/ppermute | solution.py:437
  62.7 0.7 collective-permute-start.10
  63.4 9.9 %all_to_all.26.got = f32[32,1,128]{2,1,0:T(1,128)S(1)} all-to-all(f32[32,1,128]{2,1,0:T(1,128)S(1)} %get-tuple-element.58), channel_id=1, replica_groups=mesh['section'=4,'dom'=8] {'section','dom'}, dimensions={0} | all-to-all | bytes 32768 | tf_op jit(solution)/shard_map/all_to_all | solution.py:446
  73.4 0.9 shard_map.118
  74.2 2.1 %shard_map.119 = (f32[32,256]{1,0:T(8,128)S(1)}, f32[32,256]{1,0:T(8,128)S(1)}, f32[64,256]{1,0:T(8,128)S(1)}) custom-call(f32[32,512]{1,0:T(8,128)S(1)} %get-tuple-element.64.w_in, f32[32,512]{1,0:T(8,128)S(1)} %get-tuple-element.65.r_in, bf16[6,4,128,128]{3,2,1,0:T(8,128)(2,1)S(1)} %get-tuple-element.40.ah.refs_7_, ...), custom_call_target="tpu_custom_call" | custom-call | tf_op jit(solution)/shard_map/pallas_call | solution.py:389
  76.4 8.9 %all_to_all.27.got = f32[32,1,128]{2,1,0:T(1,128)S(1)} all-to-all(f32[32,1,128]{2,1,0:T(1,128)S(1)} %get-tuple-element.63), channel_id=1, replica_groups=mesh['section'=4,'dom'=8] {'section','dom'}, dimensions={0} | all-to-all | bytes 32768 | tf_op jit(solution)/shard_map/all_to_all | solution.py:446
  85.2 1.3 %shard_map.120 = (f32[32,256]{1,0:T(8,128)}, f32[1,128]{1,0:T(1,128)S(1)}) custom-call(s32[3]{0:T(128)S(1)} %pad_add_fusion.info.refs_0_, f32[32,1,128]{2,1,0:T(1,128)S(1)} %all_to_all.27.got, f32[32,256]{1,0:T(8,128)S(1)} %get-tuple-element.66.w, f32[32,256]{1,0:T(8,128)S(1)} %get-tuple-element.67.c, f32[64,256]{1,0:T(8,128)S(1)} %collective-permute-done.11.given, ...), custom_call_target="tpu_custom_call" | custom-call | tf_op jit(solution)/shard_map/pallas_call | solution.py:389
  (27 shorter events, 4.3 us)
Async XLA Ops:
  0.6 11.4 %collective-permute-start.1 = (f32[256,512]{1,0:T(8,128)}, f32[256,512]{1,0:T(8,128)}, u32[]{:S(2)}, u32[]{:S(2)}) collective-permute-start(f32[256,512]{1,0:T(8,128)} %bitcast.14), channel_id=1, source_target_pairs={{0,1},{1,0},{2,3},{3,2},{4,5},{5,4},{6,7},{7,6},{8,9},{9,8},{10,11... | collective-permute-start | bytes 1572872 | tf_op jit(solution)/shard_map/ppermute | solution.py:429
  3.5 7.0 %copy-start = (f32[1,2,128,128]{3,2,1,0:T(8,128)S(1)}, f32[1,2,128,128]{3,2,1,0:T(8,128)}, u32[]{:S(2)}) copy-start(f32[1,2,128,128]{3,2,1,0:T(8,128)} %param.14) | copy-start | bytes 393220
  3.5 15.1 %all-to-all-start = ((f32[32,8,128]{2,1,0:T(8,128)}), f32[32,8,128]{2,1,0:T(8,128)S(1)}, u32[]{:S(2)}, u32[]{:S(2)}) async-start(f32[32,8,128]{2,1,0:T(8,128)} %get-tuple-element.38), calls=%async_computation | async-start | bytes 262144 | tf_op jit(solution)/shard_map/all_to_all | solution.py:446
  10.4 1.5 %collective-permute-start.2 = (f32[2,128,128]{2,1,0:T(8,128)S(1)}, f32[2,128,128]{2,1,0:T(8,128)S(1)}, u32[]{:S(2)}, u32[]{:S(2)}) collective-permute-start(f32[2,128,128]{2,1,0:T(8,128)S(1)} %bitcast.19), channel_id=1, source_target_pairs={{0,1},{1,0},{2,3},{3,2},{4,5},{5,4},{6,7},{7,6},{8,9},{9,8},{10,11... | collective-permute-start | bytes 393224 | tf_op jit(solution)/shard_map/ppermute | solution.py:429
  10.8 1.2 %collective-permute-start = (f32[40,256]{1,0:T(8,128)S(1)}, f32[40,256]{1,0:T(8,128)S(1)}, u32[]{:S(2)}, u32[]{:S(2)}) collective-permute-start(f32[40,256]{1,0:T(8,128)S(1)} %get-tuple-element.39.p_own), channel_id=1, source_target_pairs={{0,1},{1,0},{2,3},{3,2},{4,5},{5,4},{6,7},{7,6},{8,9},{9,8},{10,11... | collective-permute-start | bytes 122888 | tf_op jit(solution)/shard_map/ppermute | solution.py:429
  12.0 0.7 copy-start.1
  22.0 4.3 %collective-permute-start.3 = (f32[32,512]{1,0:T(8,128)S(1)}, f32[32,512]{1,0:T(8,128)S(1)}, u32[]{:S(2)}, u32[]{:S(2)}) collective-permute-start(f32[32,512]{1,0:T(8,128)S(1)} %get-tuple-element.47), channel_id=1, source_target_pairs={{0,8},{1,3},{2,10},{3,1},{4,12},{5,7},{6,14},{7,5},{8,0},{9,11},{1... | collective-permute-start | bytes 196616 | tf_op jit(solution)/shard_map/ppermute | solution.py:437
  26.4 10.2 %collective-permute-start.4 = (f32[32,512]{1,0:T(8,128)S(1)}, f32[32,512]{1,0:T(8,128)S(1)}, u32[]{:S(2)}, u32[]{:S(2)}) collective-permute-start(f32[32,512]{1,0:T(8,128)S(1)} %add.21.refs_2_), channel_id=1, source_target_pairs={{0,8},{1,5},{2,10},{3,7},{4,12},{5,1},{6,14},{7,3},{8,0},{9,13},{1... | collective-permute-start | bytes 196616 | tf_op jit(solution)/shard_map/ppermute | solution.py:437
  40.3 4.3 %collective-permute-start.7 = (f32[64,256]{1,0:T(8,128)S(1)}, f32[64,256]{1,0:T(8,128)S(1)}, u32[]{:S(2)}, u32[]{:S(2)}) collective-permute-start(f32[64,256]{1,0:T(8,128)S(1)} %get-tuple-element.57), channel_id=1, source_target_pairs={{0,2},{1,9},{2,0},{3,11},{4,6},{5,13},{6,4},{7,15},{8,10},{9,1},{1... | collective-permute-start | bytes 196616 | tf_op jit(solution)/shard_map/ppermute | solution.py:437
  40.9 6.9 %collective-permute-start.5 = (f32[32,512]{1,0:T(8,128)S(1)}, f32[32,512]{1,0:T(8,128)S(1)}, u32[]{:S(2)}, u32[]{:S(2)}) collective-permute-start(f32[32,512]{1,0:T(8,128)S(1)} %get-tuple-element.53), channel_id=1, source_target_pairs={{0,8},{1,3},{2,10},{3,1},{4,12},{5,7},{6,14},{7,5},{8,0},{9,11},{1... | collective-permute-start | bytes 196616 | tf_op jit(solution)/shard_map/ppermute | solution.py:437
  44.7 5.1 %collective-permute-start.8 = (f32[64,256]{1,0:T(8,128)S(1)}, f32[64,256]{1,0:T(8,128)S(1)}, u32[]{:S(2)}, u32[]{:S(2)}) collective-permute-start(f32[64,256]{1,0:T(8,128)S(1)} %multiply_add_fusion.1), channel_id=1, source_target_pairs={{0,2},{1,17},{2,0},{3,19},{4,6},{5,21},{6,4},{7,23},{8,10},{9,25},... | collective-permute-start | bytes 196616 | tf_op jit(solution)/shard_map/ppermute | solution.py:437
  45.3 9.8 %all-to-all-start.2 = ((f32[32,1,128]{2,1,0:T(1,128)}), f32[32,1,128]{2,1,0:T(1,128)S(1)}, u32[]{:S(2)}, u32[]{:S(2)}) async-start(f32[32,1,128]{2,1,0:T(1,128)} %get-tuple-element.52), calls=%async_computation.2 | async-start | bytes 32768 | tf_op jit(solution)/shard_map/all_to_all | solution.py:446
  47.9 7.1 %collective-permute-start.6 = (f32[32,512]{1,0:T(8,128)S(1)}, f32[32,512]{1,0:T(8,128)S(1)}, u32[]{:S(2)}, u32[]{:S(2)}) collective-permute-start(f32[32,512]{1,0:T(8,128)S(1)} %add.22.refs_2_), channel_id=1, source_target_pairs={{0,8},{1,5},{2,10},{3,7},{4,12},{5,1},{6,14},{7,3},{8,0},{9,13},{1... | collective-permute-start | bytes 196616 | tf_op jit(solution)/shard_map/ppermute | solution.py:437
  58.4 4.3 %collective-permute-start.9 = (f32[32,512]{1,0:T(8,128)S(1)}, f32[32,512]{1,0:T(8,128)S(1)}, u32[]{:S(2)}, u32[]{:S(2)}) collective-permute-start(f32[32,512]{1,0:T(8,128)S(1)} %get-tuple-element.59), channel_id=1, source_target_pairs={{0,8},{1,3},{2,10},{3,1},{4,12},{5,7},{6,14},{7,5},{8,0},{9,11},{1... | collective-permute-start | bytes 196616 | tf_op jit(solution)/shard_map/ppermute | solution.py:437
  62.7 10.6 %collective-permute-start.10 = (f32[32,512]{1,0:T(8,128)S(1)}, f32[32,512]{1,0:T(8,128)S(1)}, u32[]{:S(2)}, u32[]{:S(2)}) collective-permute-start(f32[32,512]{1,0:T(8,128)S(1)} %add.25.own), channel_id=1, source_target_pairs={{0,8},{1,5},{2,10},{3,7},{4,12},{5,1},{6,14},{7,3},{8,0},{9,13},{1... | collective-permute-start | bytes 196616 | tf_op jit(solution)/shard_map/ppermute | solution.py:437
  76.4 8.9 %collective-permute-start.11 = (f32[64,256]{1,0:T(8,128)S(1)}, f32[64,256]{1,0:T(8,128)S(1)}, u32[]{:S(2)}, u32[]{:S(2)}) collective-permute-start(f32[64,256]{1,0:T(8,128)S(1)} %get-tuple-element.68), channel_id=1, source_target_pairs={{0,1},{1,0},{2,3},{3,2},{4,5},{5,4},{6,7},{7,6},{8,9},{9,8},{10,11... | collective-permute-start | bytes 196616 | tf_op jit(solution)/shard_map/ppermute | solution.py:429

commit v3 on v2

--- a/solution.py
+++ b/solution.py
@@ -19,10 +19,6 @@
 
 def fdot(a, b):
     return jnp.dot(a, b, precision=HIGHEST, preferred_element_type=F32)
-
-
-def dot6(a, b):
-    return fdot(a, b)
 
 
 def bdot(a, b):
@@ -77,30 +73,30 @@
     return [p for stage in plan[1:] for p in stage]
 
 
+def tree(parts):
+    while len(parts) > 1:
+        parts = [parts[i] + parts[i + 1] if i + 1 < len(parts) else parts[i] for i in range(0, len(parts), 2)]
+    return parts[0]
+
+
 def tile_sum(x):
-    total = None
-    for i in range(0, x.shape[0], SUB):
-        for j in range(0, x.shape[1], LANES):
-            part = x[i : i + SUB, j : j + LANES]
-            total = part if total is None else total + part
-    return total
-
-
-def first_kernel(source, initial, capacitance, matrix, weight, tap, drive, gain, att, msg, pack,
-                 b_initial, b_capacitance, b_matrix, b_weight, b_tap, b_drive, b_gain, b_att, sems):
-    steps, nodes = source.shape
-    blocks, width = matrix.shape[0], matrix.shape[1]
-    channels = tap.shape[1]
-    moves = [(initial, b_initial), (weight, b_weight), (att, b_att), (tap, b_tap), (matrix, b_matrix),
-             (capacitance, b_capacitance), (drive, b_drive), (gain, b_gain), (source, pack.at[0:steps, :])]
+    return tree([x[i : i + SUB, j : j + LANES] for i in range(0, x.shape[0], SUB) for j in range(0, x.shape[1], LANES)])
+
+
+def land(moves, sems):
     copies = [pltpu.make_async_copy(src, dst, sems.at[i]) for i, (src, dst) in enumerate(moves)]
     for copy in copies:
         copy.start()
-    pack[steps : steps + SUB, :] = jnp.zeros((SUB, nodes), F32)
-    for copy in copies:
+    return copies
+
+
+def first_kernel(initial, weight, tap, att, msg, b_initial, b_weight, b_tap, b_att, sems):
+    nodes = initial.shape[1]
+    channels = tap.shape[1]
+    for copy in land([(weight, b_weight), (initial, b_initial), (tap, b_tap), (att, b_att)], sems):
         copy.wait()
     start = b_initial[...]
-    net = dot6(start, b_weight[...])
+    net = fdot(start, b_weight[...])
     rows = []
     for j in range(0, net.shape[1], LANES):
         rows.append(net[:, j : j + LANES])
@@ -113,6 +109,22 @@
     rows += [jnp.zeros((1, LANES), F32)] * (SUB - len(rows))
     tile = jnp.concatenate(rows, axis=0)
     msg[...] = jnp.broadcast_to(tile[None], msg.shape)
+
+
+def pack_kernel(source, initial, capacitance, matrix, tap, drive, gain, pack,
+                b_initial, b_capacitance, b_matrix, b_tap, b_drive, b_gain, sems):
+    steps, nodes = source.shape
+    blocks, width = matrix.shape[0], matrix.shape[1]
+    channels = tap.shape[1]
+    copies = land(
+        [(initial, b_initial), (matrix, b_matrix), (capacitance, b_capacitance), (tap, b_tap), (drive, b_drive),
+         (gain, b_gain), (source, pack.at[0:steps, :])],
+        sems,
+    )
+    pack[steps : steps + SUB, :] = jnp.zeros((SUB, nodes), F32)
+    for copy in copies:
+        copy.wait()
+    start = b_initial[...]
     parts = []
     for k in range(blocks):
         parts.append(
@@ -135,27 +147,23 @@
     return jnp.concatenate([ref_other[lo:hi, :], ref_own[lo:hi, :]], axis=1)
 
 
-def prep_kernel(plan, steps, w_other, w_own, i_other, i_own, p_other, p_own, th, tl, wh, wl, ah, al,
+def prep_kernel(plan, steps, i_other, w_other, w_own, i_own, p_other, p_own, th, tl, ah, al, wh, wl,
                 b_w, b_i, s_wh, s_wl, sems):
     nodes = w_own.shape[0]
     blocks, width = i_own.shape[0], i_own.shape[1]
-    moves = [(i_other, b_i.at[0]), (i_own, b_i.at[1]), (w_other, b_w.at[0]), (w_own, b_w.at[1])]
-    copies = [pltpu.make_async_copy(src, dst, sems.at[i]) for i, (src, dst) in enumerate(moves)]
-    for copy in copies:
-        copy.start()
+    copies = land([(i_own, b_i), (w_other, b_w.at[0]), (w_own, b_w.at[1])], sems)
     cap = both(p_other, p_own, steps + 2, steps + 3)
-    for copy in copies[2:]:
+    for copy in copies[1:]:
         copy.wait()
     for half in range(2):
         here = slice(half * nodes, (half + 1) * nodes)
         h, l = split(b_w[half])
         s_wh[here, :] = h
         s_wl[here, :] = l
-    backs = [pltpu.make_async_copy(s_wh, wh, sems.at[4]), pltpu.make_async_copy(s_wl, wl, sems.at[5])]
+    backs = [pltpu.make_async_copy(s_wh, wh, sems.at[3]), pltpu.make_async_copy(s_wl, wl, sems.at[4])]
     for copy in backs:
         copy.start()
-    for copy in copies[:2]:
-        copy.wait()
+    copies[0].wait()
     wanted = powers_of(plan)
     eye = lax.broadcasted_iota(jnp.int32, (width, width), 0) == lax.broadcasted_iota(jnp.int32, (width, width), 1)
 
@@ -163,7 +171,7 @@
         return bdot(x[0], y[0]) + bdot(x[1], y[0]) + bdot(x[0], y[1])
 
     every = range(2 * blocks)
-    inverse = [split(b_i[b // blocks, b % blocks].T) for b in every]
+    inverse = [split((i_other if b < blocks else b_i)[b % blocks].T) for b in every]
     scale = [split(jnp.where(eye, cap[:, b * width : (b + 1) * width], 0.0)) for b in every]
     made = {1: [split(times(scale[b], inverse[b])) for b in every]}
     todo = [inverse, [split(times(inverse[b], made[1][b])) for b in every]]
@@ -188,84 +196,94 @@
         copy.wait()
 
 
-def march(plan, r, ah, al):
+def march(plan, x, ah, al):
     blocks, width = ah.shape[1], ah.shape[2]
-    out = []
-    for b in range(blocks):
-        x = r[:, b * width : (b + 1) * width]
-        unit = 0
-        for s, stage in enumerate(plan):
-            total = None
-            for offset in stage:
-                part = dot3(lag(x, offset), ah[unit, b], al[unit, b])
-                total = part if total is None else total + part
-                unit += 1
-            x = total if s == 0 else total + x
-        out.append(x)
-    return jnp.concatenate(out, axis=1)
-
-
-def fetch(wh, wl, b_wh, b_wl, sems):
-    copies = [pltpu.make_async_copy(wh, b_wh, sems.at[0]), pltpu.make_async_copy(wl, b_wl, sems.at[1])]
-    for copy in copies:
-        copy.start()
-    return copies
-
-
-def send_squares(r, north, msg):
-    row = jnp.sum(tile_sum(r * r), axis=0, keepdims=True) * north
-    msg[...] = jnp.broadcast_to(row[None], msg.shape)
-
-
-def finish_round(plan, r, c_ref, p_ref, msg, ah, al, copies, b_wh, b_wl, north):
-    send_squares(r, north, msg)
+    rows = x.shape[0]
+    unit = 0
+    for s, stage in enumerate(plan):
+        sums = [None] * blocks
+        for offset in stage:
+            xh, xl = split(lag(x, offset))
+            pair = jnp.concatenate([xh, xl], axis=0)
+            for b in range(blocks):
+                here = slice(b * width, (b + 1) * width)
+                two = bdot(pair[:, here], ah[unit, b])
+                part = two[:rows] + two[rows:] + bdot(xh[:, here], al[unit, b])
+                sums[b] = part if sums[b] is None else sums[b] + part
+            unit += 1
+        total = jnp.concatenate(sums, axis=1)
+        x = total if s == 0 else total + x
+    return x
+
+
+def send_squares(r, spot, msg):
+    row = jnp.sum(tile_sum(r * r), axis=0, keepdims=True) * spot[2:3, :]
+    msg[...] = jnp.broadcast_to(row, msg.shape)
+
+
+def finish_round(plan, r, spot, c_ref, p_ref, msg, ah, al, sent, copies, wh, wl):
+    near_msg, sem = sent
+    send_squares(r, spot, near_msg)
+    leaving = pltpu.make_async_copy(near_msg, msg, sem.at[0])
+    leaving.start()
     c = march(plan, r, ah, al)
     c_ref[...] = c
     for copy in copies:
         copy.wait()
-    p_ref[...] = dot3(c, b_wh[...], b_wl[...])
+    p_ref[...] = dot3(c, wh[...], wl[...])
+    leaving.wait()
     return c
 
 
-def opening_kernel(plan, steps, channels, sections, doms, levels, info, got, p_other, p_own, ah, al, th, tl, wh, wl,
-                   w_ref, q_ref, c_ref, p_ref, msg, aux_ref, b_wh, b_wl, sems):
-    copies = fetch(wh, wl, b_wh, b_wl, sems)
-    my, chip = info[0], info[1]
-    north = info[2].astype(F32)
+def opening_kernel(plan, steps, channels, sections, doms, levels, spot, got, p_other, p_own, ah, al, th, tl, wh, wl,
+                   w_ref, q_ref, r_ref, c_ref, p_ref, msg, aux_ref, near_h, near_l, sems, *sent):
+    copies = land([(wh, near_h), (wl, near_l)], sems)
+    my, chip = spot[0:1, :], spot[1:2, :]
     nets = th.shape[0]
     net_rows = nets // LANES
     tap_rows = channels // LANES
     mine = jnp.zeros((SUB, LANES), F32)
-    base = my * doms
-    for d in range(doms):
-        mine = mine + got[base + d]
+    for t in range(sections):
+        whole = tree([got[t * doms + d] for d in range(doms)])
+        mine = jnp.where(my == float(t), whole, mine)
     net = jnp.concatenate([mine[i : i + 1, :] for i in range(net_rows)], axis=1)
+
+    tiles = []
+    for t in range(sections):
+        halves = []
+        for half in range(2):
+            tile = got[t * doms + half]
+            for z in range(1, doms // 2):
+                tile = jnp.where(chip == float(z), got[t * doms + 2 * z + half], tile)
+            halves.append(tile)
+        tiles.append(halves)
 
     def channel_row(s, first):
         pieces = []
         for half in range(2):
-            tile = got[s * doms + 2 * chip + half]
-            pieces += [tile[first + i : first + i + 1, :] for i in range(tap_rows)]
+            pieces += [tiles[s][half][first + i : first + i + 1, :] for i in range(tap_rows)]
         return jnp.concatenate(pieces, axis=1)
 
+    lanes = 2 * channels // LANES
+    here = jnp.concatenate([my] * lanes, axis=1).astype(jnp.int32)
     decay, carried, drive = [], None, jnp.zeros((1, 2 * channels), F32)
     for s in range(sections):
         a = channel_row(s, net_rows + tap_rows)
         decay.append(a)
         if carried is not None:
-            drive = jnp.where(my == s, carried, drive)
+            drive = jnp.where(here == s, carried, drive)
         tapped = channel_row(s, net_rows)
         carried = tapped if carried is None else a * carried + tapped
     one = jnp.ones((1, 2 * channels), F32)
     rows = []
     for level in range(levels):
-        bit = (my >> level) & 1
+        bit = (here >> level) & 1
         own_a, other_a, past_a = one, one, one
         for s in range(sections):
-            here = s >> level
-            own_a = jnp.where(here == (my >> level), own_a * decay[s], own_a)
-            other_a = jnp.where(here == ((my >> level) ^ 1), other_a * decay[s], other_a)
-            past_a = jnp.where((here == (my >> level)) & (s < my), past_a * decay[s], past_a)
+            up = s >> level
+            own_a = jnp.where((here >> level) == up, own_a * decay[s], own_a)
+            other_a = jnp.where(((here >> level) ^ 1) == up, other_a * decay[s], other_a)
+            past_a = jnp.where(((here >> level) == up) & (here > s), past_a * decay[s], past_a)
         rows += [jnp.where(bit == 1, one, other_a), jnp.where(bit == 1, own_a, one), jnp.where(bit == 1, past_a, 0.0)]
     nodes = p_own.shape[1]
     kept = [
@@ -284,7 +302,8 @@
     r = q + 0.5 * jnp.tanh(start)
     w_ref[...] = jnp.broadcast_to(start, w_ref.shape)
     q_ref[...] = q
-    finish_round(plan, r, c_ref, p_ref, msg, ah, al, copies, b_wh, b_wl, north)
+    r_ref[...] = r
+    finish_round(plan, r, spot, c_ref, p_ref, msg, ah, al, sent, copies, near_h, near_l)
 
 
 def chosen(index, nodes):
@@ -305,35 +324,33 @@
 
 
 def damping_of(got, cells):
-    total = got[0]
-    for i in range(1, got.shape[0]):
-        total = total + got[i]
+    total = tile_sum(got[...])
     mean = jnp.sum(jnp.sum(total, axis=0, keepdims=True), axis=1, keepdims=True) / cells
     return mean, 1.0 / (1.0 + jnp.sqrt(mean))
 
 
-def advance(got, own, recv, w0, q0, c0, th, tl, cells, mean_ref):
+def back_kernel(own, recv, r0, th, tl, u_ref):
+    u_ref[...] = r0[...] + dot3(own[...] + recv[...], th[...], tl[...])
+
+
+def advance(got, u, w0, q0, c0, cells, mean_ref):
     mean, damp = damping_of(got, cells)
     mean_ref[...] = jnp.broadcast_to(mean, mean_ref.shape)
-    back = dot3(own[...] + recv[...], th[...], tl[...])
-    w = w0[...] - damp * c0[...]
-    q = q0[...] - damp * (q0[...] + 0.5 * jnp.tanh(w0[...]) + back)
-    return w, q, damp
+    return w0[...] - damp * c0[...], q0[...] - damp * u[...], damp
 
 
 def round_kernel(plan, steps, channels, cells, mode, *refs):
     refs = list(refs)
     take = lambda n: [refs.pop(0) for _ in range(n)]
-    (info, got, own, recv, w0, q0, c0, ah, al, th, tl, wh, wl, aux) = take(14)
+    (spot, got, u, w0, q0, c0, ah, al, wh, wl, aux) = take(11)
     if mode == "drive":
         (pre,) = take(1)
-    w_ref, q_ref, c_ref, p_ref, msg, mean_ref = take(6)
+    w_ref, q_ref, r_ref, c_ref, p_ref, msg, mean_ref = take(7)
     if mode == "taps":
         (tt_ref,) = take(1)
-    b_wh, b_wl, sems = take(3)
-    copies = fetch(wh, wl, b_wh, b_wl, sems)
-    north = info[2].astype(F32)
-    w, q, damp = advance(got, own, recv, w0, q0, c0, th, tl, cells, mean_ref)
+    near_h, near_l, sems, *sent = take(5)
+    copies = land([(wh, near_h), (wl, near_l)], sems)
+    w, q, damp = advance(got, u, w0, q0, c0, cells, mean_ref)
     if mode == "drive":
         drive = pre[0:steps, :] - damp * pre[steps : 2 * steps, :]
         gain, _, driven = (aux[i : i + 1, 0 : 2 * channels] for i in (1, 2, 3))
@@ -341,7 +358,8 @@
     r = q + 0.5 * jnp.tanh(w)
     w_ref[...] = w
     q_ref[...] = q
-    c = finish_round(plan, r, c_ref, p_ref, msg, ah, al, copies, b_wh, b_wl, north)
+    r_ref[...] = r
+    c = finish_round(plan, r, spot, c_ref, p_ref, msg, ah, al, sent, copies, near_h, near_l)
     if mode == "taps":
         half = w.shape[1] // 2
         for h in range(2):
@@ -351,12 +369,12 @@
             tt_ref[:, there] = dot2(jnp.concatenate([w[:, here], c[:, here]], axis=0), tapped)
 
 
-def residual_kernel(cells, info, got, own, recv, w0, q0, c0, th, tl, w_ref, r_ref, msg, mean_ref):
-    w, q, _ = advance(got, own, recv, w0, q0, c0, th, tl, cells, mean_ref)
+def residual_kernel(cells, spot, got, u, w0, q0, c0, w_ref, r_ref, msg, mean_ref):
+    w, q, _ = advance(got, u, w0, q0, c0, cells, mean_ref)
     r = q + 0.5 * jnp.tanh(w)
     w_ref[...] = w
     r_ref[...] = r
-    send_squares(r, info[2].astype(F32), msg)
+    send_squares(r, spot, msg)
 
 
 def correct_kernel(plan, w_in, r_in, ah, al, w_ref, c_ref, give):
@@ -370,26 +388,26 @@
     give[steps : 2 * steps, :] = c[:, 0:half]
 
 
-def last_kernel(steps, cells, info, got, w, c, given, m1, m2, m3, out, means):
+def last_kernel(steps, cells, spot, got, w, c, given, m1, m2, m3, out, means):
     mean, damp = damping_of(got, cells)
-    north = info[2] == 1
+    north = jnp.concatenate([spot[2:3, :]] * (out.shape[1] // LANES), axis=1) == 1.0
     w_here = jnp.where(north, w[...], given[0:steps, :])
     c_here = jnp.where(north, c[...], given[steps : 2 * steps, :])
     out[...] = w_here - damp * c_here
     lane = lax.broadcasted_iota(jnp.int32, (1, LANES), 1)
     row = jnp.where(lane == 0, m1[...], jnp.where(lane == 1, m2[...], jnp.where(lane == 2, m3[...], mean)))
-    means[...] = row
-
-
-def call(kernel, outs, *args, smem=(), hbm=(), hbm_outs=(), scratch=()):
-    def place(i, far, scalar=()):
-        return pl.BlockSpec(memory_space=pltpu.SMEM if i in scalar else pltpu.HBM if i in far else pltpu.VMEM)
+    means[...] = row[0, 0 : means.shape[0]]
+
+
+def call(kernel, outs, *args, hbm=(), hbm_outs=(), scratch=()):
+    def place(i, far):
+        return pl.BlockSpec(memory_space=pltpu.HBM if i in far else pltpu.VMEM)
 
     args = [pltpu.with_memory_space_constraint(x, pltpu.HBM) if i in hbm else x for i, x in enumerate(args)]
     return pl.pallas_call(
         kernel,
         out_shape=[pltpu.HBM(s, d) if i in hbm_outs else jax.ShapeDtypeStruct(s, d) for i, (s, d) in enumerate(outs)],
-        in_specs=[place(i, hbm, smem) for i in range(len(args))],
+        in_specs=[place(i, hbm) for i in range(len(args))],
         out_specs=[place(i, hbm_outs) for i in range(len(outs))],
         scratch_shapes=scratch,
         compiler_params=pltpu.CompilerParams(vmem_limit_bytes=16 << 20),
@@ -443,50 +461,62 @@
         return pair(x, lambda s, d: (s ^ (1 << bit), d), lambda s, d: (s, d ^ 2))
 
     def gather(msg):
-        return lax.all_to_all(msg, everywhere, 0, 0, tiled=False)
-
-    place = lax.axis_index("dom")
-    info = jnp.stack([lax.axis_index("section"), place // 2, place % 2]).astype(jnp.int32)
-
+        spread_out = msg.reshape((devices, -1, LANES))
+        return lax.all_to_all(spread_out, everywhere, 0, 0, tiled=False).reshape(msg.shape)
+
+    core = lax.axis_index("dom")
+    spot = jnp.stack([lax.axis_index("section"), core // 2, core % 2] + [core] * 5).astype(F32)
+    spot = jnp.broadcast_to(spot[:, None], (SUB, LANES))
     w_other = swap(net_weight)
     i_other = swap(block_inverse)
     first_message = ((devices, SUB, LANES), F32)
-    message = ((devices, 1, LANES), F32)
+    message = ((devices, LANES), F32)
     row = lambda n, d=F32: pltpu.VMEM((1, n), d)
-    msg, pack = call(
+    (msg,) = call(
         first_kernel,
-        [first_message, ((steps + SUB, nodes), F32)],
-        source, initial, capacitance, block_matrix, net_weight, tap_nodes, drive_nodes, drive_gain, attenuation,
-        hbm=range(9),
+        [first_message],
+        initial, net_weight, tap_nodes, attenuation,
+        hbm=range(4),
         scratch=[
-            row(nodes), row(nodes), pltpu.VMEM(block_matrix.shape, F32), pltpu.VMEM(net_weight.shape, F32),
-            row(channels, jnp.int32), row(channels, jnp.int32), row(channels), row(channels),
-            pltpu.SemaphoreType.DMA((9,)),
+            row(nodes), pltpu.VMEM(net_weight.shape, F32), row(channels, jnp.int32), row(channels),
+            pltpu.SemaphoreType.DMA((4,)),
         ],
     )
     got = gather(msg)
+    (pack,) = call(
+        pack_kernel,
+        [((steps + SUB, nodes), F32)],
+        source, initial, capacitance, block_matrix, tap_nodes, drive_nodes, drive_gain,
+        hbm=range(7),
+        scratch=[
+            row(nodes), row(nodes), pltpu.VMEM(block_matrix.shape, F32),
+            row(channels, jnp.int32), row(channels, jnp.int32), row(channels), pltpu.SemaphoreType.DMA((7,)),
+        ],
+    )
     p_other = swap(pack)
     cut = ((units, 2 * blocks, width, width), BF16)
-    th, tl, wh, wl, ah, al = call(
+    up, down = ((nets, wide), BF16), ((wide, nets), BF16)
+    th, tl, ah, al, wh, wl = call(
         functools.partial(prep_kernel, plan, steps),
-        [((nets, wide), BF16), ((nets, wide), BF16), ((wide, nets), BF16), ((wide, nets), BF16), cut, cut],
-        w_other, net_weight, i_other, block_inverse, p_other, pack,
-        hbm=range(4),
-        hbm_outs=(2, 3),
+        [up, up, cut, cut, down, down],
+        i_other, w_other, net_weight, block_inverse, p_other, pack,
+        hbm=range(1, 4),
+        hbm_outs=(4, 5),
         scratch=[
-            pltpu.VMEM((2, nodes, nets), F32), pltpu.VMEM((2, blocks, width, width), F32),
-            pltpu.VMEM((wide, nets), BF16), pltpu.VMEM((wide, nets), BF16), pltpu.SemaphoreType.DMA((6,)),
+            pltpu.VMEM((2, nodes, nets), F32), pltpu.VMEM((blocks, width, width), F32),
+            pltpu.VMEM(*down), pltpu.VMEM(*down), pltpu.SemaphoreType.DMA((5,)),
         ],
     )
-    state = [((steps, wide), F32)] * 3
+    state = [((steps, wide), F32)] * 4
+    landing = [pltpu.VMEM(*down), pltpu.VMEM(*down), pltpu.SemaphoreType.DMA((2,))]
+    landing = landing + [pltpu.VMEM(*message), pltpu.SemaphoreType.DMA((1,))]
     aux_shape = (-(-(4 + 3 * levels) // SUB) * SUB, max(wide, 2 * channels))
-    landing = [pltpu.VMEM((wide, nets), BF16), pltpu.VMEM((wide, nets), BF16), pltpu.SemaphoreType.DMA((2,))]
-    w, q, c, part, msg, aux = call(
+    w, q, r, c, part, msg, aux = call(
         functools.partial(opening_kernel, plan, steps, channels, sections, doms, levels),
         state + [((steps, nets), F32), message, (aux_shape, F32)],
-        info, got, p_other, pack, ah, al, th, tl, wh, wl,
-        smem=(0,),
+        spot, got, p_other, pack, ah, al, th, tl, wh, wl,
         hbm=(8, 9),
+        hbm_outs=(5,),
         scratch=landing,
     )
     means = []
@@ -499,7 +529,9 @@
         for bit in range(1, bits):
             own = own + recv
             recv = along_dom(own, bit)
-        if index == NEWTON * SWEEPS - 1:
+        last = index == NEWTON * SWEEPS - 1
+        (u,) = call(back_kernel, [((steps, wide), F32)], own, recv, r, th, tl)
+        if last:
             break
         boundary = index % NEWTON == 0
         before = index % NEWTON == NEWTON - 1
@@ -521,20 +553,19 @@
         result = call(
             functools.partial(round_kernel, plan, steps, channels, cells, mode),
             outs,
-            info, got, own, recv, w, q, c, ah, al, th, tl, wh, wl, aux, *extra,
-            smem=(0,),
-            hbm=(11, 12),
+            spot, got, u, w, q, c, ah, al, wh, wl, aux, *extra,
+            hbm=(8, 9),
+            hbm_outs=(5,),
             scratch=landing,
         )
-        w, q, c, part, msg, mean = result[:6]
+        w, q, r, c, part, msg, mean = result[:7]
         means.append(mean)
         if mode == "taps":
-            taps = result[6]
+            taps = result[7]
     w, r, msg, mean = call(
         functools.partial(residual_kernel, cells),
         [((steps, wide), F32), ((steps, wide), F32), message, ((1, LANES), F32)],
-        info, got, own, recv, w, q, c, th, tl,
-        smem=(0,),
+        spot, got, u, w, q, c,
     )
     means.append(mean)
     got = gather(msg)
@@ -546,11 +577,10 @@
     given = swap(give)
     out, history = call(
         functools.partial(last_kernel, steps, cells),
-        [((steps, nodes), F32), ((1, LANES), F32)],
-        info, got, w, c, given, *means,
-        smem=(0,),
-    )
-    return (out[None], history[0, : NEWTON * SWEEPS])
+        [((steps, nodes), F32), ((NEWTON * SWEEPS,), F32)],
+        spot, got, w, c, given, *means,
+    )
+    return (out[None], history)
 
 
 def solution(mesh):

time: 87.4 us -> 80.7 us (0.923)
  blocking collectives: 28.2 us -> 8.87 us
  waiting for transfers between devices: 19.6 us -> 31.5 us
  starting transfers between devices: 17.4 us -> 24.5 us
  Pallas kernels: 19.8 us -> 13.6 us
    all_to_all x3 -> x1, blocking collectives: 28.2 us -> 8.87 us  [gather(): lax.all_to_all(spread_out, everywhere, 0, 0, tiled=False).reshape(msg.shape)]
    all_to_all x2 -> x4, waiting for transfers between devices: 8.45 us -> 17.5 us  [gather(): lax.all_to_all(spread_out, everywhere, 0, 0, tiled=False).reshape(msg.shape)]
    all_to_all x2 -> x4, starting transfers between devices: 9.54 us -> 16.6 us  [gather(): lax.all_to_all(spread_out, everywhere, 0, 0, tiled=False).reshape(msg.shape)]
    pallas_call x8 -> x12, Pallas kernels: 19.8 us -> 13.6 us  [call(): pl.pallas_call(kernel, out_shape=[pltpu.HBM(s, d) if i in hbm_outs else j...]
    ppermute x8, waiting for transfers between devices: 10.3 us -> 13.2 us  [pair(): return lax.ppermute(x, everywhere, links)]
  transfers between devices with their start and end apart: 14 -> 16, of which waited for: 6 -> 10; matrix products, arithmetic and copies ran while one was open for 0% -> 0% of each run, Pallas kernels for 6% -> 9%
where the time goes in v3:
time: 80.7 us; the launch traced here: 80.3 us
  waiting for transfers between devices  31.5 us (39%)
  starting transfers between devices  24.5 us (30%)
  Pallas kernels  13.6 us (17%)
  blocking collectives  8.87 us (11%)
  local copies, waits for them, and re-layouts  0.97 us (1%)
    all_to_all x4, waiting for transfers between devices, gather(): lax.all_to_all(spread_out, everywhere, 0, 0, tiled=False).reshape(msg.shape)  17.5 us
    all_to_all x4, starting transfers between devices, gather(): lax.all_to_all(spread_out, everywhere, 0, 0, tiled=False).reshape(msg.shape)  16.6 us
    pallas_call x12, Pallas kernels, call(): pl.pallas_call(kernel, out_shape=[pltpu.HBM(s, d) if i in hbm_outs else j...  13.6 us
    ppermute x8, waiting for transfers between devices, pair(): return lax.ppermute(x, everywhere, links)  13.2 us
    all_to_all x1, blocking collectives, gather(): lax.all_to_all(spread_out, everywhere, 0, 0, tiled=False).reshape(msg.shape)  8.87 us
    ppermute x8, starting transfers between devices, pair(): return lax.ppermute(x, everywhere, links)  6.71 us
  transfers between devices with their start and end apart: 16, of which 10 were waited for; matrix products, arithmetic and copies ran while one was open for 0% of the time, Pallas kernels for 9%

profile of v3, /device:TPU:0, one launch (start us, length us, event | category | flops | bytes accessed | tf_op | source)
XLA Modules:
  0.0 80.3 jit_solution(17558990581530700873)
XLA Ops:
  1.2 2.2 %shard_map.113 = f32[32,8,128]{2,1,0:T(8,128)} custom-call(f32[1,256]{1,0:T(1,128)} %initial.3, f32[256,512]{1,0:T(8,128)} %bitcast.35, s32[1,128]{1,0:T(1,128)} %tap.3, f32[1,128]{1,0:T(1,128)} %att.1), custom_call_target="tpu_custom_call" | custom-call | tf_op jit(solution)/shard_map/pallas_call | solution.py:407
  3.4 7.0 %all-to-all-start = ((f32[32,8,128]{2,1,0:T(8,128)}), f32[32,8,128]{2,1,0:T(8,128)S(1)}, u32[]{:S(2)}, u32[]{:S(2)}) async-start(f32[32,8,128]{2,1,0:T(8,128)} %shard_map.113), calls=%async_computation | async-start | bytes 262144 | tf_op jit(solution)/shard_map/all_to_all | solution.py:465
  10.7 1.3 %shard_map.114.p_own = f32[40,256]{1,0:T(8,128)S(1)} custom-call(f32[32,256]{1,0:T(8,128)} %bitcast.40, f32[1,256]{1,0:T(1,128)} %initial.3, f32[1,256]{1,0:T(1,128)} %capacitance.1, f32[2,128,128]{2,1,0:T(8,128)} %bitcast.37, s32[1,128]{1,0:T(1,128)} %tap.3, s32[1,128]{1,0:T(1,128)} %drive.1, f32[1,128]{1,0:T(1,128)} %gain.1), custom_call_target="tpu_custom_call" | custom-call | tf_op jit(solution)/shard_map/pallas_call | solution.py:407
  12.4 0.9 %collective-permute-done.p_other = f32[40,256]{1,0:T(8,128)S(1)} collective-permute-done((f32[40,256]{1,0:T(8,128)S(1)}, f32[40,256]{1,0:T(8,128)S(1)}, u32[]{:S(2)}, u32[]{:S(2)}) %collective-permute-start) | collective-permute-done | bytes 40992 | tf_op jit(solution)/shard_map/ppermute | solution.py:447
  14.1 2.7 %shard_map.115 = (bf16[512,512]{1,0:T(8,128)(2,1)S(1)}, bf16[512,512]{1,0:T(8,128)(2,1)S(1)}, bf16[6,4,128,128]{3,2,1,0:T(8,128)(2,1)S(1)}, bf16[6,4,128,128]{3,...) custom-call(f32[2,128,128]{2,1,0:T(8,128)S(1)} %collective-permute-done.1.i_other, ...), custom_call_target="tpu_custom_call" | custom-call | tf_op jit(solution)/shard_map/pallas_call | solution.py:407
  16.8 1.7 %all-to-all-done.got = f32[32,8,128]{2,1,0:T(8,128)S(1)} async-done(((f32[32,8,128]{2,1,0:T(8,128)}), f32[32,8,128]{2,1,0:T(8,128)S(1)}, u32[]{:S(2)}, u32[]{:S(2)}) %all-to-all-start) | async-done | bytes 131104 | tf_op jit(solution)/shard_map/all_to_all | solution.py:465
  18.6 1.5 %shard_map.116 = (f32[32,512]{1,0:T(8,128)S(1)}, f32[32,512]{1,0:T(8,128)S(1)}, f32[32,512]{1,0:T(8,128)S(1)}, f32[32,512]{1,0:T(8,128)S(1)}, f32[32,512]{1,0:T(...) custom-call(f32[8,128]{1,0:T(8,128)S(1)} %broadcast_in_dim.4.spot.refs_0_, f32[32,8,128]{2,1,0:T(8,128)S(1)} %all-to-all-done.got, ...), custom_call_target="tpu_custom_call" | custom-call | tf_op jit(solution)/shard_map/pallas_call | solution.py:407
  20.1 0.9 %collective-permute-start.3 = (f32[32,512]{1,0:T(8,128)S(1)}, f32[32,512]{1,0:T(8,128)S(1)}, u32[]{:S(2)}, u32[]{:S(2)}) collective-permute-start(f32[32,512]{1,0:T(8,128)S(1)} %get-tuple-element.46), channel_id=1, source_target_pairs={{0,8},{1,3},{2,10},{3,1},{4,12},{5,7},{6,14},{7,5},{8,0},{9,11},{1... | collective-permute-start | bytes 196616 | tf_op jit(solution)/shard_map/ppermute | solution.py:455
  21.0 3.5 %collective-permute-done.3 = f32[32,512]{1,0:T(8,128)S(1)} collective-permute-done((f32[32,512]{1,0:T(8,128)S(1)}, f32[32,512]{1,0:T(8,128)S(1)}, u32[]{:S(2)}, u32[]{:S(2)}) %collective-permute-start.3) | collective-permute-done | bytes 65568 | tf_op jit(solution)/shard_map/ppermute | solution.py:455
  24.4 0.9 %collective-permute-start.4 = (f32[32,512]{1,0:T(8,128)S(1)}, f32[32,512]{1,0:T(8,128)S(1)}, u32[]{:S(2)}, u32[]{:S(2)}) collective-permute-start(f32[32,512]{1,0:T(8,128)S(1)} %add.21.own), channel_id=1, source_target_pairs={{0,8},{1,5},{2,10},{3,7},{4,12},{5,1},{6,14},{7,3},{8,0},{9,13},{1... | collective-permute-start | bytes 196616 | tf_op jit(solution)/shard_map/ppermute | solution.py:455
  25.3 3.8 %all-to-all-start.1 = ((f32[32,1,128]{2,1,0:T(1,128)}), f32[32,1,128]{2,1,0:T(1,128)S(1)}, u32[]{:S(2)}, u32[]{:S(2)}) async-start(f32[32,1,128]{2,1,0:T(1,128)} %bitcast.9), calls=%async_computation.1 | async-start | bytes 32768 | tf_op jit(solution)/shard_map/all_to_all | solution.py:465
  29.4 6.8 %all-to-all-done.1 = f32[32,1,128]{2,1,0:T(1,128)S(1)} async-done(((f32[32,1,128]{2,1,0:T(1,128)}), f32[32,1,128]{2,1,0:T(1,128)S(1)}, u32[]{:S(2)}, u32[]{:S(2)}) %all-to-all-start.1) | async-done | bytes 16416 | tf_op jit(solution)/shard_map/all_to_all | solution.py:465
  36.2 1.8 %shard_map.118 = (f32[32,512]{1,0:T(8,128)S(1)}, f32[32,512]{1,0:T(8,128)S(1)}, f32[32,512]{1,0:T(8,128)S(1)}, f32[32,512]{1,0:T(8,128)S(1)}, f32[32,512]{1,0:T(...) custom-call(f32[8,128]{1,0:T(8,128)S(1)} %broadcast_in_dim.4.spot.refs_0_, ...), custom_call_target="tpu_custom_call" | custom-call | tf_op jit(solution)/shard_map/pallas_call | solution.py:407
  39.2 3.1 %collective-permute-done.7 = f32[64,256]{1,0:T(8,128)S(1)} collective-permute-done((f32[64,256]{1,0:T(8,128)S(1)}, f32[64,256]{1,0:T(8,128)S(1)}, u32[]{:S(2)}, u32[]{:S(2)}) %collective-permute-start.7) | collective-permute-done | bytes 65568 | tf_op jit(solution)/shard_map/ppermute | solution.py:455
  43.0 2.6 %all-to-all-start.2 = ((f32[32,1,128]{2,1,0:T(1,128)}), f32[32,1,128]{2,1,0:T(1,128)S(1)}, u32[]{:S(2)}, u32[]{:S(2)}) async-start(f32[32,1,128]{2,1,0:T(1,128)} %bitcast.12), calls=%async_computation.2 | async-start | bytes 32768 | tf_op jit(solution)/shard_map/all_to_all | solution.py:465
  45.6 1.8 %collective-permute-start.6 = (f32[32,512]{1,0:T(8,128)S(1)}, f32[32,512]{1,0:T(8,128)S(1)}, u32[]{:S(2)}, u32[]{:S(2)}) collective-permute-start(f32[32,512]{1,0:T(8,128)S(1)} %add.22.own), channel_id=1, source_target_pairs={{0,8},{1,5},{2,10},{3,7},{4,12},{5,1},{6,14},{7,3},{8,0},{9,13},{1... | collective-permute-start | bytes 196616 | tf_op jit(solution)/shard_map/ppermute | solution.py:455
  47.4 2.5 %collective-permute-done.6.recv = f32[32,512]{1,0:T(8,128)S(1)} collective-permute-done((f32[32,512]{1,0:T(8,128)S(1)}, f32[32,512]{1,0:T(8,128)S(1)}, u32[]{:S(2)}, u32[]{:S(2)}) %collective-permute-start.6) | collective-permute-done | bytes 65568 | tf_op jit(solution)/shard_map/ppermute | solution.py:455
  50.2 2.5 %all-to-all-done.2 = f32[32,1,128]{2,1,0:T(1,128)S(1)} async-done(((f32[32,1,128]{2,1,0:T(1,128)}), f32[32,1,128]{2,1,0:T(1,128)S(1)}, u32[]{:S(2)}, u32[]{:S(2)}) %all-to-all-start.2) | async-done | bytes 16416 | tf_op jit(solution)/shard_map/all_to_all | solution.py:465
  52.7 1.6 %shard_map.120 = (f32[32,512]{1,0:T(8,128)S(1)}, f32[32,512]{1,0:T(8,128)S(1)}, f32[32,512]{1,0:T(8,128)S(1)}, f32[32,512]{1,0:T(8,128)S(1)}, f32[32,512]{1,0:T(...) custom-call(f32[8,128]{1,0:T(8,128)S(1)} %broadcast_in_dim.4.spot.refs_0_, f32[32,128]{1,0:T(8,128)S(1)} %bitcast.29, ...), custom_call_target="tpu_custom_call" | custom-call | tf_op jit(solution)/shard_map/pallas_call | solution.py:407
  55.0 3.7 %collective-permute-done.9 = f32[32,512]{1,0:T(8,128)S(1)} collective-permute-done((f32[32,512]{1,0:T(8,128)S(1)}, f32[32,512]{1,0:T(8,128)S(1)}, u32[]{:S(2)}, u32[]{:S(2)}) %collective-permute-start.9) | collective-permute-done | bytes 65568 | tf_op jit(solution)/shard_map/ppermute | solution.py:455
  59.4 3.3 %all-to-all-start.3 = ((f32[32,1,128]{2,1,0:T(1,128)}), f32[32,1,128]{2,1,0:T(1,128)S(1)}, u32[]{:S(2)}, u32[]{:S(2)}) async-start(f32[32,1,128]{2,1,0:T(1,128)} %bitcast.19), calls=%async_computation.3 | async-start | bytes 32768 | tf_op jit(solution)/shard_map/all_to_all | solution.py:465
  63.3 6.5 %all-to-all-done.3 = f32[32,1,128]{2,1,0:T(1,128)S(1)} async-done(((f32[32,1,128]{2,1,0:T(1,128)}), f32[32,1,128]{2,1,0:T(1,128)S(1)}, u32[]{:S(2)}, u32[]{:S(2)}) %all-to-all-start.3) | async-done | bytes 16416 | tf_op jit(solution)/shard_map/all_to_all | solution.py:465
  69.9 0.8 %shard_map.123 = (f32[32,256]{1,0:T(8,128)S(1)}, f32[32,256]{1,0:T(8,128)S(1)}, f32[64,256]{1,0:T(8,128)S(1)}) custom-call(f32[32,512]{1,0:T(8,128)S(1)} %get-tuple-element.66.w_in, f32[32,512]{1,0:T(8,128)S(1)} %get-tuple-element.67.r_in, bf16[6,4,128,128]{3,2,1,0:T(8,128)(2,1)S(1)} %get-tuple-element.39.ah.refs_6_, ...), custom_call_target="tpu_custom_call" | custom-call | tf_op jit(solution)/shard_map/pallas_call | solution.py:407
  70.7 8.9 %all_to_all.25 = f32[32,1,128]{2,1,0:T(1,128)S(1)} all-to-all(f32[32,1,128]{2,1,0:T(1,128)S(1)} %bitcast.33), channel_id=1, replica_groups=mesh['section'=4,'dom'=8] {'section','dom'}, dimensions={0} | all-to-all | bytes 32768 | tf_op jit(solution)/shard_map/all_to_all | solution.py:465
  (34 shorter events, 7.4 us)
Async XLA Ops:
  0.6 12.6 %collective-permute-start.2 = (f32[256,512]{1,0:T(8,128)}, f32[256,512]{1,0:T(8,128)S(1)}, u32[]{:S(2)}, u32[]{:S(2)}) collective-permute-start(f32[256,512]{1,0:T(8,128)} %bitcast.34), channel_id=1, source_target_pairs={{0,1},{1,0},{2,3},{3,2},{4,5},{5,4},{6,7},{7,6},{8,9},{9,8},{10,11... | collective-permute-start | bytes 1572872 | tf_op jit(solution)/shard_map/ppermute | solution.py:447
  3.4 7.0 %copy-start.1 = (f32[1,2,128,128]{3,2,1,0:T(8,128)S(1)}, f32[1,2,128,128]{3,2,1,0:T(8,128)}, u32[]{:S(2)}) copy-start(f32[1,2,128,128]{3,2,1,0:T(8,128)} %param.14) | copy-start | bytes 393220
  3.4 15.1 %all-to-all-start = ((f32[32,8,128]{2,1,0:T(8,128)}), f32[32,8,128]{2,1,0:T(8,128)S(1)}, u32[]{:S(2)}, u32[]{:S(2)}) async-start(f32[32,8,128]{2,1,0:T(8,128)} %shard_map.113), calls=%async_computation | async-start | bytes 262144 | tf_op jit(solution)/shard_map/all_to_all | solution.py:465
  10.3 2.9 %collective-permute-start.1 = (f32[2,128,128]{2,1,0:T(8,128)S(1)}, f32[2,128,128]{2,1,0:T(8,128)S(1)}, u32[]{:S(2)}, u32[]{:S(2)}) collective-permute-start(f32[2,128,128]{2,1,0:T(8,128)S(1)} %bitcast.39), channel_id=1, source_target_pairs={{0,1},{1,0},{2,3},{3,2},{4,5},{5,4},{6,7},{7,6},{8,9},{9,8},{10,11... | collective-permute-start | bytes 393224 | tf_op jit(solution)/shard_map/ppermute | solution.py:447
  12.0 1.3 %collective-permute-start = (f32[40,256]{1,0:T(8,128)S(1)}, f32[40,256]{1,0:T(8,128)S(1)}, u32[]{:S(2)}, u32[]{:S(2)}) collective-permute-start(f32[40,256]{1,0:T(8,128)S(1)} %shard_map.114.p_own), channel_id=1, source_target_pairs={{0,1},{1,0},{2,3},{3,2},{4,5},{5,4},{6,7},{7,6},{8,9},{9,8},{10,11... | collective-permute-start | bytes 122888 | tf_op jit(solution)/shard_map/ppermute | solution.py:447
  13.3 0.8 %copy-start = (f32[256,512]{1,0:T(8,128)}, f32[256,512]{1,0:T(8,128)S(1)}, u32[]{:S(2)}) copy-start(f32[256,512]{1,0:T(8,128)S(1)} %collective-permute-done.2.w_other) | copy-start | bytes 1572868
  20.1 4.3 %collective-permute-start.3 = (f32[32,512]{1,0:T(8,128)S(1)}, f32[32,512]{1,0:T(8,128)S(1)}, u32[]{:S(2)}, u32[]{:S(2)}) collective-permute-start(f32[32,512]{1,0:T(8,128)S(1)} %get-tuple-element.46), channel_id=1, source_target_pairs={{0,8},{1,3},{2,10},{3,1},{4,12},{5,7},{6,14},{7,5},{8,0},{9,11},{1... | collective-permute-start | bytes 196616 | tf_op jit(solution)/shard_map/ppermute | solution.py:455
  24.4 4.7 %collective-permute-start.4 = (f32[32,512]{1,0:T(8,128)S(1)}, f32[32,512]{1,0:T(8,128)S(1)}, u32[]{:S(2)}, u32[]{:S(2)}) collective-permute-start(f32[32,512]{1,0:T(8,128)S(1)} %add.21.own), channel_id=1, source_target_pairs={{0,8},{1,5},{2,10},{3,7},{4,12},{5,1},{6,14},{7,3},{8,0},{9,13},{1... | collective-permute-start | bytes 196616 | tf_op jit(solution)/shard_map/ppermute | solution.py:455
  25.3 10.9 %all-to-all-start.1 = ((f32[32,1,128]{2,1,0:T(1,128)}), f32[32,1,128]{2,1,0:T(1,128)S(1)}, u32[]{:S(2)}, u32[]{:S(2)}) async-start(f32[32,1,128]{2,1,0:T(1,128)} %bitcast.9), calls=%async_computation.1 | async-start | bytes 32768 | tf_op jit(solution)/shard_map/all_to_all | solution.py:465
  38.0 4.3 %collective-permute-start.7 = (f32[64,256]{1,0:T(8,128)S(1)}, f32[64,256]{1,0:T(8,128)S(1)}, u32[]{:S(2)}, u32[]{:S(2)}) collective-permute-start(f32[64,256]{1,0:T(8,128)S(1)} %get-tuple-element.58), channel_id=1, source_target_pairs={{0,2},{1,9},{2,0},{3,11},{4,6},{5,13},{6,4},{7,15},{8,10},{9,1},{1... | collective-permute-start | bytes 196616 | tf_op jit(solution)/shard_map/ppermute | solution.py:455
  38.6 6.9 %collective-permute-start.5 = (f32[32,512]{1,0:T(8,128)S(1)}, f32[32,512]{1,0:T(8,128)S(1)}, u32[]{:S(2)}, u32[]{:S(2)}) collective-permute-start(f32[32,512]{1,0:T(8,128)S(1)} %get-tuple-element.53), channel_id=1, source_target_pairs={{0,8},{1,3},{2,10},{3,1},{4,12},{5,7},{6,14},{7,5},{8,0},{9,11},{1... | collective-permute-start | bytes 196616 | tf_op jit(solution)/shard_map/ppermute | solution.py:455
  42.4 5.1 %collective-permute-start.8 = (f32[64,256]{1,0:T(8,128)S(1)}, f32[64,256]{1,0:T(8,128)S(1)}, u32[]{:S(2)}, u32[]{:S(2)}) collective-permute-start(f32[64,256]{1,0:T(8,128)S(1)} %multiply_add_fusion.1), channel_id=1, source_target_pairs={{0,2},{1,17},{2,0},{3,19},{4,6},{5,21},{6,4},{7,23},{8,10},{9,25},... | collective-permute-start | bytes 196616 | tf_op jit(solution)/shard_map/ppermute | solution.py:455
  43.0 9.8 %all-to-all-start.2 = ((f32[32,1,128]{2,1,0:T(1,128)}), f32[32,1,128]{2,1,0:T(1,128)S(1)}, u32[]{:S(2)}, u32[]{:S(2)}) async-start(f32[32,1,128]{2,1,0:T(1,128)} %bitcast.12), calls=%async_computation.2 | async-start | bytes 32768 | tf_op jit(solution)/shard_map/all_to_all | solution.py:465
  45.6 4.4 %collective-permute-start.6 = (f32[32,512]{1,0:T(8,128)S(1)}, f32[32,512]{1,0:T(8,128)S(1)}, u32[]{:S(2)}, u32[]{:S(2)}) collective-permute-start(f32[32,512]{1,0:T(8,128)S(1)} %add.22.own), channel_id=1, source_target_pairs={{0,8},{1,5},{2,10},{3,7},{4,12},{5,1},{6,14},{7,3},{8,0},{9,13},{1... | collective-permute-start | bytes 196616 | tf_op jit(solution)/shard_map/ppermute | solution.py:455
  54.4 4.3 %collective-permute-start.9 = (f32[32,512]{1,0:T(8,128)S(1)}, f32[32,512]{1,0:T(8,128)S(1)}, u32[]{:S(2)}, u32[]{:S(2)}) collective-permute-start(f32[32,512]{1,0:T(8,128)S(1)} %get-tuple-element.60), channel_id=1, source_target_pairs={{0,8},{1,3},{2,10},{3,1},{4,12},{5,7},{6,14},{7,5},{8,0},{9,11},{1... | collective-permute-start | bytes 196616 | tf_op jit(solution)/shard_map/ppermute | solution.py:455
  58.7 4.3 %collective-permute-start.10 = (f32[32,512]{1,0:T(8,128)S(1)}, f32[32,512]{1,0:T(8,128)S(1)}, u32[]{:S(2)}, u32[]{:S(2)}) collective-permute-start(f32[32,512]{1,0:T(8,128)S(1)} %add.25.own), channel_id=1, source_target_pairs={{0,8},{1,5},{2,10},{3,7},{4,12},{5,1},{6,14},{7,3},{8,0},{9,13},{1... | collective-permute-start | bytes 196616 | tf_op jit(solution)/shard_map/ppermute | solution.py:455
  59.4 10.4 %all-to-all-start.3 = ((f32[32,1,128]{2,1,0:T(1,128)}), f32[32,1,128]{2,1,0:T(1,128)S(1)}, u32[]{:S(2)}, u32[]{:S(2)}) async-start(f32[32,1,128]{2,1,0:T(1,128)} %bitcast.19), calls=%async_computation.3 | async-start | bytes 32768 | tf_op jit(solution)/shard_map/all_to_all | solution.py:465
  70.7 8.9 %collective-permute-start.11 = (f32[64,256]{1,0:T(8,128)S(1)}, f32[64,256]{1,0:T(8,128)S(1)}, u32[]{:S(2)}, u32[]{:S(2)}) collective-permute-start(f32[64,256]{1,0:T(8,128)S(1)} %get-tuple-element.70), channel_id=1, source_target_pairs={{0,1},{1,0},{2,3},{3,2},{4,5},{5,4},{6,7},{7,6},{8,9},{9,8},{10,11... | collective-permute-start | bytes 196616 | tf_op jit(solution)/shard_map/ppermute | solution.py:447

commit v4 on v3

--- a/solution.py
+++ b/solution.py
@@ -111,14 +111,14 @@
     msg[...] = jnp.broadcast_to(tile[None], msg.shape)
 
 
-def pack_kernel(source, initial, capacitance, matrix, tap, drive, gain, pack,
+def pack_kernel(source, initial, capacitance, matrix, tap, drive, gain, inverse, pack, near_inverse,
                 b_initial, b_capacitance, b_matrix, b_tap, b_drive, b_gain, sems):
     steps, nodes = source.shape
     blocks, width = matrix.shape[0], matrix.shape[1]
     channels = tap.shape[1]
     copies = land(
         [(initial, b_initial), (matrix, b_matrix), (capacitance, b_capacitance), (tap, b_tap), (drive, b_drive),
-         (gain, b_gain), (source, pack.at[0:steps, :])],
+         (gain, b_gain), (source, pack.at[0:steps, :]), (inverse, near_inverse)],
         sems,
     )
     pack[steps : steps + SUB, :] = jnp.zeros((SUB, nodes), F32)
@@ -147,23 +147,11 @@
     return jnp.concatenate([ref_other[lo:hi, :], ref_own[lo:hi, :]], axis=1)
 
 
-def prep_kernel(plan, steps, i_other, w_other, w_own, i_own, p_other, p_own, th, tl, ah, al, wh, wl,
-                b_w, b_i, s_wh, s_wl, sems):
+def prep_kernel(plan, w_other, w_own, i_other, i_own, cap_other, cap_own, th, tl, ah, al, b_w, sems):
     nodes = w_own.shape[0]
     blocks, width = i_own.shape[0], i_own.shape[1]
-    copies = land([(i_own, b_i), (w_other, b_w.at[0]), (w_own, b_w.at[1])], sems)
-    cap = both(p_other, p_own, steps + 2, steps + 3)
-    for copy in copies[1:]:
-        copy.wait()
-    for half in range(2):
-        here = slice(half * nodes, (half + 1) * nodes)
-        h, l = split(b_w[half])
-        s_wh[here, :] = h
-        s_wl[here, :] = l
-    backs = [pltpu.make_async_copy(s_wh, wh, sems.at[3]), pltpu.make_async_copy(s_wl, wl, sems.at[4])]
-    for copy in backs:
-        copy.start()
-    copies[0].wait()
+    copies = land([(w_other, b_w.at[0]), (w_own, b_w.at[1])], sems)
+    cap = jnp.concatenate([cap_other[...], cap_own[...]], axis=1)
     wanted = powers_of(plan)
     eye = lax.broadcasted_iota(jnp.int32, (width, width), 0) == lax.broadcasted_iota(jnp.int32, (width, width), 1)
 
@@ -171,7 +159,7 @@
         return bdot(x[0], y[0]) + bdot(x[1], y[0]) + bdot(x[0], y[1])
 
     every = range(2 * blocks)
-    inverse = [split((i_other if b < blocks else b_i)[b % blocks].T) for b in every]
+    inverse = [split((i_other if b < blocks else i_own)[b % blocks].T) for b in every]
     scale = [split(jnp.where(eye, cap[:, b * width : (b + 1) * width], 0.0)) for b in every]
     made = {1: [split(times(scale[b], inverse[b])) for b in every]}
     todo = [inverse, [split(times(inverse[b], made[1][b])) for b in every]]
@@ -187,13 +175,13 @@
     for i, value in enumerate(todo):
         for b in every:
             ah[i, b], al[i, b] = value[b]
+    for copy in copies:
+        copy.wait()
     for half in range(2):
         here = slice(half * nodes, (half + 1) * nodes)
         h, l = split(b_w[half].T)
         th[:, here] = h
         tl[:, here] = l
-    for copy in backs:
-        copy.wait()
 
 
 def march(plan, x, ah, al):
@@ -221,23 +209,23 @@
     msg[...] = jnp.broadcast_to(row, msg.shape)
 
 
-def finish_round(plan, r, spot, c_ref, p_ref, msg, ah, al, sent, copies, wh, wl):
+def finish_round(plan, r, spot, c_ref, p_ref, msg, ah, al, sent, th, tl):
     near_msg, sem = sent
     send_squares(r, spot, near_msg)
     leaving = pltpu.make_async_copy(near_msg, msg, sem.at[0])
     leaving.start()
     c = march(plan, r, ah, al)
     c_ref[...] = c
-    for copy in copies:
-        copy.wait()
-    p_ref[...] = dot3(c, wh[...], wl[...])
+    rows = c.shape[0]
+    ch, cl = split(c)
+    two = tdot(jnp.concatenate([ch, cl], axis=0), th[...])
+    p_ref[...] = two[:rows] + two[rows:] + tdot(ch, tl[...])
     leaving.wait()
     return c
 
 
-def opening_kernel(plan, steps, channels, sections, doms, levels, spot, got, p_other, p_own, ah, al, th, tl, wh, wl,
-                   w_ref, q_ref, r_ref, c_ref, p_ref, msg, aux_ref, near_h, near_l, sems, *sent):
-    copies = land([(wh, near_h), (wl, near_l)], sems)
+def opening_kernel(plan, steps, channels, sections, doms, levels, spot, got, p_other, p_own, ah, al, th, tl,
+                   w_ref, q_ref, r_ref, c_ref, p_ref, msg, aux_ref, *sent):
     my, chip = spot[0:1, :], spot[1:2, :]
     nets = th.shape[0]
     net_rows = nets // LANES
@@ -303,7 +291,7 @@
     w_ref[...] = jnp.broadcast_to(start, w_ref.shape)
     q_ref[...] = q
     r_ref[...] = r
-    finish_round(plan, r, spot, c_ref, p_ref, msg, ah, al, sent, copies, near_h, near_l)
+    finish_round(plan, r, spot, c_ref, p_ref, msg, ah, al, sent, th, tl)
 
 
 def chosen(index, nodes):
@@ -342,14 +330,13 @@
 def round_kernel(plan, steps, channels, cells, mode, *refs):
     refs = list(refs)
     take = lambda n: [refs.pop(0) for _ in range(n)]
-    (spot, got, u, w0, q0, c0, ah, al, wh, wl, aux) = take(11)
+    (spot, got, u, w0, q0, c0, ah, al, th, tl, aux) = take(11)
     if mode == "drive":
         (pre,) = take(1)
     w_ref, q_ref, r_ref, c_ref, p_ref, msg, mean_ref = take(7)
     if mode == "taps":
         (tt_ref,) = take(1)
-    near_h, near_l, sems, *sent = take(5)
-    copies = land([(wh, near_h), (wl, near_l)], sems)
+    sent = take(2)
     w, q, damp = advance(got, u, w0, q0, c0, cells, mean_ref)
     if mode == "drive":
         drive = pre[0:steps, :] - damp * pre[steps : 2 * steps, :]
@@ -359,7 +346,7 @@
     w_ref[...] = w
     q_ref[...] = q
     r_ref[...] = r
-    c = finish_round(plan, r, spot, c_ref, p_ref, msg, ah, al, sent, copies, near_h, near_l)
+    c = finish_round(plan, r, spot, c_ref, p_ref, msg, ah, al, sent, th, tl)
     if mode == "taps":
         half = w.shape[1] // 2
         for h in range(2):
@@ -469,6 +456,7 @@
     spot = jnp.broadcast_to(spot[:, None], (SUB, LANES))
     w_other = swap(net_weight)
     i_other = swap(block_inverse)
+    cap_other = swap(capacitance)
     first_message = ((devices, SUB, LANES), F32)
     message = ((devices, LANES), F32)
     row = lambda n, d=F32: pltpu.VMEM((1, n), d)
@@ -483,39 +471,35 @@
         ],
     )
     got = gather(msg)
-    (pack,) = call(
+    pack, i_own = call(
         pack_kernel,
-        [((steps + SUB, nodes), F32)],
-        source, initial, capacitance, block_matrix, tap_nodes, drive_nodes, drive_gain,
-        hbm=range(7),
+        [((steps + SUB, nodes), F32), (block_inverse.shape, F32)],
+        source, initial, capacitance, block_matrix, tap_nodes, drive_nodes, drive_gain, block_inverse,
+        hbm=range(8),
         scratch=[
             row(nodes), row(nodes), pltpu.VMEM(block_matrix.shape, F32),
-            row(channels, jnp.int32), row(channels, jnp.int32), row(channels), pltpu.SemaphoreType.DMA((7,)),
+            row(channels, jnp.int32), row(channels, jnp.int32), row(channels), pltpu.SemaphoreType.DMA((8,)),
         ],
     )
     p_other = swap(pack)
     cut = ((units, 2 * blocks, width, width), BF16)
-    up, down = ((nets, wide), BF16), ((wide, nets), BF16)
-    th, tl, ah, al, wh, wl = call(
-        functools.partial(prep_kernel, plan, steps),
-        [up, up, cut, cut, down, down],
-        i_other, w_other, net_weight, block_inverse, p_other, pack,
-        hbm=range(1, 4),
-        hbm_outs=(4, 5),
+    up = ((nets, wide), BF16)
+    th, tl, ah, al = call(
+        functools.partial(prep_kernel, plan),
+        [up, up, cut, cut],
+        w_other, net_weight, i_other, i_own, cap_other, capacitance,
+        hbm=range(2),
         scratch=[
-            pltpu.VMEM((2, nodes, nets), F32), pltpu.VMEM((blocks, width, width), F32),
-            pltpu.VMEM(*down), pltpu.VMEM(*down), pltpu.SemaphoreType.DMA((5,)),
+            pltpu.VMEM((2, nodes, nets), F32), pltpu.SemaphoreType.DMA((2,)),
         ],
     )
     state = [((steps, wide), F32)] * 4
-    landing = [pltpu.VMEM(*down), pltpu.VMEM(*down), pltpu.SemaphoreType.DMA((2,))]
-    landing = landing + [pltpu.VMEM(*message), pltpu.SemaphoreType.DMA((1,))]
+    landing = [pltpu.VMEM(*message), pltpu.SemaphoreType.DMA((1,))]
     aux_shape = (-(-(4 + 3 * levels) // SUB) * SUB, max(wide, 2 * channels))
     w, q, r, c, part, msg, aux = call(
         functools.partial(opening_kernel, plan, steps, channels, sections, doms, levels),
         state + [((steps, nets), F32), message, (aux_shape, F32)],
-        spot, got, p_other, pack, ah, al, th, tl, wh, wl,
-        hbm=(8, 9),
+        spot, got, p_other, pack, ah, al, th, tl,
         hbm_outs=(5,),
         scratch=landing,
     )
@@ -553,8 +537,7 @@
         result = call(
             functools.partial(round_kernel, plan, steps, channels, cells, mode),
             outs,
-            spot, got, u, w, q, c, ah, al, wh, wl, aux, *extra,
-            hbm=(8, 9),
+            spot, got, u, w, q, c, ah, al, th, tl, aux, *extra,
             hbm_outs=(5,),
             scratch=landing,
         )

time: 80.7 us -> 80.2 us (level)
  Pallas kernels: 13.6 us -> 12.6 us
    pallas_call x12, Pallas kernels: 13.6 us -> 12.6 us  [call(): pl.pallas_call(kernel, out_shape=[pltpu.HBM(s, d) if i in hbm_outs else j...]
  transfers between devices with their start and end apart: 16 -> 17, of which waited for: 10 -> 10; matrix products, arithmetic and copies ran while one was open for 0% -> 0% of each run, Pallas kernels for 9% -> 8%
where the time goes in v4:
time: 80.2 us; the launch traced here: 79.9 us
  waiting for transfers between devices  31.7 us (40%)
  starting transfers between devices  24.5 us (31%)
  Pallas kernels  12.6 us (16%)
  blocking collectives  8.87 us (11%)
  local copies, waits for them, and re-layouts  1.32 us (2%)
  between operations  0.81 us (1%)
    all_to_all x4, waiting for transfers between devices, gather(): lax.all_to_all(spread_out, everywhere, 0, 0, tiled=False).reshape(msg.shape)  17.7 us
    all_to_all x4, starting transfers between devices, gather(): lax.all_to_all(spread_out, everywhere, 0, 0, tiled=False).reshape(msg.shape)  16.4 us
    ppermute x8, waiting for transfers between devices, pair(): return lax.ppermute(x, everywhere, links)  13.2 us
    pallas_call x12, Pallas kernels, call(): pl.pallas_call(kernel, out_shape=[pltpu.HBM(s, d) if i in hbm_outs else j...  12.6 us
    all_to_all x1, blocking collectives, gather(): lax.all_to_all(spread_out, everywhere, 0, 0, tiled=False).reshape(msg.shape)  8.87 us
    ppermute x8, starting transfers between devices, pair(): return lax.ppermute(x, everywhere, links)  6.71 us
  transfers between devices with their start and end apart: 17, of which 10 were waited for; matrix products, arithmetic and copies ran while one was open for 0% of the time, Pallas kernels for 8%

profile of v4, /device:TPU:0, one launch (start us, length us, event | category | flops | bytes accessed | tf_op | source)
XLA Modules:
  0.0 79.9 jit_solution(251096729267805737)
XLA Ops:
  1.2 2.2 %shard_map.113 = f32[32,8,128]{2,1,0:T(8,128)} custom-call(f32[1,256]{1,0:T(1,128)} %initial.3, f32[256,512]{1,0:T(8,128)} %bitcast.35, s32[1,128]{1,0:T(1,128)} %tap.3, f32[1,128]{1,0:T(1,128)} %att.1), custom_call_target="tpu_custom_call" | custom-call | tf_op jit(solution)/shard_map/pallas_call | solution.py:394
  3.4 7.0 %all-to-all-start = ((f32[32,8,128]{2,1,0:T(8,128)}), f32[32,8,128]{2,1,0:T(8,128)S(1)}, u32[]{:S(2)}, u32[]{:S(2)}) async-start(f32[32,8,128]{2,1,0:T(8,128)} %shard_map.113), calls=%async_computation | async-start | bytes 262144 | tf_op jit(solution)/shard_map/all_to_all | solution.py:452
  10.7 1.5 %shard_map.114 = (f32[40,256]{1,0:T(8,128)S(1)}, f32[2,128,128]{2,1,0:T(8,128)S(1)}) custom-call(f32[32,256]{1,0:T(8,128)} %bitcast.40, f32[1,256]{1,0:T(1,128)} %initial.3, f32[1,256]{1,0:T(1,128)} %cap_own.1, f32[2,128,128]{2,1,0:T(8,128)} %bitcast.37, s32[1,128]{1,0:T(1,128)} %tap.3, s32[1,128]{1,0:T(1,128)} %drive.1, f32[1,128]{1,0:T(1,128)} %gain.1, ...), custom_call_target="tpu_custom_call" | custom-call | tf_op jit(solution)/shard_map/pallas_call | solution.py:394
  13.1 0.8 %collective-permute-done.3.cap_other = f32[1,256]{1,0:T(1,128)S(1)} collective-permute-done((f32[1,256]{1,0:T(1,128)S(1)}, f32[1,256]{1,0:T(1,128)S(1)}, u32[]{:S(2)}, u32[]{:S(2)}) %collective-permute-start.3) | collective-permute-done | bytes 1056 | tf_op jit(solution)/shard_map/ppermute | solution.py:434
  14.8 1.7 %shard_map.115 = (bf16[512,512]{1,0:T(8,128)(2,1)S(1)}, bf16[512,512]{1,0:T(8,128)(2,1)S(1)}, bf16[6,4,128,128]{3,2,1,0:T(8,128)(2,1)S(1)}, bf16[6,4,128,128]{3,2,1,0:T(8,128)(2,1)S(1)}) custom-call(f32[256,512]{1,0:T(8,128)} %copy-done.1, f32[256,512]{1,0:T(8,128)} %bitcast.36, f32[2,128,128]{2,1,0:T(8,128)S(1)} %collective-permute-done.2.i_other, ...), custom_call_target="tpu_custom_call" | custom-call | tf_op jit(solution)/shard_map/pallas_call | solution.py:394
  16.5 2.0 %all-to-all-done.got = f32[32,8,128]{2,1,0:T(8,128)S(1)} async-done(((f32[32,8,128]{2,1,0:T(8,128)}), f32[32,8,128]{2,1,0:T(8,128)S(1)}, u32[]{:S(2)}, u32[]{:S(2)}) %all-to-all-start) | async-done | bytes 131104 | tf_op jit(solution)/shard_map/all_to_all | solution.py:452
  18.6 1.6 %shard_map.116 = (f32[32,512]{1,0:T(8,128)S(1)}, f32[32,512]{1,0:T(8,128)S(1)}, f32[32,512]{1,0:T(8,128)S(1)}, f32[32,512]{1,0:T(8,128)S(1)}, f32[32,512]{1,0:T(...) custom-call(f32[8,128]{1,0:T(8,128)S(1)} %broadcast_in_dim.4.spot.refs_0_, f32[32,8,128]{2,1,0:T(8,128)S(1)} %all-to-all-done.got, ...), custom_call_target="tpu_custom_call" | custom-call | tf_op jit(solution)/shard_map/pallas_call | solution.py:394
  20.2 0.9 %collective-permute-start.4 = (f32[32,512]{1,0:T(8,128)S(1)}, f32[32,512]{1,0:T(8,128)S(1)}, u32[]{:S(2)}, u32[]{:S(2)}) collective-permute-start(f32[32,512]{1,0:T(8,128)S(1)} %get-tuple-element.46), channel_id=1, source_target_pairs={{0,8},{1,3},{2,10},{3,1},{4,12},{5,7},{6,14},{7,5},{8,0},{9,11},{1... | collective-permute-start | bytes 196616 | tf_op jit(solution)/shard_map/ppermute | solution.py:442
  21.0 3.5 %collective-permute-done.4 = f32[32,512]{1,0:T(8,128)S(1)} collective-permute-done((f32[32,512]{1,0:T(8,128)S(1)}, f32[32,512]{1,0:T(8,128)S(1)}, u32[]{:S(2)}, u32[]{:S(2)}) %collective-permute-start.4) | collective-permute-done | bytes 65568 | tf_op jit(solution)/shard_map/ppermute | solution.py:442
  24.5 0.9 %collective-permute-start.5 = (f32[32,512]{1,0:T(8,128)S(1)}, f32[32,512]{1,0:T(8,128)S(1)}, u32[]{:S(2)}, u32[]{:S(2)}) collective-permute-start(f32[32,512]{1,0:T(8,128)S(1)} %add.21.own), channel_id=1, source_target_pairs={{0,8},{1,5},{2,10},{3,7},{4,12},{5,1},{6,14},{7,3},{8,0},{9,13},{1... | collective-permute-start | bytes 196616 | tf_op jit(solution)/shard_map/ppermute | solution.py:442
  25.4 3.5 %all-to-all-start.1 = ((f32[32,1,128]{2,1,0:T(1,128)}), f32[32,1,128]{2,1,0:T(1,128)S(1)}, u32[]{:S(2)}, u32[]{:S(2)}) async-start(f32[32,1,128]{2,1,0:T(1,128)} %bitcast.9), calls=%async_computation.1 | async-start | bytes 32768 | tf_op jit(solution)/shard_map/all_to_all | solution.py:452
  29.2 6.8 %all-to-all-done.1 = f32[32,1,128]{2,1,0:T(1,128)S(1)} async-done(((f32[32,1,128]{2,1,0:T(1,128)}), f32[32,1,128]{2,1,0:T(1,128)S(1)}, u32[]{:S(2)}, u32[]{:S(2)}) %all-to-all-start.1) | async-done | bytes 16416 | tf_op jit(solution)/shard_map/all_to_all | solution.py:452
  36.0 1.6 %shard_map.118 = (f32[32,512]{1,0:T(8,128)S(1)}, f32[32,512]{1,0:T(8,128)S(1)}, f32[32,512]{1,0:T(8,128)S(1)}, f32[32,512]{1,0:T(8,128)S(1)}, f32[32,512]{1,0:T(...) custom-call(f32[8,128]{1,0:T(8,128)S(1)} %broadcast_in_dim.4.spot.refs_0_, ...), custom_call_target="tpu_custom_call" | custom-call | tf_op jit(solution)/shard_map/pallas_call | solution.py:394
  38.8 3.1 %collective-permute-done.8 = f32[64,256]{1,0:T(8,128)S(1)} collective-permute-done((f32[64,256]{1,0:T(8,128)S(1)}, f32[64,256]{1,0:T(8,128)S(1)}, u32[]{:S(2)}, u32[]{:S(2)}) %collective-permute-start.8) | collective-permute-done | bytes 65568 | tf_op jit(solution)/shard_map/ppermute | solution.py:442
  42.6 2.6 %all-to-all-start.2 = ((f32[32,1,128]{2,1,0:T(1,128)}), f32[32,1,128]{2,1,0:T(1,128)S(1)}, u32[]{:S(2)}, u32[]{:S(2)}) async-start(f32[32,1,128]{2,1,0:T(1,128)} %bitcast.12), calls=%async_computation.2 | async-start | bytes 32768 | tf_op jit(solution)/shard_map/all_to_all | solution.py:452
  45.2 1.8 %collective-permute-start.7 = (f32[32,512]{1,0:T(8,128)S(1)}, f32[32,512]{1,0:T(8,128)S(1)}, u32[]{:S(2)}, u32[]{:S(2)}) collective-permute-start(f32[32,512]{1,0:T(8,128)S(1)} %add.22.own), channel_id=1, source_target_pairs={{0,8},{1,5},{2,10},{3,7},{4,12},{5,1},{6,14},{7,3},{8,0},{9,13},{1... | collective-permute-start | bytes 196616 | tf_op jit(solution)/shard_map/ppermute | solution.py:442
  47.1 2.5 %collective-permute-done.7.recv = f32[32,512]{1,0:T(8,128)S(1)} collective-permute-done((f32[32,512]{1,0:T(8,128)S(1)}, f32[32,512]{1,0:T(8,128)S(1)}, u32[]{:S(2)}, u32[]{:S(2)}) %collective-permute-start.7) | collective-permute-done | bytes 65568 | tf_op jit(solution)/shard_map/ppermute | solution.py:442
  49.9 2.5 %all-to-all-done.2 = f32[32,1,128]{2,1,0:T(1,128)S(1)} async-done(((f32[32,1,128]{2,1,0:T(1,128)}), f32[32,1,128]{2,1,0:T(1,128)S(1)}, u32[]{:S(2)}, u32[]{:S(2)}) %all-to-all-start.2) | async-done | bytes 16416 | tf_op jit(solution)/shard_map/all_to_all | solution.py:452
  52.3 1.6 %shard_map.120 = (f32[32,512]{1,0:T(8,128)S(1)}, f32[32,512]{1,0:T(8,128)S(1)}, f32[32,512]{1,0:T(8,128)S(1)}, f32[32,512]{1,0:T(8,128)S(1)}, f32[32,512]{1,0:T(...) custom-call(f32[8,128]{1,0:T(8,128)S(1)} %broadcast_in_dim.4.spot.refs_0_, f32[32,128]{1,0:T(8,128)S(1)} %bitcast.29, ...), custom_call_target="tpu_custom_call" | custom-call | tf_op jit(solution)/shard_map/pallas_call | solution.py:394
  54.6 3.7 %collective-permute-done.10 = f32[32,512]{1,0:T(8,128)S(1)} collective-permute-done((f32[32,512]{1,0:T(8,128)S(1)}, f32[32,512]{1,0:T(8,128)S(1)}, u32[]{:S(2)}, u32[]{:S(2)}) %collective-permute-start.10) | collective-permute-done | bytes 65568 | tf_op jit(solution)/shard_map/ppermute | solution.py:442
  58.9 3.3 %all-to-all-start.3 = ((f32[32,1,128]{2,1,0:T(1,128)}), f32[32,1,128]{2,1,0:T(1,128)S(1)}, u32[]{:S(2)}, u32[]{:S(2)}) async-start(f32[32,1,128]{2,1,0:T(1,128)} %bitcast.19), calls=%async_computation.3 | async-start | bytes 32768 | tf_op jit(solution)/shard_map/all_to_all | solution.py:452
  62.9 6.5 %all-to-all-done.3 = f32[32,1,128]{2,1,0:T(1,128)S(1)} async-done(((f32[32,1,128]{2,1,0:T(1,128)}), f32[32,1,128]{2,1,0:T(1,128)S(1)}, u32[]{:S(2)}, u32[]{:S(2)}) %all-to-all-start.3) | async-done | bytes 16416 | tf_op jit(solution)/shard_map/all_to_all | solution.py:452
  69.5 0.8 %shard_map.123 = (f32[32,256]{1,0:T(8,128)S(1)}, f32[32,256]{1,0:T(8,128)S(1)}, f32[64,256]{1,0:T(8,128)S(1)}) custom-call(f32[32,512]{1,0:T(8,128)S(1)} %get-tuple-element.66.w_in, f32[32,512]{1,0:T(8,128)S(1)} %get-tuple-element.67.r_in, bf16[6,4,128,128]{3,2,1,0:T(8,128)(2,1)S(1)} %get-tuple-element.41.ah.refs_6_, ...), custom_call_target="tpu_custom_call" | custom-call | tf_op jit(solution)/shard_map/pallas_call | solution.py:394
  70.3 8.9 %all_to_all.25 = f32[32,1,128]{2,1,0:T(1,128)S(1)} all-to-all(f32[32,1,128]{2,1,0:T(1,128)S(1)} %bitcast.33), channel_id=1, replica_groups=mesh['section'=4,'dom'=8] {'section','dom'}, dimensions={0} | all-to-all | bytes 32768 | tf_op jit(solution)/shard_map/all_to_all | solution.py:452
  (38 shorter events, 8.0 us)
Async XLA Ops:
  0.6 13.3 %collective-permute-start.1 = (f32[256,512]{1,0:T(8,128)}, f32[256,512]{1,0:T(8,128)S(1)}, u32[]{:S(2)}, u32[]{:S(2)}) collective-permute-start(f32[256,512]{1,0:T(8,128)} %bitcast.34), channel_id=1, source_target_pairs={{0,1},{1,0},{2,3},{3,2},{4,5},{5,4},{6,7},{7,6},{8,9},{9,8},{10,11... | collective-permute-start | bytes 1572872 | tf_op jit(solution)/shard_map/ppermute | solution.py:434
  3.4 7.0 %copy-start.2 = (f32[1,2,128,128]{3,2,1,0:T(8,128)S(1)}, f32[1,2,128,128]{3,2,1,0:T(8,128)}, u32[]{:S(2)}) copy-start(f32[1,2,128,128]{3,2,1,0:T(8,128)} %param.14) | copy-start | bytes 393220
  3.4 15.1 %all-to-all-start = ((f32[32,8,128]{2,1,0:T(8,128)}), f32[32,8,128]{2,1,0:T(8,128)S(1)}, u32[]{:S(2)}, u32[]{:S(2)}) async-start(f32[32,8,128]{2,1,0:T(8,128)} %shard_map.113), calls=%async_computation | async-start | bytes 262144 | tf_op jit(solution)/shard_map/all_to_all | solution.py:452
  10.3 3.6 %collective-permute-start.2 = (f32[2,128,128]{2,1,0:T(8,128)S(1)}, f32[2,128,128]{2,1,0:T(8,128)S(1)}, u32[]{:S(2)}, u32[]{:S(2)}) collective-permute-start(f32[2,128,128]{2,1,0:T(8,128)S(1)} %bitcast.39), channel_id=1, source_target_pairs={{0,1},{1,0},{2,3},{3,2},{4,5},{5,4},{6,7},{7,6},{8,9},{9,8},{10,11... | collective-permute-start | bytes 393224 | tf_op jit(solution)/shard_map/ppermute | solution.py:434
  12.1 0.7 copy-start
  12.1 4.4 %collective-permute-start = (f32[40,256]{1,0:T(8,128)S(1)}, f32[40,256]{1,0:T(8,128)S(1)}, u32[]{:S(2)}, u32[]{:S(2)}) collective-permute-start(f32[40,256]{1,0:T(8,128)S(1)} %get-tuple-element.39.p_own), channel_id=1, source_target_pairs={{0,1},{1,0},{2,3},{3,2},{4,5},{5,4},{6,7},{7,6},{8,9},{9,8},{10,11... | collective-permute-start | bytes 122888 | tf_op jit(solution)/shard_map/ppermute | solution.py:434
  12.8 1.2 %collective-permute-start.3 = (f32[1,256]{1,0:T(1,128)S(1)}, f32[1,256]{1,0:T(1,128)S(1)}, u32[]{:S(2)}, u32[]{:S(2)}) collective-permute-start(f32[1,256]{1,0:T(1,128)S(1)} %copy-done), channel_id=1, source_target_pairs={{0,1},{1,0},{2,3},{3,2},{4,5},{5,4},{6,7},{7,6},{8,9},{9,8},{10,11... | collective-permute-start | bytes 3080 | tf_op jit(solution)/shard_map/ppermute | solution.py:434
  14.0 0.8 %copy-start.1 = (f32[256,512]{1,0:T(8,128)}, f32[256,512]{1,0:T(8,128)S(1)}, u32[]{:S(2)}) copy-start(f32[256,512]{1,0:T(8,128)S(1)} %collective-permute-done.1.w_other) | copy-start | bytes 1572868
  20.2 4.3 %collective-permute-start.4 = (f32[32,512]{1,0:T(8,128)S(1)}, f32[32,512]{1,0:T(8,128)S(1)}, u32[]{:S(2)}, u32[]{:S(2)}) collective-permute-start(f32[32,512]{1,0:T(8,128)S(1)} %get-tuple-element.46), channel_id=1, source_target_pairs={{0,8},{1,3},{2,10},{3,1},{4,12},{5,7},{6,14},{7,5},{8,0},{9,11},{1... | collective-permute-start | bytes 196616 | tf_op jit(solution)/shard_map/ppermute | solution.py:442
  24.5 4.4 %collective-permute-start.5 = (f32[32,512]{1,0:T(8,128)S(1)}, f32[32,512]{1,0:T(8,128)S(1)}, u32[]{:S(2)}, u32[]{:S(2)}) collective-permute-start(f32[32,512]{1,0:T(8,128)S(1)} %add.21.own), channel_id=1, source_target_pairs={{0,8},{1,5},{2,10},{3,7},{4,12},{5,1},{6,14},{7,3},{8,0},{9,13},{1... | collective-permute-start | bytes 196616 | tf_op jit(solution)/shard_map/ppermute | solution.py:442
  25.4 10.6 %all-to-all-start.1 = ((f32[32,1,128]{2,1,0:T(1,128)}), f32[32,1,128]{2,1,0:T(1,128)S(1)}, u32[]{:S(2)}, u32[]{:S(2)}) async-start(f32[32,1,128]{2,1,0:T(1,128)} %bitcast.9), calls=%async_computation.1 | async-start | bytes 32768 | tf_op jit(solution)/shard_map/all_to_all | solution.py:452
  37.6 4.3 %collective-permute-start.8 = (f32[64,256]{1,0:T(8,128)S(1)}, f32[64,256]{1,0:T(8,128)S(1)}, u32[]{:S(2)}, u32[]{:S(2)}) collective-permute-start(f32[64,256]{1,0:T(8,128)S(1)} %get-tuple-element.58), channel_id=1, source_target_pairs={{0,2},{1,9},{2,0},{3,11},{4,6},{5,13},{6,4},{7,15},{8,10},{9,1},{1... | collective-permute-start | bytes 196616 | tf_op jit(solution)/shard_map/ppermute | solution.py:442
  38.2 6.9 %collective-permute-start.6 = (f32[32,512]{1,0:T(8,128)S(1)}, f32[32,512]{1,0:T(8,128)S(1)}, u32[]{:S(2)}, u32[]{:S(2)}) collective-permute-start(f32[32,512]{1,0:T(8,128)S(1)} %get-tuple-element.53), channel_id=1, source_target_pairs={{0,8},{1,3},{2,10},{3,1},{4,12},{5,7},{6,14},{7,5},{8,0},{9,11},{1... | collective-permute-start | bytes 196616 | tf_op jit(solution)/shard_map/ppermute | solution.py:442
  42.0 5.1 %collective-permute-start.9 = (f32[64,256]{1,0:T(8,128)S(1)}, f32[64,256]{1,0:T(8,128)S(1)}, u32[]{:S(2)}, u32[]{:S(2)}) collective-permute-start(f32[64,256]{1,0:T(8,128)S(1)} %multiply_add_fusion.1), channel_id=1, source_target_pairs={{0,2},{1,17},{2,0},{3,19},{4,6},{5,21},{6,4},{7,23},{8,10},{9,25},... | collective-permute-start | bytes 196616 | tf_op jit(solution)/shard_map/ppermute | solution.py:442
  42.6 9.8 %all-to-all-start.2 = ((f32[32,1,128]{2,1,0:T(1,128)}), f32[32,1,128]{2,1,0:T(1,128)S(1)}, u32[]{:S(2)}, u32[]{:S(2)}) async-start(f32[32,1,128]{2,1,0:T(1,128)} %bitcast.12), calls=%async_computation.2 | async-start | bytes 32768 | tf_op jit(solution)/shard_map/all_to_all | solution.py:452
  45.2 4.4 %collective-permute-start.7 = (f32[32,512]{1,0:T(8,128)S(1)}, f32[32,512]{1,0:T(8,128)S(1)}, u32[]{:S(2)}, u32[]{:S(2)}) collective-permute-start(f32[32,512]{1,0:T(8,128)S(1)} %add.22.own), channel_id=1, source_target_pairs={{0,8},{1,5},{2,10},{3,7},{4,12},{5,1},{6,14},{7,3},{8,0},{9,13},{1... | collective-permute-start | bytes 196616 | tf_op jit(solution)/shard_map/ppermute | solution.py:442
  53.9 4.3 %collective-permute-start.10 = (f32[32,512]{1,0:T(8,128)S(1)}, f32[32,512]{1,0:T(8,128)S(1)}, u32[]{:S(2)}, u32[]{:S(2)}) collective-permute-start(f32[32,512]{1,0:T(8,128)S(1)} %get-tuple-element.60), channel_id=1, source_target_pairs={{0,8},{1,3},{2,10},{3,1},{4,12},{5,7},{6,14},{7,5},{8,0},{9,11},{1... | collective-permute-start | bytes 196616 | tf_op jit(solution)/shard_map/ppermute | solution.py:442
  58.3 4.3 %collective-permute-start.11 = (f32[32,512]{1,0:T(8,128)S(1)}, f32[32,512]{1,0:T(8,128)S(1)}, u32[]{:S(2)}, u32[]{:S(2)}) collective-permute-start(f32[32,512]{1,0:T(8,128)S(1)} %add.25.own), channel_id=1, source_target_pairs={{0,8},{1,5},{2,10},{3,7},{4,12},{5,1},{6,14},{7,3},{8,0},{9,13},{1... | collective-permute-start | bytes 196616 | tf_op jit(solution)/shard_map/ppermute | solution.py:442
  58.9 10.4 %all-to-all-start.3 = ((f32[32,1,128]{2,1,0:T(1,128)}), f32[32,1,128]{2,1,0:T(1,128)S(1)}, u32[]{:S(2)}, u32[]{:S(2)}) async-start(f32[32,1,128]{2,1,0:T(1,128)} %bitcast.19), calls=%async_computation.3 | async-start | bytes 32768 | tf_op jit(solution)/shard_map/all_to_all | solution.py:452
  70.3 8.9 %collective-permute-start.12 = (f32[64,256]{1,0:T(8,128)S(1)}, f32[64,256]{1,0:T(8,128)S(1)}, u32[]{:S(2)}, u32[]{:S(2)}) collective-permute-start(f32[64,256]{1,0:T(8,128)S(1)} %get-tuple-element.70), channel_id=1, source_target_pairs={{0,1},{1,0},{2,3},{3,2},{4,5},{5,4},{6,7},{7,6},{8,9},{9,8},{10,11... | collective-permute-start | bytes 196616 | tf_op jit(solution)/shard_map/ppermute | solution.py:434

commit v5 on v4

--- a/solution.py
+++ b/solution.py
@@ -63,9 +63,8 @@
     plan = [(0, 1)]
     span = 2
     while span < steps:
-        wide = 2
-        plan.append(tuple(span * i for i in range(1, wide)))
-        span *= wide
+        plan.append((span,))
+        span *= 2
     return plan
 
 
@@ -93,15 +92,17 @@
 def first_kernel(initial, weight, tap, att, msg, b_initial, b_weight, b_tap, b_att, sems):
     nodes = initial.shape[1]
     channels = tap.shape[1]
-    for copy in land([(weight, b_weight), (initial, b_initial), (tap, b_tap), (att, b_att)], sems):
+    copies = land([(initial, b_initial), (tap, b_tap), (att, b_att), (weight, b_weight)], sems)
+    for copy in copies[:3]:
         copy.wait()
     start = b_initial[...]
+    node = lax.broadcasted_iota(jnp.int32, (nodes, channels), 0)
+    taps = fdot(start, (node == b_tap[...]).astype(F32))
+    copies[3].wait()
     net = fdot(start, b_weight[...])
     rows = []
     for j in range(0, net.shape[1], LANES):
         rows.append(net[:, j : j + LANES])
-    node = lax.broadcasted_iota(jnp.int32, (nodes, channels), 0)
-    taps = fdot(start, (node == b_tap[...]).astype(F32))
     for row in (taps, b_att[...]):
         for j in range(0, channels, LANES):
             rows.append(row[:, j : j + LANES])
@@ -174,7 +175,8 @@
         todo.append(made[p])
     for i, value in enumerate(todo):
         for b in every:
-            ah[i, b], al[i, b] = value[b]
+            here = slice(i * width, (i + 1) * width)
+            ah[b, here, :], al[b, here, :] = value[b]
     for copy in copies:
         copy.wait()
     for half in range(2):
@@ -185,20 +187,20 @@
 
 
 def march(plan, x, ah, al):
-    blocks, width = ah.shape[1], ah.shape[2]
+    blocks, width = ah.shape[0], ah.shape[2]
     rows = x.shape[0]
     unit = 0
     for s, stage in enumerate(plan):
-        sums = [None] * blocks
-        for offset in stage:
-            xh, xl = split(lag(x, offset))
-            pair = jnp.concatenate([xh, xl], axis=0)
-            for b in range(blocks):
-                here = slice(b * width, (b + 1) * width)
-                two = bdot(pair[:, here], ah[unit, b])
-                part = two[:rows] + two[rows:] + bdot(xh[:, here], al[unit, b])
-                sums[b] = part if sums[b] is None else sums[b] + part
-            unit += 1
+        parts = [split(lag(x, offset)) for offset in stage]
+        there = slice(unit * width, (unit + len(stage)) * width)
+        unit += len(stage)
+        sums = []
+        for b in range(blocks):
+            here = slice(b * width, (b + 1) * width)
+            xh = jnp.concatenate([h[:, here] for h, _ in parts], axis=1)
+            xl = jnp.concatenate([l[:, here] for _, l in parts], axis=1)
+            two = bdot(jnp.concatenate([xh, xl], axis=0), ah[b, there, :])
+            sums.append(two[:rows] + two[rows:] + bdot(xh, al[b, there, :]))
         total = jnp.concatenate(sums, axis=1)
         x = total if s == 0 else total + x
     return x
@@ -209,23 +211,35 @@
     msg[...] = jnp.broadcast_to(row, msg.shape)
 
 
-def finish_round(plan, r, spot, c_ref, p_ref, msg, ah, al, sent, th, tl):
+def finish_round(plan, r, spot, r_ref, c_ref, p_ref, msg, ah, al, sent, th, tl, more=None):
     near_msg, sem = sent
+    r_ref[...] = r
     send_squares(r, spot, near_msg)
     leaving = pltpu.make_async_copy(near_msg, msg, sem.at[0])
     leaving.start()
-    c = march(plan, r, ah, al)
-    c_ref[...] = c
-    rows = c.shape[0]
-    ch, cl = split(c)
-    two = tdot(jnp.concatenate([ch, cl], axis=0), th[...])
-    p_ref[...] = two[:rows] + two[rows:] + tdot(ch, tl[...])
+    owner = jnp.max(spot[2:3, :]) > 0.5
+
+    @pl.when(owner)
+    def _():
+        c = march(plan, r_ref[...], ah, al)
+        c_ref[...] = c
+        rows = c.shape[0]
+        ch, cl = split(c)
+        two = tdot(jnp.concatenate([ch, cl], axis=0), th[...])
+        p_ref[...] = two[:rows] + two[rows:] + tdot(ch, tl[...])
+        if more is not None:
+            more(c)
+
+    @pl.when(jnp.logical_not(owner))
+    def _():
+        c_ref[...] = jnp.zeros_like(c_ref)
+        p_ref[...] = jnp.zeros_like(p_ref)
+
     leaving.wait()
-    return c
 
 
 def opening_kernel(plan, steps, channels, sections, doms, levels, spot, got, p_other, p_own, ah, al, th, tl,
-                   w_ref, q_ref, r_ref, c_ref, p_ref, msg, aux_ref, *sent):
+                   w_ref, r_ref, c_ref, p_ref, msg, aux_ref, *sent):
     my, chip = spot[0:1, :], spot[1:2, :]
     nets = th.shape[0]
     net_rows = nets // LANES
@@ -289,9 +303,7 @@
     q = (held + back - inj) - both(p_other, p_own, 0, steps)
     r = q + 0.5 * jnp.tanh(start)
     w_ref[...] = jnp.broadcast_to(start, w_ref.shape)
-    q_ref[...] = q
-    r_ref[...] = r
-    finish_round(plan, r, spot, c_ref, p_ref, msg, ah, al, sent, th, tl)
+    finish_round(plan, r, spot, r_ref, c_ref, p_ref, msg, ah, al, sent, th, tl)
 
 
 def chosen(index, nodes):
@@ -321,43 +333,48 @@
     u_ref[...] = r0[...] + dot3(own[...] + recv[...], th[...], tl[...])
 
 
-def advance(got, u, w0, q0, c0, cells, mean_ref):
+def advance(got, u, w0, r0, c0, cells, mean_ref):
     mean, damp = damping_of(got, cells)
     mean_ref[...] = jnp.broadcast_to(mean, mean_ref.shape)
-    return w0[...] - damp * c0[...], q0[...] - damp * u[...], damp
+    q0 = r0[...] - 0.5 * jnp.tanh(w0[...])
+    return w0[...] - damp * c0[...], q0 - damp * u[...], damp
 
 
 def round_kernel(plan, steps, channels, cells, mode, *refs):
     refs = list(refs)
     take = lambda n: [refs.pop(0) for _ in range(n)]
-    (spot, got, u, w0, q0, c0, ah, al, th, tl, aux) = take(11)
+    (spot, got, u, w0, r0, c0, ah, al, th, tl, aux) = take(11)
     if mode == "drive":
         (pre,) = take(1)
-    w_ref, q_ref, r_ref, c_ref, p_ref, msg, mean_ref = take(7)
+    w_ref, r_ref, c_ref, p_ref, msg, mean_ref = take(6)
     if mode == "taps":
         (tt_ref,) = take(1)
     sent = take(2)
-    w, q, damp = advance(got, u, w0, q0, c0, cells, mean_ref)
+    w, q, damp = advance(got, u, w0, r0, c0, cells, mean_ref)
     if mode == "drive":
         drive = pre[0:steps, :] - damp * pre[steps : 2 * steps, :]
         gain, _, driven = (aux[i : i + 1, 0 : 2 * channels] for i in (1, 2, 3))
         q = q - (spread(drive * gain, driven, w.shape[1] // 2) - aux[0:1, 0 : w.shape[1]])
     r = q + 0.5 * jnp.tanh(w)
     w_ref[...] = w
-    q_ref[...] = q
-    r_ref[...] = r
-    c = finish_round(plan, r, spot, c_ref, p_ref, msg, ah, al, sent, th, tl)
-    if mode == "taps":
-        half = w.shape[1] // 2
+    half = w.shape[1] // 2
+
+    def tap(c):
         for h in range(2):
             here = slice(h * half, (h + 1) * half)
             there = slice(h * channels, (h + 1) * channels)
             tapped = chosen(aux[2:3, there], half)
-            tt_ref[:, there] = dot2(jnp.concatenate([w[:, here], c[:, here]], axis=0), tapped)
-
-
-def residual_kernel(cells, spot, got, u, w0, q0, c0, w_ref, r_ref, msg, mean_ref):
-    w, q, _ = advance(got, u, w0, q0, c0, cells, mean_ref)
+            tt_ref[:, there] = dot2(jnp.concatenate([w_ref[:, here], c[:, here]], axis=0), tapped)
+
+    more = None
+    if mode == "taps":
+        more = tap
+        tt_ref[...] = jnp.zeros_like(tt_ref)
+    finish_round(plan, r, spot, r_ref, c_ref, p_ref, msg, ah, al, sent, th, tl, more)
+
+
+def residual_kernel(cells, spot, got, u, w0, r0, c0, w_ref, r_ref, msg, mean_ref):
+    w, q, _ = advance(got, u, w0, r0, c0, cells, mean_ref)
     r = q + 0.5 * jnp.tanh(w)
     w_ref[...] = w
     r_ref[...] = r
@@ -482,7 +499,7 @@
         ],
     )
     p_other = swap(pack)
-    cut = ((units, 2 * blocks, width, width), BF16)
+    cut = ((2 * blocks, units * width, width), BF16)
     up = ((nets, wide), BF16)
     th, tl, ah, al = call(
         functools.partial(prep_kernel, plan),
@@ -493,14 +510,14 @@
             pltpu.VMEM((2, nodes, nets), F32), pltpu.SemaphoreType.DMA((2,)),
         ],
     )
-    state = [((steps, wide), F32)] * 4
+    state = [((steps, wide), F32)] * 3
     landing = [pltpu.VMEM(*message), pltpu.SemaphoreType.DMA((1,))]
     aux_shape = (-(-(4 + 3 * levels) // SUB) * SUB, max(wide, 2 * channels))
-    w, q, r, c, part, msg, aux = call(
+    w, r, c, part, msg, aux = call(
         functools.partial(opening_kernel, plan, steps, channels, sections, doms, levels),
         state + [((steps, nets), F32), message, (aux_shape, F32)],
         spot, got, p_other, pack, ah, al, th, tl,
-        hbm_outs=(5,),
+        hbm_outs=(4,),
         scratch=landing,
     )
     means = []
@@ -537,18 +554,18 @@
         result = call(
             functools.partial(round_kernel, plan, steps, channels, cells, mode),
             outs,
-            spot, got, u, w, q, c, ah, al, th, tl, aux, *extra,
-            hbm_outs=(5,),
+            spot, got, u, w, r, c, ah, al, th, tl, aux, *extra,
+            hbm_outs=(4,),
             scratch=landing,
         )
-        w, q, r, c, part, msg, mean = result[:7]
+        w, r, c, part, msg, mean = result[:6]
         means.append(mean)
         if mode == "taps":
-            taps = result[7]
+            taps = result[6]
     w, r, msg, mean = call(
         functools.partial(residual_kernel, cells),
         [((steps, wide), F32), ((steps, wide), F32), message, ((1, LANES), F32)],
-        spot, got, u, w, q, c,
+        spot, got, u, w, r, c,
     )
     means.append(mean)
     got = gather(msg)

time: 80.2 us -> 78.4 us (0.978)
  Pallas kernels: 12.6 us -> 10.3 us
    pallas_call x12, Pallas kernels: 12.6 us -> 10.3 us  [call(): pl.pallas_call(kernel, out_shape=[pltpu.HBM(s, d) if i in hbm_outs else j...]
where the time goes in v5:
time: 78.4 us; the launch traced here: 78.1 us
  waiting for transfers between devices  32.1 us (41%)
  starting transfers between devices  24.5 us (31%)
  Pallas kernels  10.3 us (13%)
  blocking collectives  8.87 us (11%)
  local copies, waits for them, and re-layouts  1.32 us (2%)
  between operations  0.81 us (1%)
    all_to_all x4, waiting for transfers between devices, gather(): lax.all_to_all(spread_out, everywhere, 0, 0, tiled=False).reshape(msg.shape)  17.7 us
    all_to_all x4, starting transfers between devices, gather(): lax.all_to_all(spread_out, everywhere, 0, 0, tiled=False).reshape(msg.shape)  16.3 us
    ppermute x8, waiting for transfers between devices, pair(): return lax.ppermute(x, everywhere, links)  13.6 us
    pallas_call x12, Pallas kernels, call(): pl.pallas_call(kernel, out_shape=[pltpu.HBM(s, d) if i in hbm_outs else j...  10.3 us
    all_to_all x1, blocking collectives, gather(): lax.all_to_all(spread_out, everywhere, 0, 0, tiled=False).reshape(msg.shape)  8.87 us
    ppermute x8, starting transfers between devices, pair(): return lax.ppermute(x, everywhere, links)  6.72 us
  transfers between devices with their start and end apart: 17, of which 10 were waited for; matrix products, arithmetic and copies ran while one was open for 0% of the time, Pallas kernels for 8%

profile of v5, /device:TPU:0, one launch (start us, length us, event | category | flops | bytes accessed | tf_op | source)
XLA Modules:
  0.0 78.1 jit_solution(16572932448863380421)
XLA Ops:
  1.2 2.1 %shard_map.113 = f32[32,8,128]{2,1,0:T(8,128)} custom-call(f32[1,256]{1,0:T(1,128)} %initial.3, f32[256,512]{1,0:T(8,128)} %bitcast.35, s32[1,128]{1,0:T(1,128)} %tap.3, f32[1,128]{1,0:T(1,128)} %att.1), custom_call_target="tpu_custom_call" | custom-call | tf_op jit(solution)/shard_map/pallas_call | solution.py:411
  3.4 7.0 %all-to-all-start = ((f32[32,8,128]{2,1,0:T(8,128)}), f32[32,8,128]{2,1,0:T(8,128)S(1)}, u32[]{:S(2)}, u32[]{:S(2)}) async-start(f32[32,8,128]{2,1,0:T(8,128)} %shard_map.113), calls=%async_computation | async-start | bytes 262144 | tf_op jit(solution)/shard_map/all_to_all | solution.py:469
  10.6 1.5 %shard_map.114 = (f32[40,256]{1,0:T(8,128)S(1)}, f32[2,128,128]{2,1,0:T(8,128)S(1)}) custom-call(f32[32,256]{1,0:T(8,128)} %bitcast.40, f32[1,256]{1,0:T(1,128)} %initial.3, f32[1,256]{1,0:T(1,128)} %cap_own.1, f32[2,128,128]{2,1,0:T(8,128)} %bitcast.37, s32[1,128]{1,0:T(1,128)} %tap.3, s32[1,128]{1,0:T(1,128)} %drive.1, f32[1,128]{1,0:T(1,128)} %gain.1, ...), custom_call_target="tpu_custom_call" | custom-call | tf_op jit(solution)/shard_map/pallas_call | solution.py:411
  13.1 0.8 %collective-permute-done.3.cap_other = f32[1,256]{1,0:T(1,128)S(1)} collective-permute-done((f32[1,256]{1,0:T(1,128)S(1)}, f32[1,256]{1,0:T(1,128)S(1)}, u32[]{:S(2)}, u32[]{:S(2)}) %collective-permute-start.3) | collective-permute-done | bytes 1056 | tf_op jit(solution)/shard_map/ppermute | solution.py:451
  14.0 0.8 %copy-done.1 = f32[256,512]{1,0:T(8,128)} copy-done((f32[256,512]{1,0:T(8,128)}, f32[256,512]{1,0:T(8,128)S(1)}, u32[]{:S(2)}) %copy-start.1) | copy-done | bytes 524312
  14.8 1.7 %shard_map.115 = (bf16[512,512]{1,0:T(8,128)(2,1)S(1)}, bf16[512,512]{1,0:T(8,128)(2,1)S(1)}, bf16[4,768,128]{2,1,0:T(8,128)(2,1)S(1)}, bf16[4,768,128]{2,1,0:T(8,128)(2,1)S(1)}) custom-call(f32[256,512]{1,0:T(8,128)} %copy-done.1, f32[256,512]{1,0:T(8,128)} %bitcast.36, f32[2,128,128]{2,1,0:T(8,128)S(1)} %collective-permute-done.2.i_other, ...), custom_call_target="tpu_custom_call" | custom-call | tf_op jit(solution)/shard_map/pallas_call | solution.py:411
  16.5 2.0 %all-to-all-done.got = f32[32,8,128]{2,1,0:T(8,128)S(1)} async-done(((f32[32,8,128]{2,1,0:T(8,128)}), f32[32,8,128]{2,1,0:T(8,128)S(1)}, u32[]{:S(2)}, u32[]{:S(2)}) %all-to-all-start) | async-done | bytes 131104 | tf_op jit(solution)/shard_map/all_to_all | solution.py:469
  18.5 0.9 %shard_map.116 = (f32[32,512]{1,0:T(8,128)S(1)}, f32[32,512]{1,0:T(8,128)S(1)}, f32[32,512]{1,0:T(8,128)S(1)}, f32[32,512]{1,0:T(8,128)S(1)}, f32[32,128]{1,0:T(8,128)}, /*index=5*/f32[16,512]{1,0:T(8,128)S(1)}) custom-call(f32[8,128]{1,0:T(8,128)S(1)} %broadcast_in_dim.4.spot.refs_0_, f32[32,8,128]{2,1,0:T(8,128)S(1)} %all-to-all-done.got, ...), custom_call_target="tpu_custom_call" | custom-call | tf_op jit(solution)/shard_map/pallas_call | solution.py:411
  19.5 0.9 %collective-permute-start.4 = (f32[32,512]{1,0:T(8,128)S(1)}, f32[32,512]{1,0:T(8,128)S(1)}, u32[]{:S(2)}, u32[]{:S(2)}) collective-permute-start(f32[32,512]{1,0:T(8,128)S(1)} %get-tuple-element.43), channel_id=1, source_target_pairs={{0,8},{1,3},{2,10},{3,1},{4,12},{5,7},{6,14},{7,5},{8,0},{9,11},{1... | collective-permute-start | bytes 196616 | tf_op jit(solution)/shard_map/ppermute | solution.py:459
  20.4 3.5 %collective-permute-done.4 = f32[32,512]{1,0:T(8,128)S(1)} collective-permute-done((f32[32,512]{1,0:T(8,128)S(1)}, f32[32,512]{1,0:T(8,128)S(1)}, u32[]{:S(2)}, u32[]{:S(2)}) %collective-permute-start.4) | collective-permute-done | bytes 65568 | tf_op jit(solution)/shard_map/ppermute | solution.py:459
  23.8 0.9 %collective-permute-start.5 = (f32[32,512]{1,0:T(8,128)S(1)}, f32[32,512]{1,0:T(8,128)S(1)}, u32[]{:S(2)}, u32[]{:S(2)}) collective-permute-start(f32[32,512]{1,0:T(8,128)S(1)} %add.21.own), channel_id=1, source_target_pairs={{0,8},{1,5},{2,10},{3,7},{4,12},{5,1},{6,14},{7,3},{8,0},{9,13},{1... | collective-permute-start | bytes 196616 | tf_op jit(solution)/shard_map/ppermute | solution.py:459
  24.7 3.5 %all-to-all-start.1 = ((f32[32,1,128]{2,1,0:T(1,128)}), f32[32,1,128]{2,1,0:T(1,128)S(1)}, u32[]{:S(2)}, u32[]{:S(2)}) async-start(f32[32,1,128]{2,1,0:T(1,128)} %bitcast.9), calls=%async_computation.1 | async-start | bytes 32768 | tf_op jit(solution)/shard_map/all_to_all | solution.py:469
  28.6 6.8 %all-to-all-done.1 = f32[32,1,128]{2,1,0:T(1,128)S(1)} async-done(((f32[32,1,128]{2,1,0:T(1,128)}), f32[32,1,128]{2,1,0:T(1,128)S(1)}, u32[]{:S(2)}, u32[]{:S(2)}) %all-to-all-start.1) | async-done | bytes 16416 | tf_op jit(solution)/shard_map/all_to_all | solution.py:469
  35.4 0.8 shard_map.118
  37.3 3.5 %collective-permute-done.8 = f32[64,256]{1,0:T(8,128)S(1)} collective-permute-done((f32[64,256]{1,0:T(8,128)S(1)}, f32[64,256]{1,0:T(8,128)S(1)}, u32[]{:S(2)}, u32[]{:S(2)}) %collective-permute-start.8) | collective-permute-done | bytes 65568 | tf_op jit(solution)/shard_map/ppermute | solution.py:459
  41.5 2.5 %all-to-all-start.2 = ((f32[32,1,128]{2,1,0:T(1,128)}), f32[32,1,128]{2,1,0:T(1,128)S(1)}, u32[]{:S(2)}, u32[]{:S(2)}) async-start(f32[32,1,128]{2,1,0:T(1,128)} %bitcast.12), calls=%async_computation.2 | async-start | bytes 32768 | tf_op jit(solution)/shard_map/all_to_all | solution.py:469
  44.1 1.7 %collective-permute-start.7 = (f32[32,512]{1,0:T(8,128)S(1)}, f32[32,512]{1,0:T(8,128)S(1)}, u32[]{:S(2)}, u32[]{:S(2)}) collective-permute-start(f32[32,512]{1,0:T(8,128)S(1)} %add.22.own), channel_id=1, source_target_pairs={{0,8},{1,5},{2,10},{3,7},{4,12},{5,1},{6,14},{7,3},{8,0},{9,13},{1... | collective-permute-start | bytes 196616 | tf_op jit(solution)/shard_map/ppermute | solution.py:459
  45.8 2.6 %collective-permute-done.7.recv = f32[32,512]{1,0:T(8,128)S(1)} collective-permute-done((f32[32,512]{1,0:T(8,128)S(1)}, f32[32,512]{1,0:T(8,128)S(1)}, u32[]{:S(2)}, u32[]{:S(2)}) %collective-permute-start.7) | collective-permute-done | bytes 65568 | tf_op jit(solution)/shard_map/ppermute | solution.py:459
  48.7 2.5 %all-to-all-done.2 = f32[32,1,128]{2,1,0:T(1,128)S(1)} async-done(((f32[32,1,128]{2,1,0:T(1,128)}), f32[32,1,128]{2,1,0:T(1,128)S(1)}, u32[]{:S(2)}, u32[]{:S(2)}) %all-to-all-start.2) | async-done | bytes 16416 | tf_op jit(solution)/shard_map/all_to_all | solution.py:469
  51.2 0.9 %shard_map.120 = (f32[32,512]{1,0:T(8,128)S(1)}, f32[32,512]{1,0:T(8,128)S(1)}, f32[32,512]{1,0:T(8,128)S(1)}, f32[32,512]{1,0:T(8,128)S(1)}, f32[32,128]{1,0:T(8,128)}, /*index=5*/f32[1,128]{1,0:T(1,128)S(1)}) custom-call(f32[8,128]{1,0:T(8,128)S(1)} %broadcast_in_dim.4.spot.refs_0_, f32[32,128]{1,0:T(8,128)S(1)} %bitcast.29, ...), custom_call_target="tpu_custom_call" | custom-call | tf_op jit(solution)/shard_map/pallas_call | solution.py:411
  52.8 3.7 %collective-permute-done.10 = f32[32,512]{1,0:T(8,128)S(1)} collective-permute-done((f32[32,512]{1,0:T(8,128)S(1)}, f32[32,512]{1,0:T(8,128)S(1)}, u32[]{:S(2)}, u32[]{:S(2)}) %collective-permute-start.10) | collective-permute-done | bytes 65568 | tf_op jit(solution)/shard_map/ppermute | solution.py:459
  57.2 3.3 %all-to-all-start.3 = ((f32[32,1,128]{2,1,0:T(1,128)}), f32[32,1,128]{2,1,0:T(1,128)S(1)}, u32[]{:S(2)}, u32[]{:S(2)}) async-start(f32[32,1,128]{2,1,0:T(1,128)} %bitcast.19), calls=%async_computation.3 | async-start | bytes 32768 | tf_op jit(solution)/shard_map/all_to_all | solution.py:469
  61.1 6.5 %all-to-all-done.3 = f32[32,1,128]{2,1,0:T(1,128)S(1)} async-done(((f32[32,1,128]{2,1,0:T(1,128)}), f32[32,1,128]{2,1,0:T(1,128)S(1)}, u32[]{:S(2)}, u32[]{:S(2)}) %all-to-all-start.3) | async-done | bytes 16416 | tf_op jit(solution)/shard_map/all_to_all | solution.py:469
  68.5 8.9 %all_to_all.25 = f32[32,1,128]{2,1,0:T(1,128)S(1)} all-to-all(f32[32,1,128]{2,1,0:T(1,128)S(1)} %bitcast.33), channel_id=1, replica_groups=mesh['section'=4,'dom'=8] {'section','dom'}, dimensions={0} | all-to-all | bytes 32768 | tf_op jit(solution)/shard_map/all_to_all | solution.py:469
  (38 shorter events, 8.2 us)
Async XLA Ops:
  0.6 13.3 %collective-permute-start.1 = (f32[256,512]{1,0:T(8,128)}, f32[256,512]{1,0:T(8,128)S(1)}, u32[]{:S(2)}, u32[]{:S(2)}) collective-permute-start(f32[256,512]{1,0:T(8,128)} %bitcast.34), channel_id=1, source_target_pairs={{0,1},{1,0},{2,3},{3,2},{4,5},{5,4},{6,7},{7,6},{8,9},{9,8},{10,11... | collective-permute-start | bytes 1572872 | tf_op jit(solution)/shard_map/ppermute | solution.py:451
  3.3 7.0 %copy-start.2 = (f32[1,2,128,128]{3,2,1,0:T(8,128)S(1)}, f32[1,2,128,128]{3,2,1,0:T(8,128)}, u32[]{:S(2)}) copy-start(f32[1,2,128,128]{3,2,1,0:T(8,128)} %param.14) | copy-start | bytes 393220
  3.4 15.1 %all-to-all-start = ((f32[32,8,128]{2,1,0:T(8,128)}), f32[32,8,128]{2,1,0:T(8,128)S(1)}, u32[]{:S(2)}, u32[]{:S(2)}) async-start(f32[32,8,128]{2,1,0:T(8,128)} %shard_map.113), calls=%async_computation | async-start | bytes 262144 | tf_op jit(solution)/shard_map/all_to_all | solution.py:469
  10.3 3.6 %collective-permute-start.2 = (f32[2,128,128]{2,1,0:T(8,128)S(1)}, f32[2,128,128]{2,1,0:T(8,128)S(1)}, u32[]{:S(2)}, u32[]{:S(2)}) collective-permute-start(f32[2,128,128]{2,1,0:T(8,128)S(1)} %bitcast.39), channel_id=1, source_target_pairs={{0,1},{1,0},{2,3},{3,2},{4,5},{5,4},{6,7},{7,6},{8,9},{9,8},{10,11... | collective-permute-start | bytes 393224 | tf_op jit(solution)/shard_map/ppermute | solution.py:451
  12.1 0.7 copy-start
  12.1 4.4 %collective-permute-start = (f32[40,256]{1,0:T(8,128)S(1)}, f32[40,256]{1,0:T(8,128)S(1)}, u32[]{:S(2)}, u32[]{:S(2)}) collective-permute-start(f32[40,256]{1,0:T(8,128)S(1)} %get-tuple-element.36.p_own), channel_id=1, source_target_pairs={{0,1},{1,0},{2,3},{3,2},{4,5},{5,4},{6,7},{7,6},{8,9},{9,8},{10,11... | collective-permute-start | bytes 122888 | tf_op jit(solution)/shard_map/ppermute | solution.py:451
  12.8 1.2 %collective-permute-start.3 = (f32[1,256]{1,0:T(1,128)S(1)}, f32[1,256]{1,0:T(1,128)S(1)}, u32[]{:S(2)}, u32[]{:S(2)}) collective-permute-start(f32[1,256]{1,0:T(1,128)S(1)} %copy-done), channel_id=1, source_target_pairs={{0,1},{1,0},{2,3},{3,2},{4,5},{5,4},{6,7},{7,6},{8,9},{9,8},{10,11... | collective-permute-start | bytes 3080 | tf_op jit(solution)/shard_map/ppermute | solution.py:451
  14.0 0.8 %copy-start.1 = (f32[256,512]{1,0:T(8,128)}, f32[256,512]{1,0:T(8,128)S(1)}, u32[]{:S(2)}) copy-start(f32[256,512]{1,0:T(8,128)S(1)} %collective-permute-done.1.w_other) | copy-start | bytes 1572868
  19.5 4.3 %collective-permute-start.4 = (f32[32,512]{1,0:T(8,128)S(1)}, f32[32,512]{1,0:T(8,128)S(1)}, u32[]{:S(2)}, u32[]{:S(2)}) collective-permute-start(f32[32,512]{1,0:T(8,128)S(1)} %get-tuple-element.43), channel_id=1, source_target_pairs={{0,8},{1,3},{2,10},{3,1},{4,12},{5,7},{6,14},{7,5},{8,0},{9,11},{1... | collective-permute-start | bytes 196616 | tf_op jit(solution)/shard_map/ppermute | solution.py:459
  23.8 4.4 %collective-permute-start.5 = (f32[32,512]{1,0:T(8,128)S(1)}, f32[32,512]{1,0:T(8,128)S(1)}, u32[]{:S(2)}, u32[]{:S(2)}) collective-permute-start(f32[32,512]{1,0:T(8,128)S(1)} %add.21.own), channel_id=1, source_target_pairs={{0,8},{1,5},{2,10},{3,7},{4,12},{5,1},{6,14},{7,3},{8,0},{9,13},{1... | collective-permute-start | bytes 196616 | tf_op jit(solution)/shard_map/ppermute | solution.py:459
  24.7 10.6 %all-to-all-start.1 = ((f32[32,1,128]{2,1,0:T(1,128)}), f32[32,1,128]{2,1,0:T(1,128)S(1)}, u32[]{:S(2)}, u32[]{:S(2)}) async-start(f32[32,1,128]{2,1,0:T(1,128)} %bitcast.9), calls=%async_computation.1 | async-start | bytes 32768 | tf_op jit(solution)/shard_map/all_to_all | solution.py:469
  36.1 4.6 %collective-permute-start.8 = (f32[64,256]{1,0:T(8,128)S(1)}, f32[64,256]{1,0:T(8,128)S(1)}, u32[]{:S(2)}, u32[]{:S(2)}) collective-permute-start(f32[64,256]{1,0:T(8,128)S(1)} %get-tuple-element.53), channel_id=1, source_target_pairs={{0,2},{1,9},{2,0},{3,11},{4,6},{5,13},{6,4},{7,15},{8,10},{9,1},{1... | collective-permute-start | bytes 196616 | tf_op jit(solution)/shard_map/ppermute | solution.py:459
  36.7 7.3 %collective-permute-start.6 = (f32[32,512]{1,0:T(8,128)S(1)}, f32[32,512]{1,0:T(8,128)S(1)}, u32[]{:S(2)}, u32[]{:S(2)}) collective-permute-start(f32[32,512]{1,0:T(8,128)S(1)} %get-tuple-element.49), channel_id=1, source_target_pairs={{0,8},{1,3},{2,10},{3,1},{4,12},{5,7},{6,14},{7,5},{8,0},{9,11},{1... | collective-permute-start | bytes 196616 | tf_op jit(solution)/shard_map/ppermute | solution.py:459
  40.8 5.0 %collective-permute-start.9 = (f32[64,256]{1,0:T(8,128)S(1)}, f32[64,256]{1,0:T(8,128)S(1)}, u32[]{:S(2)}, u32[]{:S(2)}) collective-permute-start(f32[64,256]{1,0:T(8,128)S(1)} %multiply_add_fusion.1), channel_id=1, source_target_pairs={{0,2},{1,17},{2,0},{3,19},{4,6},{5,21},{6,4},{7,23},{8,10},{9,25},... | collective-permute-start | bytes 196616 | tf_op jit(solution)/shard_map/ppermute | solution.py:459
  41.5 9.7 %all-to-all-start.2 = ((f32[32,1,128]{2,1,0:T(1,128)}), f32[32,1,128]{2,1,0:T(1,128)S(1)}, u32[]{:S(2)}, u32[]{:S(2)}) async-start(f32[32,1,128]{2,1,0:T(1,128)} %bitcast.12), calls=%async_computation.2 | async-start | bytes 32768 | tf_op jit(solution)/shard_map/all_to_all | solution.py:469
  44.1 4.4 %collective-permute-start.7 = (f32[32,512]{1,0:T(8,128)S(1)}, f32[32,512]{1,0:T(8,128)S(1)}, u32[]{:S(2)}, u32[]{:S(2)}) collective-permute-start(f32[32,512]{1,0:T(8,128)S(1)} %add.22.own), channel_id=1, source_target_pairs={{0,8},{1,5},{2,10},{3,7},{4,12},{5,1},{6,14},{7,3},{8,0},{9,13},{1... | collective-permute-start | bytes 196616 | tf_op jit(solution)/shard_map/ppermute | solution.py:459
  52.1 4.3 %collective-permute-start.10 = (f32[32,512]{1,0:T(8,128)S(1)}, f32[32,512]{1,0:T(8,128)S(1)}, u32[]{:S(2)}, u32[]{:S(2)}) collective-permute-start(f32[32,512]{1,0:T(8,128)S(1)} %get-tuple-element.55), channel_id=1, source_target_pairs={{0,8},{1,3},{2,10},{3,1},{4,12},{5,7},{6,14},{7,5},{8,0},{9,11},{1... | collective-permute-start | bytes 196616 | tf_op jit(solution)/shard_map/ppermute | solution.py:459
  56.5 4.3 %collective-permute-start.11 = (f32[32,512]{1,0:T(8,128)S(1)}, f32[32,512]{1,0:T(8,128)S(1)}, u32[]{:S(2)}, u32[]{:S(2)}) collective-permute-start(f32[32,512]{1,0:T(8,128)S(1)} %add.25.own), channel_id=1, source_target_pairs={{0,8},{1,5},{2,10},{3,7},{4,12},{5,1},{6,14},{7,3},{8,0},{9,13},{1... | collective-permute-start | bytes 196616 | tf_op jit(solution)/shard_map/ppermute | solution.py:459
  57.2 10.4 %all-to-all-start.3 = ((f32[32,1,128]{2,1,0:T(1,128)}), f32[32,1,128]{2,1,0:T(1,128)S(1)}, u32[]{:S(2)}, u32[]{:S(2)}) async-start(f32[32,1,128]{2,1,0:T(1,128)} %bitcast.19), calls=%async_computation.3 | async-start | bytes 32768 | tf_op jit(solution)/shard_map/all_to_all | solution.py:469
  68.4 8.9 %collective-permute-start.12 = (f32[64,256]{1,0:T(8,128)S(1)}, f32[64,256]{1,0:T(8,128)S(1)}, u32[]{:S(2)}, u32[]{:S(2)}) collective-permute-start(f32[64,256]{1,0:T(8,128)S(1)} %get-tuple-element.64), channel_id=1, source_target_pairs={{0,1},{1,0},{2,3},{3,2},{4,5},{5,4},{6,7},{7,6},{8,9},{9,8},{10,11... | collective-permute-start | bytes 196616 | tf_op jit(solution)/shard_map/ppermute | solution.py:451

commit v6 on v5

--- a/solution.py
+++ b/solution.py
@@ -34,11 +34,11 @@
     return high, (x - high.astype(F32)).astype(BF16)
 
 
-def dot3(x, high, low):
+def dot3(x, high, low, dot):
     rows = x.shape[0]
     xh, xl = split(x)
-    both = bdot(jnp.concatenate([xh, xl], axis=0), high)
-    return both[:rows] + both[rows:] + bdot(xh, low)
+    both = dot(jnp.concatenate([xh, xl], axis=0), high)
+    return both[:rows] + both[rows:] + dot(xh, low)
 
 
 def dot2(x, exact):
@@ -148,7 +148,7 @@
     return jnp.concatenate([ref_other[lo:hi, :], ref_own[lo:hi, :]], axis=1)
 
 
-def prep_kernel(plan, w_other, w_own, i_other, i_own, cap_other, cap_own, th, tl, ah, al, b_w, sems):
+def prep_kernel(plan, w_other, w_own, i_other, i_own, cap_other, cap_own, wh, wl, ah, al, b_w, sems):
     nodes = w_own.shape[0]
     blocks, width = i_own.shape[0], i_own.shape[1]
     copies = land([(w_other, b_w.at[0]), (w_own, b_w.at[1])], sems)
@@ -181,9 +181,9 @@
         copy.wait()
     for half in range(2):
         here = slice(half * nodes, (half + 1) * nodes)
-        h, l = split(b_w[half].T)
-        th[:, here] = h
-        tl[:, here] = l
+        h, l = split(b_w[half])
+        wh[here, :] = h
+        wl[here, :] = l
 
 
 def march(plan, x, ah, al):
@@ -211,7 +211,7 @@
     msg[...] = jnp.broadcast_to(row, msg.shape)
 
 
-def finish_round(plan, r, spot, r_ref, c_ref, p_ref, msg, ah, al, sent, th, tl, more=None):
+def finish_round(plan, r, spot, r_ref, c_ref, p_ref, msg, ah, al, sent, wh, wl, more=None):
     near_msg, sem = sent
     r_ref[...] = r
     send_squares(r, spot, near_msg)
@@ -225,8 +225,8 @@
         c_ref[...] = c
         rows = c.shape[0]
         ch, cl = split(c)
-        two = tdot(jnp.concatenate([ch, cl], axis=0), th[...])
-        p_ref[...] = two[:rows] + two[rows:] + tdot(ch, tl[...])
+        two = bdot(jnp.concatenate([ch, cl], axis=0), wh[...])
+        p_ref[...] = two[:rows] + two[rows:] + bdot(ch, wl[...])
         if more is not None:
             more(c)
 
@@ -238,10 +238,10 @@
     leaving.wait()
 
 
-def opening_kernel(plan, steps, channels, sections, doms, levels, spot, got, p_other, p_own, ah, al, th, tl,
+def opening_kernel(plan, steps, channels, sections, doms, levels, spot, got, p_other, p_own, ah, al, wh, wl,
                    w_ref, r_ref, c_ref, p_ref, msg, aux_ref, *sent):
     my, chip = spot[0:1, :], spot[1:2, :]
-    nets = th.shape[0]
+    nets = wh.shape[1]
     net_rows = nets // LANES
     tap_rows = channels // LANES
     mine = jnp.zeros((SUB, LANES), F32)
@@ -297,13 +297,13 @@
     aux_ref[0:1, 0 : inj.shape[1]] = inj
     for i, row in enumerate(kept + rows):
         aux_ref[1 + i : 2 + i, 0 : 2 * channels] = row
-    back = dot3(jnp.broadcast_to(net, (SUB, nets)), th[...], tl[...])[0:1]
+    back = dot3(jnp.broadcast_to(net, (SUB, nets)), wh[...], wl[...], tdot)[0:1]
     start = both(p_other, p_own, steps + 1, steps + 2)
     held = both(p_other, p_own, steps, steps + 1)
     q = (held + back - inj) - both(p_other, p_own, 0, steps)
     r = q + 0.5 * jnp.tanh(start)
     w_ref[...] = jnp.broadcast_to(start, w_ref.shape)
-    finish_round(plan, r, spot, r_ref, c_ref, p_ref, msg, ah, al, sent, th, tl)
+    finish_round(plan, r, spot, r_ref, c_ref, p_ref, msg, ah, al, sent, wh, wl)
 
 
 def chosen(index, nodes):
@@ -329,8 +329,8 @@
     return mean, 1.0 / (1.0 + jnp.sqrt(mean))
 
 
-def back_kernel(own, recv, r0, th, tl, u_ref):
-    u_ref[...] = r0[...] + dot3(own[...] + recv[...], th[...], tl[...])
+def back_kernel(own, recv, r0, wh, wl, u_ref):
+    u_ref[...] = r0[...] + dot3(own[...] + recv[...], wh[...], wl[...], tdot)
 
 
 def advance(got, u, w0, r0, c0, cells, mean_ref):
@@ -343,7 +343,7 @@
 def round_kernel(plan, steps, channels, cells, mode, *refs):
     refs = list(refs)
     take = lambda n: [refs.pop(0) for _ in range(n)]
-    (spot, got, u, w0, r0, c0, ah, al, th, tl, aux) = take(11)
+    (spot, got, u, w0, r0, c0, ah, al, wh, wl, aux) = take(11)
     if mode == "drive":
         (pre,) = take(1)
     w_ref, r_ref, c_ref, p_ref, msg, mean_ref = take(6)
@@ -370,7 +370,7 @@
     if mode == "taps":
         more = tap
         tt_ref[...] = jnp.zeros_like(tt_ref)
-    finish_round(plan, r, spot, r_ref, c_ref, p_ref, msg, ah, al, sent, th, tl, more)
+    finish_round(plan, r, spot, r_ref, c_ref, p_ref, msg, ah, al, sent, wh, wl, more)
 
 
 def residual_kernel(cells, spot, got, u, w0, r0, c0, w_ref, r_ref, msg, mean_ref):
@@ -500,8 +500,8 @@
     )
     p_other = swap(pack)
     cut = ((2 * blocks, units * width, width), BF16)
-    up = ((nets, wide), BF16)
-    th, tl, ah, al = call(
+    up = ((wide, nets), BF16)
+    wh, wl, ah, al = call(
         functools.partial(prep_kernel, plan),
         [up, up, cut, cut],
         w_other, net_weight, i_other, i_own, cap_other, capacitance,
@@ -516,7 +516,7 @@
     w, r, c, part, msg, aux = call(
         functools.partial(opening_kernel, plan, steps, channels, sections, doms, levels),
         state + [((steps, nets), F32), message, (aux_shape, F32)],
-        spot, got, p_other, pack, ah, al, th, tl,
+        spot, got, p_other, pack, ah, al, wh, wl,
         hbm_outs=(4,),
         scratch=landing,
     )
@@ -531,7 +531,7 @@
             own = own + recv
             recv = along_dom(own, bit)
         last = index == NEWTON * SWEEPS - 1
-        (u,) = call(back_kernel, [((steps, wide), F32)], own, recv, r, th, tl)
+        (u,) = call(back_kernel, [((steps, wide), F32)], own, recv, r, wh, wl)
         if last:
             break
         boundary = index % NEWTON == 0
@@ -554,7 +554,7 @@
         result = call(
             functools.partial(round_kernel, plan, steps, channels, cells, mode),
             outs,
-            spot, got, u, w, r, c, ah, al, th, tl, aux, *extra,
+            spot, got, u, w, r, c, ah, al, wh, wl, aux, *extra,
             hbm_outs=(4,),
             scratch=landing,
         )

time: 78.4 us -> 78.4 us (level)
  transfers between devices with their start and end apart: 17 -> 17, of which waited for: 10 -> 11; matrix products, arithmetic and copies ran while one was open for 0% -> 0% of each run, Pallas kernels for 8% -> 8%
where the time goes in v6:
time: 78.4 us; the launch traced here: 78.1 us
  waiting for transfers between devices  31.8 us (41%)
  starting transfers between devices  24.5 us (31%)
  Pallas kernels  10.7 us (14%)
  blocking collectives  8.87 us (11%)
  local copies, waits for them, and re-layouts  1.32 us (2%)
  between operations  0.8 us (1%)
    all_to_all x4, waiting for transfers between devices, gather(): lax.all_to_all(spread_out, everywhere, 0, 0, tiled=False).reshape(msg.shape)  17.6 us
    all_to_all x4, starting transfers between devices, gather(): lax.all_to_all(spread_out, everywhere, 0, 0, tiled=False).reshape(msg.shape)  16.3 us
    ppermute x8, waiting for transfers between devices, pair(): return lax.ppermute(x, everywhere, links)  13.4 us
    pallas_call x12, Pallas kernels, call(): pl.pallas_call(kernel, out_shape=[pltpu.HBM(s, d) if i in hbm_outs else j...  10.7 us
    all_to_all x1, blocking collectives, gather(): lax.all_to_all(spread_out, everywhere, 0, 0, tiled=False).reshape(msg.shape)  8.87 us
    ppermute x8, starting transfers between devices, pair(): return lax.ppermute(x, everywhere, links)  6.72 us
  transfers between devices with their start and end apart: 17, of which 11 were waited for; matrix products, arithmetic and copies ran while one was open for 0% of the time, Pallas kernels for 8%

profile of v6, /device:TPU:0, one launch (start us, length us, event | category | flops | bytes accessed | tf_op | source)
XLA Modules:
  0.0 78.1 jit_solution(11431649573077015852)
XLA Ops:
  1.2 2.1 %shard_map.113 = f32[32,8,128]{2,1,0:T(8,128)} custom-call(f32[1,256]{1,0:T(1,128)} %initial.3, f32[256,512]{1,0:T(8,128)} %bitcast.35, s32[1,128]{1,0:T(1,128)} %tap.3, f32[1,128]{1,0:T(1,128)} %att.1), custom_call_target="tpu_custom_call" | custom-call | tf_op jit(solution)/shard_map/pallas_call | solution.py:411
  3.4 7.0 %all-to-all-start = ((f32[32,8,128]{2,1,0:T(8,128)}), f32[32,8,128]{2,1,0:T(8,128)S(1)}, u32[]{:S(2)}, u32[]{:S(2)}) async-start(f32[32,8,128]{2,1,0:T(8,128)} %shard_map.113), calls=%async_computation | async-start | bytes 262144 | tf_op jit(solution)/shard_map/all_to_all | solution.py:469
  10.6 1.5 %shard_map.114 = (f32[40,256]{1,0:T(8,128)S(1)}, f32[2,128,128]{2,1,0:T(8,128)S(1)}) custom-call(f32[32,256]{1,0:T(8,128)} %bitcast.40, f32[1,256]{1,0:T(1,128)} %initial.3, f32[1,256]{1,0:T(1,128)} %cap_own.1, f32[2,128,128]{2,1,0:T(8,128)} %bitcast.37, s32[1,128]{1,0:T(1,128)} %tap.3, s32[1,128]{1,0:T(1,128)} %drive.1, f32[1,128]{1,0:T(1,128)} %gain.1, ...), custom_call_target="tpu_custom_call" | custom-call | tf_op jit(solution)/shard_map/pallas_call | solution.py:411
  13.1 0.8 %collective-permute-done.3.cap_other = f32[1,256]{1,0:T(1,128)S(1)} collective-permute-done((f32[1,256]{1,0:T(1,128)S(1)}, f32[1,256]{1,0:T(1,128)S(1)}, u32[]{:S(2)}, u32[]{:S(2)}) %collective-permute-start.3) | collective-permute-done | bytes 1056 | tf_op jit(solution)/shard_map/ppermute | solution.py:451
  14.0 0.8 %copy-done.1 = f32[256,512]{1,0:T(8,128)} copy-done((f32[256,512]{1,0:T(8,128)}, f32[256,512]{1,0:T(8,128)S(1)}, u32[]{:S(2)}) %copy-start.1) | copy-done | bytes 524312
  14.8 1.6 %shard_map.115 = (bf16[512,512]{1,0:T(8,128)(2,1)S(1)}, bf16[512,512]{1,0:T(8,128)(2,1)S(1)}, bf16[4,768,128]{2,1,0:T(8,128)(2,1)S(1)}, bf16[4,768,128]{2,1,0:T(8,128)(2,1)S(1)}) custom-call(f32[256,512]{1,0:T(8,128)} %copy-done.1, f32[256,512]{1,0:T(8,128)} %bitcast.36, f32[2,128,128]{2,1,0:T(8,128)S(1)} %collective-permute-done.2.i_other, ...), custom_call_target="tpu_custom_call" | custom-call | tf_op jit(solution)/shard_map/pallas_call | solution.py:411
  16.3 2.1 %all-to-all-done.got = f32[32,8,128]{2,1,0:T(8,128)S(1)} async-done(((f32[32,8,128]{2,1,0:T(8,128)}), f32[32,8,128]{2,1,0:T(8,128)S(1)}, u32[]{:S(2)}, u32[]{:S(2)}) %all-to-all-start) | async-done | bytes 131104 | tf_op jit(solution)/shard_map/all_to_all | solution.py:469
  18.5 1.1 %shard_map.116 = (f32[32,512]{1,0:T(8,128)S(1)}, f32[32,512]{1,0:T(8,128)S(1)}, f32[32,512]{1,0:T(8,128)S(1)}, f32[32,512]{1,0:T(8,128)S(1)}, f32[32,128]{1,0:T(8,128)}, /*index=5*/f32[16,512]{1,0:T(8,128)S(1)}) custom-call(f32[8,128]{1,0:T(8,128)S(1)} %broadcast_in_dim.4.spot.refs_0_, f32[32,8,128]{2,1,0:T(8,128)S(1)} %all-to-all-done.got, ...), custom_call_target="tpu_custom_call" | custom-call | tf_op jit(solution)/shard_map/pallas_call | solution.py:411
  19.6 0.9 %collective-permute-start.4 = (f32[32,512]{1,0:T(8,128)S(1)}, f32[32,512]{1,0:T(8,128)S(1)}, u32[]{:S(2)}, u32[]{:S(2)}) collective-permute-start(f32[32,512]{1,0:T(8,128)S(1)} %get-tuple-element.43), channel_id=1, source_target_pairs={{0,8},{1,3},{2,10},{3,1},{4,12},{5,7},{6,14},{7,5},{8,0},{9,11},{1... | collective-permute-start | bytes 196616 | tf_op jit(solution)/shard_map/ppermute | solution.py:459
  20.5 3.5 %collective-permute-done.4 = f32[32,512]{1,0:T(8,128)S(1)} collective-permute-done((f32[32,512]{1,0:T(8,128)S(1)}, f32[32,512]{1,0:T(8,128)S(1)}, u32[]{:S(2)}, u32[]{:S(2)}) %collective-permute-start.4) | collective-permute-done | bytes 65568 | tf_op jit(solution)/shard_map/ppermute | solution.py:459
  24.0 0.9 %collective-permute-start.5 = (f32[32,512]{1,0:T(8,128)S(1)}, f32[32,512]{1,0:T(8,128)S(1)}, u32[]{:S(2)}, u32[]{:S(2)}) collective-permute-start(f32[32,512]{1,0:T(8,128)S(1)} %add.21.own), channel_id=1, source_target_pairs={{0,8},{1,5},{2,10},{3,7},{4,12},{5,1},{6,14},{7,3},{8,0},{9,13},{1... | collective-permute-start | bytes 196616 | tf_op jit(solution)/shard_map/ppermute | solution.py:459
  24.9 3.4 %all-to-all-start.1 = ((f32[32,1,128]{2,1,0:T(1,128)}), f32[32,1,128]{2,1,0:T(1,128)S(1)}, u32[]{:S(2)}, u32[]{:S(2)}) async-start(f32[32,1,128]{2,1,0:T(1,128)} %bitcast.9), calls=%async_computation.1 | async-start | bytes 32768 | tf_op jit(solution)/shard_map/all_to_all | solution.py:469
  28.7 6.6 %all-to-all-done.1 = f32[32,1,128]{2,1,0:T(1,128)S(1)} async-done(((f32[32,1,128]{2,1,0:T(1,128)}), f32[32,1,128]{2,1,0:T(1,128)S(1)}, u32[]{:S(2)}, u32[]{:S(2)}) %all-to-all-start.1) | async-done | bytes 16416 | tf_op jit(solution)/shard_map/all_to_all | solution.py:469
  35.3 0.8 shard_map.118
  37.3 3.4 %collective-permute-done.8 = f32[64,256]{1,0:T(8,128)S(1)} collective-permute-done((f32[64,256]{1,0:T(8,128)S(1)}, f32[64,256]{1,0:T(8,128)S(1)}, u32[]{:S(2)}, u32[]{:S(2)}) %collective-permute-start.8) | collective-permute-done | bytes 65568 | tf_op jit(solution)/shard_map/ppermute | solution.py:459
  41.4 2.5 %all-to-all-start.2 = ((f32[32,1,128]{2,1,0:T(1,128)}), f32[32,1,128]{2,1,0:T(1,128)S(1)}, u32[]{:S(2)}, u32[]{:S(2)}) async-start(f32[32,1,128]{2,1,0:T(1,128)} %bitcast.12), calls=%async_computation.2 | async-start | bytes 32768 | tf_op jit(solution)/shard_map/all_to_all | solution.py:469
  44.0 1.7 %collective-permute-start.7 = (f32[32,512]{1,0:T(8,128)S(1)}, f32[32,512]{1,0:T(8,128)S(1)}, u32[]{:S(2)}, u32[]{:S(2)}) collective-permute-start(f32[32,512]{1,0:T(8,128)S(1)} %add.22.own), channel_id=1, source_target_pairs={{0,8},{1,5},{2,10},{3,7},{4,12},{5,1},{6,14},{7,3},{8,0},{9,13},{1... | collective-permute-start | bytes 196616 | tf_op jit(solution)/shard_map/ppermute | solution.py:459
  45.7 2.6 %collective-permute-done.7.recv = f32[32,512]{1,0:T(8,128)S(1)} collective-permute-done((f32[32,512]{1,0:T(8,128)S(1)}, f32[32,512]{1,0:T(8,128)S(1)}, u32[]{:S(2)}, u32[]{:S(2)}) %collective-permute-start.7) | collective-permute-done | bytes 65568 | tf_op jit(solution)/shard_map/ppermute | solution.py:459
  48.7 2.4 %all-to-all-done.2 = f32[32,1,128]{2,1,0:T(1,128)S(1)} async-done(((f32[32,1,128]{2,1,0:T(1,128)}), f32[32,1,128]{2,1,0:T(1,128)S(1)}, u32[]{:S(2)}, u32[]{:S(2)}) %all-to-all-start.2) | async-done | bytes 16416 | tf_op jit(solution)/shard_map/all_to_all | solution.py:469
  51.1 0.9 %shard_map.120 = (f32[32,512]{1,0:T(8,128)S(1)}, f32[32,512]{1,0:T(8,128)S(1)}, f32[32,512]{1,0:T(8,128)S(1)}, f32[32,512]{1,0:T(8,128)S(1)}, f32[32,128]{1,0:T(8,128)}, /*index=5*/f32[1,128]{1,0:T(1,128)S(1)}) custom-call(f32[8,128]{1,0:T(8,128)S(1)} %broadcast_in_dim.4.spot.refs_0_, f32[32,128]{1,0:T(8,128)S(1)} %bitcast.29, ...), custom_call_target="tpu_custom_call" | custom-call | tf_op jit(solution)/shard_map/pallas_call | solution.py:411
  52.7 3.7 %collective-permute-done.10 = f32[32,512]{1,0:T(8,128)S(1)} collective-permute-done((f32[32,512]{1,0:T(8,128)S(1)}, f32[32,512]{1,0:T(8,128)S(1)}, u32[]{:S(2)}, u32[]{:S(2)}) %collective-permute-start.10) | collective-permute-done | bytes 65568 | tf_op jit(solution)/shard_map/ppermute | solution.py:459
  57.0 3.4 %all-to-all-start.3 = ((f32[32,1,128]{2,1,0:T(1,128)}), f32[32,1,128]{2,1,0:T(1,128)S(1)}, u32[]{:S(2)}, u32[]{:S(2)}) async-start(f32[32,1,128]{2,1,0:T(1,128)} %bitcast.19), calls=%async_computation.3 | async-start | bytes 32768 | tf_op jit(solution)/shard_map/all_to_all | solution.py:469
  61.1 6.5 %all-to-all-done.3 = f32[32,1,128]{2,1,0:T(1,128)S(1)} async-done(((f32[32,1,128]{2,1,0:T(1,128)}), f32[32,1,128]{2,1,0:T(1,128)S(1)}, u32[]{:S(2)}, u32[]{:S(2)}) %all-to-all-start.3) | async-done | bytes 16416 | tf_op jit(solution)/shard_map/all_to_all | solution.py:469
  68.5 8.9 %all_to_all.25 = f32[32,1,128]{2,1,0:T(1,128)S(1)} all-to-all(f32[32,1,128]{2,1,0:T(1,128)S(1)} %bitcast.33), channel_id=1, replica_groups=mesh['section'=4,'dom'=8] {'section','dom'}, dimensions={0} | all-to-all | bytes 32768 | tf_op jit(solution)/shard_map/all_to_all | solution.py:469
  (38 shorter events, 8.5 us)
Async XLA Ops:
  0.6 13.3 %collective-permute-start.1 = (f32[256,512]{1,0:T(8,128)}, f32[256,512]{1,0:T(8,128)S(1)}, u32[]{:S(2)}, u32[]{:S(2)}) collective-permute-start(f32[256,512]{1,0:T(8,128)} %bitcast.34), channel_id=1, source_target_pairs={{0,1},{1,0},{2,3},{3,2},{4,5},{5,4},{6,7},{7,6},{8,9},{9,8},{10,11... | collective-permute-start | bytes 1572872 | tf_op jit(solution)/shard_map/ppermute | solution.py:451
  3.3 7.0 %copy-start.2 = (f32[1,2,128,128]{3,2,1,0:T(8,128)S(1)}, f32[1,2,128,128]{3,2,1,0:T(8,128)}, u32[]{:S(2)}) copy-start(f32[1,2,128,128]{3,2,1,0:T(8,128)} %param.14) | copy-start | bytes 393220
  3.4 15.1 %all-to-all-start = ((f32[32,8,128]{2,1,0:T(8,128)}), f32[32,8,128]{2,1,0:T(8,128)S(1)}, u32[]{:S(2)}, u32[]{:S(2)}) async-start(f32[32,8,128]{2,1,0:T(8,128)} %shard_map.113), calls=%async_computation | async-start | bytes 262144 | tf_op jit(solution)/shard_map/all_to_all | solution.py:469
  10.3 3.6 %collective-permute-start.2 = (f32[2,128,128]{2,1,0:T(8,128)S(1)}, f32[2,128,128]{2,1,0:T(8,128)S(1)}, u32[]{:S(2)}, u32[]{:S(2)}) collective-permute-start(f32[2,128,128]{2,1,0:T(8,128)S(1)} %bitcast.39), channel_id=1, source_target_pairs={{0,1},{1,0},{2,3},{3,2},{4,5},{5,4},{6,7},{7,6},{8,9},{9,8},{10,11... | collective-permute-start | bytes 393224 | tf_op jit(solution)/shard_map/ppermute | solution.py:451
  12.1 0.7 copy-start
  12.1 4.2 %collective-permute-start = (f32[40,256]{1,0:T(8,128)S(1)}, f32[40,256]{1,0:T(8,128)S(1)}, u32[]{:S(2)}, u32[]{:S(2)}) collective-permute-start(f32[40,256]{1,0:T(8,128)S(1)} %get-tuple-element.36.p_own), channel_id=1, source_target_pairs={{0,1},{1,0},{2,3},{3,2},{4,5},{5,4},{6,7},{7,6},{8,9},{9,8},{10,11... | collective-permute-start | bytes 122888 | tf_op jit(solution)/shard_map/ppermute | solution.py:451
  12.8 1.2 %collective-permute-start.3 = (f32[1,256]{1,0:T(1,128)S(1)}, f32[1,256]{1,0:T(1,128)S(1)}, u32[]{:S(2)}, u32[]{:S(2)}) collective-permute-start(f32[1,256]{1,0:T(1,128)S(1)} %copy-done), channel_id=1, source_target_pairs={{0,1},{1,0},{2,3},{3,2},{4,5},{5,4},{6,7},{7,6},{8,9},{9,8},{10,11... | collective-permute-start | bytes 3080 | tf_op jit(solution)/shard_map/ppermute | solution.py:451
  14.0 0.8 %copy-start.1 = (f32[256,512]{1,0:T(8,128)}, f32[256,512]{1,0:T(8,128)S(1)}, u32[]{:S(2)}) copy-start(f32[256,512]{1,0:T(8,128)S(1)} %collective-permute-done.1.w_other) | copy-start | bytes 1572868
  19.6 4.3 %collective-permute-start.4 = (f32[32,512]{1,0:T(8,128)S(1)}, f32[32,512]{1,0:T(8,128)S(1)}, u32[]{:S(2)}, u32[]{:S(2)}) collective-permute-start(f32[32,512]{1,0:T(8,128)S(1)} %get-tuple-element.43), channel_id=1, source_target_pairs={{0,8},{1,3},{2,10},{3,1},{4,12},{5,7},{6,14},{7,5},{8,0},{9,11},{1... | collective-permute-start | bytes 196616 | tf_op jit(solution)/shard_map/ppermute | solution.py:459
  24.0 4.3 %collective-permute-start.5 = (f32[32,512]{1,0:T(8,128)S(1)}, f32[32,512]{1,0:T(8,128)S(1)}, u32[]{:S(2)}, u32[]{:S(2)}) collective-permute-start(f32[32,512]{1,0:T(8,128)S(1)} %add.21.own), channel_id=1, source_target_pairs={{0,8},{1,5},{2,10},{3,7},{4,12},{5,1},{6,14},{7,3},{8,0},{9,13},{1... | collective-permute-start | bytes 196616 | tf_op jit(solution)/shard_map/ppermute | solution.py:459
  24.9 10.5 %all-to-all-start.1 = ((f32[32,1,128]{2,1,0:T(1,128)}), f32[32,1,128]{2,1,0:T(1,128)S(1)}, u32[]{:S(2)}, u32[]{:S(2)}) async-start(f32[32,1,128]{2,1,0:T(1,128)} %bitcast.9), calls=%async_computation.1 | async-start | bytes 32768 | tf_op jit(solution)/shard_map/all_to_all | solution.py:469
  36.1 4.5 %collective-permute-start.8 = (f32[64,256]{1,0:T(8,128)S(1)}, f32[64,256]{1,0:T(8,128)S(1)}, u32[]{:S(2)}, u32[]{:S(2)}) collective-permute-start(f32[64,256]{1,0:T(8,128)S(1)} %get-tuple-element.53), channel_id=1, source_target_pairs={{0,2},{1,9},{2,0},{3,11},{4,6},{5,13},{6,4},{7,15},{8,10},{9,1},{1... | collective-permute-start | bytes 196616 | tf_op jit(solution)/shard_map/ppermute | solution.py:459
  36.7 7.2 %collective-permute-start.6 = (f32[32,512]{1,0:T(8,128)S(1)}, f32[32,512]{1,0:T(8,128)S(1)}, u32[]{:S(2)}, u32[]{:S(2)}) collective-permute-start(f32[32,512]{1,0:T(8,128)S(1)} %get-tuple-element.49), channel_id=1, source_target_pairs={{0,8},{1,3},{2,10},{3,1},{4,12},{5,7},{6,14},{7,5},{8,0},{9,11},{1... | collective-permute-start | bytes 196616 | tf_op jit(solution)/shard_map/ppermute | solution.py:459
  40.7 5.0 %collective-permute-start.9 = (f32[64,256]{1,0:T(8,128)S(1)}, f32[64,256]{1,0:T(8,128)S(1)}, u32[]{:S(2)}, u32[]{:S(2)}) collective-permute-start(f32[64,256]{1,0:T(8,128)S(1)} %multiply_add_fusion.1), channel_id=1, source_target_pairs={{0,2},{1,17},{2,0},{3,19},{4,6},{5,21},{6,4},{7,23},{8,10},{9,25},... | collective-permute-start | bytes 196616 | tf_op jit(solution)/shard_map/ppermute | solution.py:459
  41.4 9.7 %all-to-all-start.2 = ((f32[32,1,128]{2,1,0:T(1,128)}), f32[32,1,128]{2,1,0:T(1,128)S(1)}, u32[]{:S(2)}, u32[]{:S(2)}) async-start(f32[32,1,128]{2,1,0:T(1,128)} %bitcast.12), calls=%async_computation.2 | async-start | bytes 32768 | tf_op jit(solution)/shard_map/all_to_all | solution.py:469
  44.0 4.4 %collective-permute-start.7 = (f32[32,512]{1,0:T(8,128)S(1)}, f32[32,512]{1,0:T(8,128)S(1)}, u32[]{:S(2)}, u32[]{:S(2)}) collective-permute-start(f32[32,512]{1,0:T(8,128)S(1)} %add.22.own), channel_id=1, source_target_pairs={{0,8},{1,5},{2,10},{3,7},{4,12},{5,1},{6,14},{7,3},{8,0},{9,13},{1... | collective-permute-start | bytes 196616 | tf_op jit(solution)/shard_map/ppermute | solution.py:459
  52.0 4.3 %collective-permute-start.10 = (f32[32,512]{1,0:T(8,128)S(1)}, f32[32,512]{1,0:T(8,128)S(1)}, u32[]{:S(2)}, u32[]{:S(2)}) collective-permute-start(f32[32,512]{1,0:T(8,128)S(1)} %get-tuple-element.55), channel_id=1, source_target_pairs={{0,8},{1,3},{2,10},{3,1},{4,12},{5,7},{6,14},{7,5},{8,0},{9,11},{1... | collective-permute-start | bytes 196616 | tf_op jit(solution)/shard_map/ppermute | solution.py:459
  56.4 4.3 %collective-permute-start.11 = (f32[32,512]{1,0:T(8,128)S(1)}, f32[32,512]{1,0:T(8,128)S(1)}, u32[]{:S(2)}, u32[]{:S(2)}) collective-permute-start(f32[32,512]{1,0:T(8,128)S(1)} %add.25.own), channel_id=1, source_target_pairs={{0,8},{1,5},{2,10},{3,7},{4,12},{5,1},{6,14},{7,3},{8,0},{9,13},{1... | collective-permute-start | bytes 196616 | tf_op jit(solution)/shard_map/ppermute | solution.py:459
  57.0 10.5 %all-to-all-start.3 = ((f32[32,1,128]{2,1,0:T(1,128)}), f32[32,1,128]{2,1,0:T(1,128)S(1)}, u32[]{:S(2)}, u32[]{:S(2)}) async-start(f32[32,1,128]{2,1,0:T(1,128)} %bitcast.19), calls=%async_computation.3 | async-start | bytes 32768 | tf_op jit(solution)/shard_map/all_to_all | solution.py:469
  68.4 8.9 %collective-permute-start.12 = (f32[64,256]{1,0:T(8,128)S(1)}, f32[64,256]{1,0:T(8,128)S(1)}, u32[]{:S(2)}, u32[]{:S(2)}) collective-permute-start(f32[64,256]{1,0:T(8,128)S(1)} %get-tuple-element.64), channel_id=1, source_target_pairs={{0,1},{1,0},{2,3},{3,2},{4,5},{5,4},{6,7},{7,6},{8,9},{9,8},{10,11... | collective-permute-start | bytes 196616 | tf_op jit(solution)/shard_map/ppermute | solution.py:451
